TPU v7x, 128 devices: a whole 4x4x4 slice. The times are simulated.
128 devices in a mesh: seq: 32 (over z, x, core), batch: 4 (over y).
Axes of the slice: x: 4, y: 4, z: 4, core: 2. Of those that a mesh axis runs over, the one named last changes fastest.
Arguments:
- hidden: bfloat16 [4, 4096, 1024], P('batch', 'seq'), may hold values from -6 to 6
- queries: bfloat16 [4, 4096, 2048], P('batch', 'seq'), may hold values from -0.19921875 to 0.19921875
- w_key: bfloat16 [1024, 2048], replicated, may hold values from -0.1875 to 0.1875
- w_value: bfloat16 [1024, 2048], replicated, may hold values from -0.1875 to 0.1875
- log_gate: float32 [4, 32, 4096], P('batch', None, 'seq'), may hold values from -0.1 to 0, as said below
- level_gain: float32 [32, 18], replicated, may hold values from 0.1 to 1
- segment_ids: int32 [4, 4096], P('batch', 'seq'), may hold values from 0 to 7, never falling along the last dimension, each value on 1 to 1024 neighbouring positions
- out_grad: bfloat16 [4, 4096, 2048], P('batch', 'seq'), may hold values from -0.19921875 to 0.19921875
Outputs:
- query_grad: bfloat16 [4, 4096, 2048], P('batch', 'seq')
- input_grad: bfloat16 [4, 4096, 1024], P('batch', 'seq')
- gate_grad: float32 [4, 32, 4096], P('batch', None, 'seq')
- key_weight_grad: float32 [1024, 2048], P(('seq', 'batch'))
- value_weight_grad: float32 [1024, 2048], P(('seq', 'batch'))
- gain_grad: float32 [32, 18], replicated
Inputs may be any that keep to these rules, and one draw needn't show every extreme that they name: `log_gate`: entries are zero or negative. `segment_ids`: along each sequence the ids never fall, so each document is one run of tokens; the longest document has exactly a quarter of 4096 tokens in every draw.
All inputs are finite; a program needn't handle non-finite values.
Results may differ from a plain program's by a relative error of at most 0.0058.
Values sent between devices are 32-bit elements; how exact they have to be, the bound alone decides.
A program may use at most 128 MiB of HBM per device.

v0:
```python
import jax
import jax.numpy as jnp
from jax import lax
from jax.sharding import Mesh
from jax.sharding import PartitionSpec as P

SEQ = ("seq_0", "seq_1", "seq_2")
SEQ_BATCH = ("seq_0", "seq_1", "seq_2", "batch")


HIGH = lax.Precision.HIGHEST


def partner(value, axis, distance):
    mask = 2**distance
    pairs = [(source, source ^ mask) for source in range(lax.axis_size(axis))]
    return lax.ppermute(value, axis, pairs)


def sent_to_all(x, axis):
    copies = jnp.broadcast_to(x, (lax.axis_size(axis), *x.shape))
    return lax.all_to_all(copies, axis, split_axis=0, concat_axis=0, tiled=True)


def combined_pairwise(pieces, combine):
    while len(jax.tree.leaves(pieces)[0]) > 1:
        pieces = jax.vmap(combine)(*(pieces[side::2] for side in (0, 1)))
    return pieces[0]


def prefix(x, axis, combine, identity):
    size, place = (lax.axis_size(axis), lax.axis_index(axis))
    passed = jnp.arange(size) > place

    def kept(part, zero, own):
        part = jnp.where(
            passed.reshape(-1, *(1 for _ in own.shape)), part, jnp.asarray(zero, own.dtype)
        )
        return part[::-1]

    pieces = sent_to_all(x, axis)
    return combined_pairwise(kept(pieces, identity, x), combine)


def over_axes(x, axes):
    for axis in axes:
        x = lax.psum(x, axis)
    return x


def in_blocks(x, dim, size):
    before, after = (x.shape[:dim], x.shape[dim + 1 :])
    return jnp.moveaxis(x.reshape(*before, size, -1, *after), dim, 0)


def sum_at_owner(x, axis, dim):
    size = lax.axis_size(axis)
    pieces = lax.all_to_all(in_blocks(x, dim, size), axis, 0, 0, tiled=True)
    return jnp.sum(pieces, axis=0)


def bit_count(values, limit):
    total_bits = jnp.zeros_like(values)
    for bit_pos in range(limit):
        total_bits = total_bits + (values >= 1 << bit_pos).astype(jnp.int32)
    return total_bits


def local_states(query_f, key_f, value_f, grad_f, cumulative, segment):
    block_decay = cumulative[:, -1]
    last_w = jnp.where(
        (segment == segment[-1])[None], jnp.exp(block_decay[:, None] - cumulative), 0.0
    )
    fwd_state = jnp.einsum("shp,shq->hpq", key_f * last_w.T[:, :, None], value_f, precision=HIGH)
    first_w = jnp.where((segment == segment[0])[None], jnp.exp(cumulative), 0.0)
    rev_state = jnp.einsum("thp,thq->hpq", query_f * first_w.T[:, :, None], grad_f, precision=HIGH)
    return (fwd_state, rev_state)


def pair_terms(query_g, key_g, value_g, grad_g, cumulative, gains, level_map, allowed, log_tok):
    levels = gains.shape[1]
    scores = jnp.einsum("thp,shp->hts", query_g, key_g, preferred_element_type=jnp.float32)
    dprobs = jnp.einsum("thp,shp->hts", grad_g, value_g, preferred_element_type=jnp.float32)
    spread = cumulative[:, :, None] - cumulative[:, None, :]
    decays = jnp.where(allowed[None], jnp.exp(jnp.where(allowed[None], spread, 0.0)), 0.0)
    joined = decays * scores * dprobs
    level_w = jnp.zeros_like(decays)
    gain_part = jnp.zeros((gains.shape[0], levels), jnp.float32)
    for level_idx in range(log_tok + 1):
        chosen = (level_map == level_idx)[None]
        level_w = jnp.where(chosen, gains[:, level_idx][:, None, None], level_w)
        gain_part = gain_part.at[:, level_idx].set(
            jnp.sum(jnp.where(chosen, joined, 0.0), axis=(1, 2))
        )
    coeffs = level_w * decays
    weighted = coeffs * dprobs
    query_acc = jnp.einsum("hts,shp->thp", weighted, key_g.astype(jnp.float32), precision=HIGH)
    key_acc = jnp.einsum("hts,thp->shp", weighted, query_g.astype(jnp.float32), precision=HIGH)
    value_acc = jnp.einsum(
        "hts,thp->shp", coeffs * scores, grad_g.astype(jnp.float32), precision=HIGH
    )
    grid = weighted * scores
    return (query_acc, key_acc, value_acc, jnp.sum(grid, axis=2), jnp.sum(grid, axis=1), gain_part)


def cross_terms(
    query_f, key_f, value_f, grad_f, cumulative, segment, incoming, gains, log_tok, sums
):
    query_acc, key_acc, value_acc, row_sum, col_sum, gain_part = sums
    block_decay = cumulative[:, -1]
    for section_bit in range(len(incoming)):
        fwd_in, fwd_key, rev_in, rev_key = incoming[section_bit]
        level_idx = log_tok + section_bit + 1
        tier_gain = gains[:, level_idx][:, None]
        fwd_weight = jnp.where((segment == fwd_key)[None], jnp.exp(cumulative), 0.0)
        state_grad = jnp.einsum("hpq,thq->thp", fwd_in, grad_f, precision=HIGH)
        row_term = fwd_weight * jnp.sum(query_f * state_grad, axis=2).T
        gain_part = gain_part.at[:, level_idx].add(jnp.sum(row_term, axis=1))
        row_sum = row_sum + tier_gain * row_term
        query_acc = query_acc + (tier_gain * fwd_weight).T[:, :, None] * state_grad
        rev_weight = jnp.where(
            (segment == rev_key)[None], jnp.exp(block_decay[:, None] - cumulative), 0.0
        )
        rev_values = jnp.einsum("hpq,shq->shp", rev_in, value_f, precision=HIGH)
        rev_keys = jnp.einsum("hpq,shp->shq", rev_in, key_f, precision=HIGH)
        col_term = rev_weight * jnp.sum(key_f * rev_values, axis=2).T
        col_sum = col_sum + tier_gain * col_term
        rev_scale = (tier_gain * rev_weight).T[:, :, None]
        key_acc = key_acc + rev_scale * rev_values
        value_acc = value_acc + rev_scale * rev_keys
    return (query_acc, key_acc, value_acc, row_sum, col_sum, gain_part)


def add_pair(earlier, later_val):
    return earlier + later_val


def local(hidden, queries, w_key, w_value, log_gate, level_gain, segment_ids, out_grad):
    block_len = hidden.shape[1]
    head_count, levels = level_gain.shape
    head_dim = queries.shape[2] // head_count
    log_tok = block_len.bit_length() - 1
    hidden_rows = hidden[0]
    key_rows = jnp.dot(hidden_rows, w_key, preferred_element_type=jnp.float32).astype(jnp.bfloat16)
    value_rows = jnp.dot(hidden_rows, w_value, preferred_element_type=jnp.float32).astype(
        jnp.bfloat16
    )
    query_rows = queries[0]
    grad_rows = out_grad[0]
    segment = segment_ids[0]
    seg_float = segment.astype(jnp.float32)
    cumulative = jnp.cumsum(log_gate[0], axis=1)
    query_f = query_rows.reshape(block_len, head_count, head_dim).astype(jnp.float32)
    key_f = key_rows.reshape(block_len, head_count, head_dim).astype(jnp.float32)
    value_f = value_rows.reshape(block_len, head_count, head_dim).astype(jnp.float32)
    grad_f = grad_rows.reshape(block_len, head_count, head_dim).astype(jnp.float32)
    fstate, rstate = local_states(query_f, key_f, value_f, grad_f, cumulative, segment)
    block_total = cumulative[:, -1]
    last_key = seg_float[-1:]
    first_key = seg_float[:1]
    before = jnp.zeros_like(block_total)
    after_sum = jnp.zeros_like(block_total)
    seq_size = lax.axis_size(SEQ)
    seq_index = lax.axis_index(SEQ)
    incoming = []
    for section_bit in range(seq_size.bit_length() - 1):
        received = partner((fstate, rstate, block_total, last_key, first_key), SEQ, section_bit)
        peer_fwd, peer_rev, peer_total, peer_last, peer_first = received
        is_upper = jnp.bitwise_and(jnp.right_shift(seq_index, section_bit), 1) == 1
        fwd_in = jnp.where(is_upper, peer_fwd * jnp.exp(before)[:, None, None], 0.0)
        rev_in = jnp.where(is_upper, 0.0, peer_rev * jnp.exp(after_sum)[:, None, None])
        incoming.append((fwd_in, peer_last[0], rev_in, peer_first[0]))
        low_fwd = jnp.where(is_upper, peer_fwd, fstate)
        high_fwd = jnp.where(is_upper, fstate, peer_fwd)
        low_rev = jnp.where(is_upper, peer_rev, rstate)
        high_rev = jnp.where(is_upper, rstate, peer_rev)
        low_total = jnp.where(is_upper, peer_total, block_total)
        high_total = jnp.where(is_upper, block_total, peer_total)
        low_last = jnp.where(is_upper, peer_last, last_key)
        high_last = jnp.where(is_upper, last_key, peer_last)
        low_first = jnp.where(is_upper, peer_first, first_key)
        high_first = jnp.where(is_upper, first_key, peer_first)
        fwd_keep = jnp.where(low_last[0] == high_last[0], jnp.exp(high_total), 0.0)
        rev_keep = jnp.where(low_first[0] == high_first[0], jnp.exp(low_total), 0.0)
        fstate = high_fwd + fwd_keep[:, None, None] * low_fwd
        rstate = low_rev + rev_keep[:, None, None] * high_rev
        before = jnp.where(is_upper, low_total + before, before)
        after_sum = jnp.where(is_upper, after_sum, after_sum + high_total)
        block_total = low_total + high_total
        last_key = high_last
        first_key = low_first
    head_group = min(8, head_count)
    group_cols = head_group * head_dim
    positions = jnp.arange(block_len, dtype=jnp.int32)
    level_map = bit_count(jnp.bitwise_xor(positions[:, None], positions[None, :]), levels - 1)
    allowed = (positions[None, :] <= positions[:, None]) & (segment[:, None] == segment[None, :])

    def intra(group_idx):
        col_start = group_idx * group_cols

        def take_cols(rows):
            return lax.dynamic_slice_in_dim(rows, col_start, group_cols, 1).reshape(
                block_len, head_group, head_dim
            )

        cumul_g = lax.dynamic_slice_in_dim(cumulative, group_idx * head_group, head_group, 0)
        gain_g = lax.dynamic_slice_in_dim(level_gain, group_idx * head_group, head_group, 0)
        return pair_terms(
            take_cols(query_rows),
            take_cols(key_rows),
            take_cols(value_rows),
            take_cols(grad_rows),
            cumul_g,
            gain_g,
            level_map,
            allowed,
            log_tok,
        )

    parts = lax.map(intra, jnp.arange(head_count // head_group))
    sums = (
        parts[0].transpose(1, 0, 2, 3).reshape(block_len, head_count, head_dim),
        parts[1].transpose(1, 0, 2, 3).reshape(block_len, head_count, head_dim),
        parts[2].transpose(1, 0, 2, 3).reshape(block_len, head_count, head_dim),
        parts[3].reshape(head_count, block_len),
        parts[4].reshape(head_count, block_len),
        parts[5].reshape(head_count, levels),
    )
    query_acc, key_acc, value_acc, row_sum, col_sum, gain_part = cross_terms(
        query_f, key_f, value_f, grad_f, cumulative, seg_float, incoming, level_gain, log_tok, sums
    )
    gate_diff = row_sum - col_sum
    local_tail = jnp.cumsum(gate_diff[:, ::-1], axis=1)[:, ::-1]
    own_total = jnp.sum(gate_diff, axis=1)
    tail_sum = prefix(own_total, SEQ, add_pair, jnp.zeros_like(own_total))
    gain_total = over_axes(gain_part, SEQ_BATCH)
    gate_grad = (local_tail + tail_sum[:, None])[None]
    query_grad = query_acc.reshape(block_len, head_count * head_dim).astype(jnp.bfloat16)[None]
    key_grad = key_acc.reshape(block_len, head_count * head_dim).astype(jnp.bfloat16)
    value_grad = value_acc.reshape(block_len, head_count * head_dim).astype(jnp.bfloat16)
    input_grad = (
        jnp.einsum("tf,df->td", key_grad, w_key, preferred_element_type=jnp.float32)
        + jnp.einsum("tf,df->td", value_grad, w_value, preferred_element_type=jnp.float32)
    ).astype(jnp.bfloat16)[None]
    both_grads = jnp.concatenate([key_grad, value_grad], axis=1)
    partial_rows = lax.psum_scatter(
        lax.dot_general(
            hidden_rows, both_grads, (((0,), (0,)), ((), ())), preferred_element_type=jnp.float32
        ),
        SEQ,
        scatter_dimension=0,
        tiled=True,
    )
    rows_here = sum_at_owner(partial_rows, "batch", 0)
    key_width = w_key.shape[1]
    return (
        query_grad,
        input_grad,
        gate_grad,
        rows_here[:, :key_width],
        rows_here[:, key_width:],
        gain_total,
    )


def solution(mesh):
    split = Mesh(
        mesh.devices.reshape(4, 4, 2, mesh.shape["batch"]), ("seq_0", "seq_1", "seq_2", "batch")
    )
    return jax.shard_map(
        local,
        mesh=split,
        in_specs=(
            P("batch", SEQ, None),
            P("batch", SEQ, None),
            P(),
            P(),
            P("batch", None, SEQ),
            P(),
            P("batch", SEQ),
            P("batch", SEQ, None),
        ),
        out_specs=(
            P("batch", SEQ, None),
            P("batch", SEQ, None),
            P("batch", None, SEQ),
            P(SEQ_BATCH, None),
            P(SEQ_BATCH, None),
            P(),
        ),
        check_vma=False,
    )
```

profile of v0, /device:TPU:0, one launch (start us, length us, event | category | flops | bytes accessed | tf_op | source)
XLA Modules:
  0.0 517.8 jit_solution(9498503488572460431)
XLA Ops:
  13.8 2.9 convolution_convert_fusion.1
  17.0 2.9 convolution_convert_fusion
  21.5 3.0 collective-permute-start.16
  28.3 4.5 collective-permute-start.18
  35.9 3.4 collective-permute-start.20
  39.9 2.7 collective-permute-start.8
  43.2 5.0 collective-permute-start.22
  50.1 3.9 collective-permute-done.11
  54.0 8.8 %compare_bitcast_fusion.5 = (pred[128]{0:T(512)(128)(4,1)S(1)}, pred[128]{0:T(512)(128)(4,1)S(1)}, pred[128]{0:T(512)(128)(4,1)S(1)}, pred[128]{0:T(512)(128)(4,...) fusion(s32[1,128]{1,0:T(1,128)} %param.42, ...), kind=kLoop, calls=%fused_computation.300 | loop fusion | flops 1664 | bytes 2096 | tf_op jit(solution)/shard_map/jit(_where)/broadcast_in_dim | solution.py:121
  84.5 15.3 %collective-permute-done.4 = f32[32,64,64]{2,1,0:T(8,128)S(1)} collective-permute-done((f32[32,64,64]{2,1,0:T(8,128)}, f32[32,64,64]{2,1,0:T(8,128)S(1)}, u32[]{:S(2)}, u32[]{:S(2)}) %collective-permute-start.4) | collective-permute-done | bytes 524320 | tf_op jit(solution)/shard_map/ppermute | solution.py:17
  99.8 2.8 multiply_add_fusion.6
  105.4 83.0 %while.39 = (s32[]{:T(128)}, f32[4,128,8,64]{1,3,2,0:T(8,128)}, f32[4,128,8,64]{1,3,2,0:T(8,128)}, f32[4,128,8,64]{1,3,2,0:T(8,128)}, f32[4,8,128]{2,1,0:T(8,128...) while((s32[]{:T(128)}, f32[4,128,8,64]{1,3,2,0:T(8,128)}, ...), condition=%wide.region_20.21_spmd.clone.clone, body=%wide.region_8.0_spmd.clone.clone.sunk | while | flops 348960704 | bytes 8666134 | solution.py:220
  193.1 3.2 collective-permute-done.9
  205.7 20.7 %collective-permute-done.10 = f32[32,64,64]{2,1,0:T(8,128)S(1)} collective-permute-done((f32[32,64,64]{2,1,0:T(8,128)S(1)}, f32[32,64,64]{2,1,0:T(8,128)S(1)}, u32[]{:S(2)}, u32[]{:S(2)}) %collective-permute-start.10) | collective-permute-done | bytes 524320 | tf_op jit(solution)/shard_map/ppermute | solution.py:17
  229.8 16.5 %collective-permute-done.13 = f32[32,64,64]{2,1,0:T(8,128)S(1)} collective-permute-done((f32[32,64,64]{2,1,0:T(8,128)S(1)}, f32[32,64,64]{2,1,0:T(8,128)S(1)}, u32[]{:S(2)}, u32[]{:S(2)}) %collective-permute-start.13) | collective-permute-done | bytes 524320 | tf_op jit(solution)/shard_map/ppermute | solution.py:17
  250.0 2.6 collective-permute-done.15
  253.7 24.6 %collective-permute-done.17 = f32[32,64,64]{2,1,0:T(8,128)S(1)} collective-permute-done((f32[32,64,64]{2,1,0:T(8,128)S(1)}, f32[32,64,64]{2,1,0:T(8,128)S(1)}, u32[]{:S(2)}, u32[]{:S(2)}) %collective-permute-start.17) | collective-permute-done | bytes 524320 | tf_op jit(solution)/shard_map/ppermute | solution.py:17
  282.4 22.0 %collective-permute-done.19 = f32[32,64,64]{2,1,0:T(8,128)S(1)} collective-permute-done((f32[32,64,64]{2,1,0:T(8,128)S(1)}, f32[32,64,64]{2,1,0:T(8,128)S(1)}, u32[]{:S(2)}, u32[]{:S(2)}) %collective-permute-start.19) | collective-permute-done | bytes 524320 | tf_op jit(solution)/shard_map/ppermute | solution.py:17
  306.8 21.5 %collective-permute-done.21 = f32[32,64,64]{2,1,0:T(8,128)S(1)} collective-permute-done((f32[32,64,64]{2,1,0:T(8,128)S(1)}, f32[32,64,64]{2,1,0:T(8,128)S(1)}, u32[]{:S(2)}, u32[]{:S(2)}) %collective-permute-start.21) | collective-permute-done | bytes 524320 | tf_op jit(solution)/shard_map/ppermute | solution.py:17
  328.6 2.7 collective-permute-start.23
  333.2 19.9 %collective-permute-done.23 = f32[32,64,64]{2,1,0:T(8,128)S(1)} collective-permute-done((f32[32,64,64]{2,1,0:T(8,128)S(1)}, f32[32,64,64]{2,1,0:T(8,128)S(1)}, u32[]{:S(2)}, u32[]{:S(2)}) %collective-permute-start.23) | collective-permute-done | bytes 524320 | tf_op jit(solution)/shard_map/ppermute | solution.py:17
  356.6 8.0 %convolution_bitcast_fusion.3 = f32[1024,4096]{0,1:T(8,128)} fusion(bf16[128,2048]{0,1:T(8,128)(2,1)S(1)} %bitcast.485, bf16[128,2048]{0,1:T(8,128)(2,1)S(1)} %bitcast.483, bf16[1,128,1024]{2,1,0:T(8,128)(2,1)S(1)} %copy-done), kind=kOutput, calls=%fused_computation.102 | convolution fusion | flops 1075838976 | bytes 18087936 | tf_op jit(solution)/shard_map/dot_general | solution.py:247
  364.6 17.5 %copy.93 = f32[1024,4096]{1,0:T(8,128)} copy(f32[1024,4096]{0,1:T(8,128)} %convolution_bitcast_fusion.3) | data formatting | bytes 33554432
  391.4 16.7 %psum.28 = f32[32,18]{1,0:T(8,128)S(1)} all-reduce(f32[32,18]{1,0:T(8,128)S(1)} %scatter-add.24), channel_id=1, replica_groups=mesh['seq_0'=4,'seq_1'=4,'seq_2'=2,'batch'=4] {'seq_0'}, use_global_device_ids=true, to_apply=%region_45.46 | all-reduce | flops 576 | bytes 4608 | tf_op jit(solution)/shard_map/psum | solution.py:47
  408.0 15.3 %psum.29 = f32[32,18]{1,0:T(8,128)S(1)} all-reduce(f32[32,18]{1,0:T(8,128)S(1)} %psum.28), channel_id=1, replica_groups=mesh['seq_0'=4,'seq_1'=4,'seq_2'=2,'batch'=4] {'seq_1'}, use_global_device_ids=true, to_apply=%region_46.47 | all-reduce | flops 576 | bytes 4608 | tf_op jit(solution)/shard_map/psum | solution.py:47
  423.3 3.3 psum.30
  426.7 17.1 %psum.31 = f32[32,18]{1,0:T(8,128)S(1)} all-reduce(f32[32,18]{1,0:T(8,128)S(1)} %psum.30), channel_id=1, replica_groups=mesh['seq_0'=4,'seq_1'=4,'seq_2'=2,'batch'=4] {'batch'}, use_global_device_ids=true, to_apply=%region_48.49 | all-reduce | flops 576 | bytes 4608 | tf_op jit(solution)/shard_map/psum | solution.py:47
  446.2 4.1 all-to-all-start
  450.3 3.9 fusion.202
  458.1 39.4 %reduce-scatter.4.cloned.1.call-done = f32[32,4096]{1,0:T(8,128)} async-done(((f32[1024,4096]{1,0:T(8,128)}), f32[32,4096]{1,0:T(8,128)}) %reduce-scatter.4.cloned.1.call-update) | async-done | bytes 524304 | tf_op jit(solution)/shard_map/reduce_scatter | solution.py:246
  497.4 4.2 all-to-all-start.1
  502.3 7.4 %all-to-all-done.1 = f32[4,8,4096]{2,1,0:T(8,128)S(1)} async-done(((f32[4,8,4096]{2,1,0:T(8,128)}), f32[4,8,4096]{2,1,0:T(8,128)S(1)}, u32[]{:S(2)}, u32[]{:S(2)}) %all-to-all-start.1) | async-done | bytes 524320 | tf_op jit(solution)/shard_map/all_to_all | solution.py:58
  (563 shorter events, 156.5 us)
Async XLA Ops:
  7.2 490.3 %reduce-scatter.4.cloned.1.call-start = ((), (), s32[]{:S(2)}) async-start(), calls=%async_computation.3 | async-start | bytes 17301504 | tf_op jit(solution)/shard_map/reduce_scatter | solution.py:246
  8.5 11.7 %collective-permute-start.14 = (f32[1]{0:T(128)}, f32[1]{0:T(128)}, u32[]{:S(2)}, u32[]{:S(2)}) collective-permute-start(f32[1]{0:T(128)} %get-tuple-element.952), channel_id=1, source_target_pairs={{0,4},{4,0},{8,12},{12,8},{16,20},{20,16},{24,28},{28,24},{32,36},... | collective-permute-start | bytes 20 | tf_op jit(solution)/shard_map/ppermute | solution.py:17
  8.5 16.0 %collective-permute-start = (f32[1]{0:T(128)}, f32[1]{0:T(128)}, u32[]{:S(2)}, u32[]{:S(2)}) collective-permute-start(f32[1]{0:T(128)} %get-tuple-element.953), channel_id=1, source_target_pairs={{0,4},{4,0},{8,12},{12,8},{16,20},{20,16},{24,28},{28,24},{32,36},... | collective-permute-start | bytes 20 | tf_op jit(solution)/shard_map/ppermute | solution.py:17
  21.5 6.1 %collective-permute-start.16 = (f32[1]{0:T(128)}, f32[1]{0:T(128)}, u32[]{:S(2)}, u32[]{:S(2)}) collective-permute-start(f32[1]{0:T(128)} %select_n.618), channel_id=1, source_target_pairs={{0,8},{4,12},{8,0},{12,4},{16,24},{20,28},{24,16},{28,20},{32,40},... | collective-permute-start | bytes 20 | tf_op jit(solution)/shard_map/ppermute | solution.py:17
  25.8 7.0 %collective-permute-start.2 = (f32[1]{0:T(128)}, f32[1]{0:T(128)}, u32[]{:S(2)}, u32[]{:S(2)}) collective-permute-start(f32[1]{0:T(128)} %select_n.559), channel_id=1, source_target_pairs={{0,8},{4,12},{8,0},{12,4},{16,24},{20,28},{24,16},{28,20},{32,40},... | collective-permute-start | bytes 20 | tf_op jit(solution)/shard_map/ppermute | solution.py:17
  28.3 7.0 %collective-permute-start.18 = (f32[1]{0:T(128)}, f32[1]{0:T(128)}, u32[]{:S(2)}, u32[]{:S(2)}) collective-permute-start(f32[1]{0:T(128)} %select_n.627), channel_id=1, source_target_pairs={{0,16},{4,20},{8,24},{12,28},{16,0},{20,4},{24,8},{28,12},{32,48},... | collective-permute-start | bytes 20 | tf_op jit(solution)/shard_map/ppermute | solution.py:17
  33.4 5.9 %collective-permute-start.5 = (f32[1]{0:T(128)}, f32[1]{0:T(128)}, u32[]{:S(2)}, u32[]{:S(2)}) collective-permute-start(f32[1]{0:T(128)} %select_n.573), channel_id=1, source_target_pairs={{0,16},{4,20},{8,24},{12,28},{16,0},{20,4},{24,8},{28,12},{32,48},... | collective-permute-start | bytes 20 | tf_op jit(solution)/shard_map/ppermute | solution.py:17
  35.9 6.6 %collective-permute-start.20 = (f32[1]{0:T(128)}, f32[1]{0:T(128)}, u32[]{:S(2)}, u32[]{:S(2)}) collective-permute-start(f32[1]{0:T(128)} %select_n.636), channel_id=1, source_target_pairs={{0,32},{4,36},{8,40},{12,44},{16,48},{20,52},{24,56},{28,60},{32,0... | collective-permute-start | bytes 20 | tf_op jit(solution)/shard_map/ppermute | solution.py:17
  39.9 8.3 %collective-permute-start.8 = (f32[1]{0:T(128)}, f32[1]{0:T(128)}, u32[]{:S(2)}, u32[]{:S(2)}) collective-permute-start(f32[1]{0:T(128)} %select_n.587), channel_id=1, source_target_pairs={{0,32},{4,36},{8,40},{12,44},{16,48},{20,52},{24,56},{28,60},{32,0... | collective-permute-start | bytes 20 | tf_op jit(solution)/shard_map/ppermute | solution.py:17
  43.2 6.9 %collective-permute-start.22 = (f32[1]{0:T(128)}, f32[1]{0:T(128)}, u32[]{:S(2)}, u32[]{:S(2)}) collective-permute-start(f32[1]{0:T(128)} %select_n.645), channel_id=1, source_target_pairs={{0,64},{4,68},{8,72},{12,76},{16,80},{20,84},{24,88},{28,92},{32,9... | collective-permute-start | bytes 20 | tf_op jit(solution)/shard_map/ppermute | solution.py:17
  48.7 5.3 %collective-permute-start.11 = (f32[1]{0:T(128)}, f32[1]{0:T(128)}, u32[]{:S(2)}, u32[]{:S(2)}) collective-permute-start(f32[1]{0:T(128)} %select_n.601), channel_id=1, source_target_pairs={{0,64},{4,68},{8,72},{12,76},{16,80},{20,84},{24,88},{28,92},{32,9... | collective-permute-start | bytes 20 | tf_op jit(solution)/shard_map/ppermute | solution.py:17
  65.3 8.0 %collective-permute-start.1 = (f32[32,64,64]{2,1,0:T(8,128)S(1)}, f32[32,64,64]{2,1,0:T(8,128)S(1)}, u32[]{:S(2)}, u32[]{:S(2)}) collective-permute-start(f32[32,64,64]{2,1,0:T(8,128)S(1)} %fusion.72), channel_id=1, source_target_pairs={{0,4},{4,0},{8,12},{12,8},{16,20},{20,16},{24,28},{28,24},{32,36},... | collective-permute-start | bytes 1572872 | tf_op jit(solution)/shard_map/ppermute | solution.py:17
  65.4 3.1 collective-permute-start.3
  69.2 3.6 collective-permute-start.6
  75.6 24.2 %collective-permute-start.4 = (f32[32,64,64]{2,1,0:T(8,128)}, f32[32,64,64]{2,1,0:T(8,128)S(1)}, u32[]{:S(2)}, u32[]{:S(2)}) collective-permute-start(f32[32,64,64]{2,1,0:T(8,128)} %multiply_add_fusion.7), channel_id=1, source_target_pairs={{0,8},{4,12},{8,0},{12,4},{16,24},{20,28},{24,16},{28,20},{32,40},... | collective-permute-start | bytes 1572872 | tf_op jit(solution)/shard_map/ppermute | solution.py:17
  102.6 98.7 %collective-permute-start.7 = (f32[32,64,64]{2,1,0:T(8,128)}, f32[32,64,64]{2,1,0:T(8,128)}, u32[]{:S(2)}, u32[]{:S(2)}) collective-permute-start(f32[32,64,64]{2,1,0:T(8,128)} %multiply_add_fusion.6), channel_id=1, source_target_pairs={{0,16},{4,20},{8,24},{12,28},{16,0},{20,4},{24,8},{28,12},{32,48},... | collective-permute-start | bytes 1572872 | tf_op jit(solution)/shard_map/ppermute | solution.py:17
  191.0 5.4 %collective-permute-start.9 = (f32[32]{0:T(128)}, f32[32]{0:T(128)S(1)}, u32[]{:S(2)}, u32[]{:S(2)}) collective-permute-start(f32[32]{0:T(128)} %get-tuple-element.950), channel_id=1, source_target_pairs={{0,16},{4,20},{8,24},{12,28},{16,0},{20,4},{24,8},{28,12},{32,48},... | collective-permute-start | bytes 392 | tf_op jit(solution)/shard_map/ppermute | solution.py:17
  197.0 3.6 collective-permute-start.12
  203.1 23.3 %collective-permute-start.10 = (f32[32,64,64]{2,1,0:T(8,128)S(1)}, f32[32,64,64]{2,1,0:T(8,128)S(1)}, u32[]{:S(2)}, u32[]{:S(2)}) collective-permute-start(f32[32,64,64]{2,1,0:T(8,128)S(1)} %multiply_add_fusion.5), channel_id=1, source_target_pairs={{0,32},{4,36},{8,40},{12,44},{16,48},{20,52},{24,56},{28,60},{32,0... | collective-permute-start | bytes 1572872 | tf_op jit(solution)/shard_map/ppermute | solution.py:17
  226.7 19.5 %collective-permute-start.13 = (f32[32,64,64]{2,1,0:T(8,128)S(1)}, f32[32,64,64]{2,1,0:T(8,128)S(1)}, u32[]{:S(2)}, u32[]{:S(2)}) collective-permute-start(f32[32,64,64]{2,1,0:T(8,128)S(1)} %multiply_add_fusion.4), channel_id=1, source_target_pairs={{0,64},{4,68},{8,72},{12,76},{16,80},{20,84},{24,88},{28,92},{32,9... | collective-permute-start | bytes 1572872 | tf_op jit(solution)/shard_map/ppermute | solution.py:17
  249.9 2.7 collective-permute-start.15
  253.0 25.3 %collective-permute-start.17 = (f32[32,64,64]{2,1,0:T(8,128)S(1)}, f32[32,64,64]{2,1,0:T(8,128)S(1)}, u32[]{:S(2)}, u32[]{:S(2)}) collective-permute-start(f32[32,64,64]{2,1,0:T(8,128)S(1)} %multiply_add_fusion.3), channel_id=1, source_target_pairs={{0,8},{4,12},{8,0},{12,4},{16,24},{20,28},{24,16},{28,20},{32,40},... | collective-permute-start | bytes 1572872 | tf_op jit(solution)/shard_map/ppermute | solution.py:17
  278.6 25.9 %collective-permute-start.19 = (f32[32,64,64]{2,1,0:T(8,128)S(1)}, f32[32,64,64]{2,1,0:T(8,128)S(1)}, u32[]{:S(2)}, u32[]{:S(2)}) collective-permute-start(f32[32,64,64]{2,1,0:T(8,128)S(1)} %multiply_add_fusion.2), channel_id=1, source_target_pairs={{0,16},{4,20},{8,24},{12,28},{16,0},{20,4},{24,8},{28,12},{32,48},... | collective-permute-start | bytes 1572872 | tf_op jit(solution)/shard_map/ppermute | solution.py:17
  304.8 23.6 %collective-permute-start.21 = (f32[32,64,64]{2,1,0:T(8,128)S(1)}, f32[32,64,64]{2,1,0:T(8,128)S(1)}, u32[]{:S(2)}, u32[]{:S(2)}) collective-permute-start(f32[32,64,64]{2,1,0:T(8,128)S(1)} %multiply_add_fusion.1), channel_id=1, source_target_pairs={{0,32},{4,36},{8,40},{12,44},{16,48},{20,52},{24,56},{28,60},{32,0... | collective-permute-start | bytes 1572872 | tf_op jit(solution)/shard_map/ppermute | solution.py:17
  328.6 24.5 %collective-permute-start.23 = (f32[32,64,64]{2,1,0:T(8,128)S(1)}, f32[32,64,64]{2,1,0:T(8,128)S(1)}, u32[]{:S(2)}, u32[]{:S(2)}) collective-permute-start(f32[32,64,64]{2,1,0:T(8,128)S(1)} %multiply_add_fusion), channel_id=1, source_target_pairs={{0,64},{4,68},{8,72},{12,76},{16,80},{20,84},{24,88},{28,92},{32,9... | collective-permute-start | bytes 1572872 | tf_op jit(solution)/shard_map/ppermute | solution.py:17
  382.1 62.4 %copy-start.29 = (f32[4,8,128]{2,1,0:T(8,128)S(1)}, f32[4,8,128]{2,1,0:T(8,128)}, u32[]{:S(2)}) copy-start(f32[4,8,128]{2,1,0:T(8,128)} %get-tuple-element.602) | copy-start | bytes 49156
  382.1 62.4 %copy-start.30 = (f32[4,8,128]{2,1,0:T(8,128)S(1)}, f32[4,8,128]{2,1,0:T(8,128)}, u32[]{:S(2)}) copy-start(f32[4,8,128]{2,1,0:T(8,128)} %get-tuple-element.601) | copy-start | bytes 49156
  382.1 62.4 %copy-start.50 = (f32[32]{0:T(128)S(1)}, f32[32]{0:T(128)}, u32[]{:S(2)}) copy-start(f32[32]{0:T(128)} %copy-done.49) | copy-start | bytes 388
  382.1 62.4 %copy-start.52 = (f32[32]{0:T(128)S(1)}, f32[32]{0:T(128)}, u32[]{:S(2)}) copy-start(f32[32]{0:T(128)} %copy-done.51) | copy-start | bytes 388
  382.1 62.4 %copy-start.54 = (f32[32]{0:T(128)S(1)}, f32[32]{0:T(128)}, u32[]{:S(2)}) copy-start(f32[32]{0:T(128)} %copy-done.53) | copy-start | bytes 388
  446.2 11.6 %all-to-all-start = ((f32[32,1,32]{2,1,0:T(1,128)}), f32[32,1,32]{2,1,0:T(1,128)S(1)}, u32[]{:S(2)}, u32[]{:S(2)}) async-start(f32[32,1,32]{2,1,0:T(1,128)} %broadcast_in_dim.583), calls=%async_computation | async-start | bytes 32768 | tf_op jit(solution)/shard_map/all_to_all | solution.py:22
  497.4 12.3 %all-to-all-start.1 = ((f32[4,8,4096]{2,1,0:T(8,128)}), f32[4,8,4096]{2,1,0:T(8,128)S(1)}, u32[]{:S(2)}, u32[]{:S(2)}) async-start(f32[4,8,4096]{2,1,0:T(8,128)} %bitcast.492), calls=%async_computation.1 | async-start | bytes 1048576 | tf_op jit(solution)/shard_map/all_to_all | solution.py:58
  (124 other events, 1761.7 us)
Sparse Core Ops, SparseCore 0:
  382.4 115.0 reduce-scatter.3
where the time goes:
time: 527 us; the launch traced here: 518 us
  waiting for transfers between devices  202 us (38%)
  other arithmetic  68.1 us (13%)
  matrix products  61.2 us (12%)
  local copies, waits for them, and re-layouts  53.5 us (10%)
  blocking collectives  52.4 us (10%)
  starting transfers between devices  44.9 us (9%)
  between operations  28.6 us (5%)
  loops' own time  6.79 us (1%)
    ppermute x24, waiting for transfers between devices, partner(): return lax.ppermute(value, axis, pairs)  155 us
    psum x4, blocking collectives, over_axes(): x = lax.psum(x, axis)  52.4 us
    reduce_scatter x1, waiting for transfers between devices, local(): lax.psum_scatter(lax.dot_general(hidden_rows, both_grads, (((0,), (0,)),...  39.4 us
    ppermute x24, starting transfers between devices, partner(): return lax.ppermute(value, axis, pairs)  36.5 us
    another operation x50, other arithmetic  31.3 us
    unnamed x129, local copies, waits for them, and re-layouts  23.2 us
  transfers between devices with their start and end apart: 27, of which 15 were waited for; matrix products, arithmetic and copies ran while one was open for 25% of the time, Pallas kernels for 0%

commit v1 on v0

v1 whole, which is shorter than its diff:
```python
import functools

import jax
import jax.numpy as jnp
from jax import lax
from jax.experimental import pallas as pl
from jax.experimental.pallas import tpu as pltpu
from jax.sharding import Mesh
from jax.sharding import PartitionSpec as P

SEQ = ("z", "x", "core")
SEQ_BATCH = ("z", "x", "core", "batch")
MESH = pl.DeviceIdType.MESH
HIGHEST = lax.Precision.HIGHEST
F32 = jnp.float32
BF16 = jnp.bfloat16

NT = (((1,), (1,)), ((), ()))
TN = (((0,), (0,)), ((), ()))
NN = (((1,), (0,)), ((), ()))

TOK = 128
PAIR = 128
HALF_ROWS = 1088
SROWS = 1024


def dot(a, b, dims):
    return lax.dot_general(a, b, dims, preferred_element_type=F32)


def dot_exact(a, b, dims):
    return lax.dot_general(a, b, dims, preferred_element_type=F32, precision=HIGHEST)


def split2(x):
    hi = x.astype(BF16)
    return hi, (x - hi.astype(F32)).astype(BF16)


def dot_left(a, b, dims):
    hi, lo = split2(a)
    return dot(hi, b, dims) + dot(lo, b, dims)


def dot_right(a, b, dims):
    hi, lo = split2(b)
    return dot(a, hi, dims) + dot(a, lo, dims)


def iota(shape, dim):
    return lax.broadcasted_iota(jnp.int32, shape, dim)


def pair_cumulative(cum_cols, p, low):
    return jnp.where(low, cum_cols[:, 2 * p : 2 * p + 1], cum_cols[:, 2 * p + 1 : 2 * p + 2])


def token_weights(cum_pair, seg_col):
    total = cum_pair[TOK - 1 : TOK, :]
    last = jnp.where(seg_col == seg_col[TOK - 1 : TOK, :], jnp.exp(total - cum_pair), 0.0)
    first = jnp.where(seg_col == seg_col[0:1, :], jnp.exp(cum_pair), 0.0)
    return first, last, total


def states_kernel(hid_ref, wk_ref, wv_ref, q_ref, g_ref, lg_ref, seg_ref, k_ref, v_ref, st_ref):
    step = pl.program_id(0)
    hid = hid_ref[...]
    keys = dot(hid, wk_ref[...], NN).astype(BF16)
    values = dot(hid, wv_ref[...], NN).astype(BF16)
    k_ref[...] = keys
    v_ref[...] = values
    lower = (iota((TOK, TOK), 1) <= iota((TOK, TOK), 0)).astype(F32)
    cum_cols = dot_exact(lower, lg_ref[0], NT)
    seg_col = seg_ref[...]
    seg_f = seg_col.astype(F32)
    low = iota((TOK, PAIR), 1) < 64
    low_half = iota((64, PAIR), 1) < 64
    row8 = iota((8, PAIR), 0)
    half = step // 4
    for p in range(2):
        cum_pair = pair_cumulative(cum_cols, p, low)
        first_w, last_w, total = token_weights(cum_pair, seg_col)
        cols = slice(p * PAIR, (p + 1) * PAIR)
        fwd = dot_left(keys[:, cols].astype(F32) * last_w, values[:, cols], TN)
        rev = dot_left(q_ref[:, cols].astype(F32) * first_w, g_ref[:, cols], TN)
        pp = 2 * (step % 4) + p
        st_ref[half, pl.ds(pl.multiple_of(pp * 64, 64), 64), :] = jnp.where(
            low_half, fwd[:64], fwd[64:]
        )
        st_ref[half, pl.ds(pl.multiple_of(512 + pp * 64, 64), 64), :] = jnp.where(
            low_half, rev[:64], rev[64:]
        )
        meta = jnp.where(
            row8 == 0,
            total,
            jnp.where(row8 == 1, seg_f[0:1, :], jnp.where(row8 == 2, seg_f[TOK - 1 : TOK, :], 0.0)),
        )
        st_ref[half, pl.ds(pl.multiple_of(1024 + pp * 8, 8), 8), :] = meta


def block_states(hidden, w_key, w_value, queries, out_grad, log_gate4, seg_col):
    cols = queries.shape[1]
    steps = cols // 256
    depth = hidden.shape[1]
    block = pl.BlockSpec((TOK, 256), lambda i: (0, i))
    weight = pl.BlockSpec((depth, 256), lambda i: (0, i))
    return pl.pallas_call(
        states_kernel,
        grid=(steps,),
        in_specs=[
            pl.BlockSpec((TOK, depth), lambda i: (0, 0)),
            weight,
            weight,
            block,
            block,
            pl.BlockSpec((1, 4, TOK), lambda i: (i, 0, 0)),
            pl.BlockSpec((TOK, 1), lambda i: (0, 0)),
        ],
        out_specs=[block, block, pl.BlockSpec((2, HALF_ROWS, PAIR), lambda i: (0, 0, 0))],
        out_shape=[
            jax.ShapeDtypeStruct((TOK, cols), BF16),
            jax.ShapeDtypeStruct((TOK, cols), BF16),
            jax.ShapeDtypeStruct((2, HALF_ROWS, PAIR), F32),
        ],
        compiler_params=pltpu.CompilerParams(dimension_semantics=("arbitrary",)),
        name="states",
    )(hidden, w_key, w_value, queries, out_grad, log_gate4, seg_col)


def remote(src, dst, ssem, rsem, target):
    return pltpu.make_async_remote_copy(
        src_ref=src,
        dst_ref=dst,
        send_sem=ssem,
        recv_sem=rsem,
        device_id=target,
        device_id_type=MESH,
    )


def entry_barrier(peers):
    barrier = pltpu.get_barrier_semaphore()
    for peer in peers:
        pl.semaphore_signal(barrier, inc=1, device_id=peer, device_id_type=MESH)
    pl.semaphore_wait(barrier, len(peers))


def ring(index, step):
    return lax.rem(index + step, 4)


def same(a, b):
    return jnp.where(a == b, 1.0, 0.0)


def linked(a, b, total):
    return jnp.where(a == b, jnp.exp(total), 0.0)


def exchange_kernel(
    st_ref,
    hid_ref,
    gain_ref,
    out_ref,
    gsum_ref,
    hy_out,
    hz_out,
    both,
    chip_send,
    chip_recv,
    tot_send,
    tot_recv,
    back_send,
    back_recv,
    own_blocks,
    hy,
    hz,
    s_chip,
    r_chip,
    s_x,
    r_x,
    s_z,
    r_z,
    s_back,
    r_back,
    s_fin,
    r_fin,
    s_h,
    r_h,
    s_f,
    r_f,
    s_d,
    r_d,
):
    x, y, z, c = (lax.axis_index(a) for a in ("x", "batch", "z", "core"))
    sib = {"core": 1 - c}
    peers = [sib]
    for axis, index in (("x", x), ("batch", y), ("z", z)):
        peers += [{axis: ring(index, d)} for d in (1, 2, 3)]
    entry_barrier(peers)

    swap = remote(st_ref.at[1 - c], both.at[c], s_chip, r_chip, sib)
    swap.start()

    hops = []
    for n, (axis, index, buf) in enumerate((("batch", y, hy), ("z", z, hz))):
        for m, d in enumerate((1, 3)):
            cp = remote(
                hid_ref, buf.at[index, c], s_h.at[n, m], r_h.at[n, m], {axis: ring(index, d)}
            )
            cp.start()
            hops.append(cp)
    down = []
    for n, (index, buf) in enumerate(((y, hy), (z, hz))):
        cp = remote(hid_ref, buf.at[index, c], s_d.at[n, 0], r_d.at[n, 0], sib)
        cp.start()
        down.append(cp)
    both[pl.ds(c, 1)] = st_ref[pl.ds(c, 1)]
    gsum_ref[...] = jnp.zeros_like(gsum_ref)
    swap.wait()

    row8 = iota((8, PAIR), 0)

    def meta_rows(total, first, last):
        return jnp.where(
            row8 == 0, total, jnp.where(row8 == 1, first, jnp.where(row8 == 2, last, 0.0))
        )

    for pp in range(8):
        f0 = both[0, pp * 64 : pp * 64 + 64, :]
        f1 = both[1, pp * 64 : pp * 64 + 64, :]
        r0 = both[0, 512 + pp * 64 : 576 + pp * 64, :]
        r1 = both[1, 512 + pp * 64 : 576 + pp * 64, :]
        m0 = both[0, 1024 + pp * 8 : 1032 + pp * 8, :]
        m1 = both[1, 1024 + pp * 8 : 1032 + pp * 8, :]
        t0, first0, last0 = m0[0:1], m0[1:2], m0[2:3]
        t1, first1, last1 = m1[0:1], m1[1:2], m1[2:3]
        q, p = pp // 2, pp % 2
        chip_send[q, p * 64 : p * 64 + 64, :] = f1 + linked(last0, last1, t1) * f0
        chip_send[q, 128 + p * 64 : 192 + p * 64, :] = r0 + linked(first0, first1, t0) * r1
        chip_send[q, 256 + p * 8 : 264 + p * 8, :] = meta_rows(t0 + t1, first0, last1)
        gsum_ref[pp, 0:1, :] = same(last0, first1) * jnp.sum(f0 * r1, axis=0, keepdims=True)

    xs = []
    for d in (1, 2, 3):
        to = ring(x, d)
        cp = remote(chip_send.at[to], chip_recv.at[x], s_x.at[d - 1], r_x.at[d - 1], {"x": to})
        cp.start()
        xs.append(cp)
    chip_recv[pl.ds(x, 1)] = chip_send[pl.ds(x, 1)]
    for cp in xs:
        cp.wait()

    def chip(j, p):
        return (
            chip_recv[j, p * 64 : p * 64 + 64, :],
            chip_recv[j, 128 + p * 64 : 192 + p * 64, :],
            chip_recv[j, 256 + p * 8 : 257 + p * 8, :],
            chip_recv[j, 257 + p * 8 : 258 + p * 8, :],
            chip_recv[j, 258 + p * 8 : 259 + p * 8, :],
        )

    def joined(p):
        (f0, r0, t0, a0, l0), (f1, r1, t1, a1, l1), (f2, r2, t2, a2, l2), (f3, r3, t3, a3, l3) = (
            chip(j, p) for j in range(4)
        )
        f01 = f1 + linked(l0, l1, t1) * f0
        r01 = r0 + linked(a0, a1, t0) * r1
        f23 = f3 + linked(l2, l3, t3) * f2
        r23 = r2 + linked(a2, a3, t2) * r3
        return f01, r01, f23, r23

    for p in range(2):
        f01, r01, f23, r23 = joined(p)
        t0, a0 = chip(0, p)[2:4]
        t1, l1 = chip(1, p)[2], chip(1, p)[4]
        t2, a2 = chip(2, p)[2:4]
        t3, l3 = chip(3, p)[2], chip(3, p)[4]
        tot_send[0, p * 64 : p * 64 + 64, :] = f23 + linked(l1, l3, t2 + t3) * f01
        tot_send[1, p * 64 : p * 64 + 64, :] = r01 + linked(a0, a2, t0 + t1) * r23
        tot_send[0, 128 + p * 8 : 136 + p * 8, :] = jnp.broadcast_to(l3, (8, PAIR))
        tot_send[1, 128 + p * 8 : 136 + p * 8, :] = jnp.broadcast_to(a0, (8, PAIR))
    zs = []
    for n, d in ((0, 1), (1, 3)):
        cp = remote(tot_send.at[n], tot_recv.at[n], s_z.at[n], r_z.at[n], {"z": ring(z, d)})
        cp.start()
        zs.append(cp)

    fwd = []
    for n, (axis, index, buf) in enumerate((("batch", y, hy), ("z", z, hz))):
        for m, d in enumerate((1, 3)):
            hops[2 * n + m].wait()
            came = ring(index, 4 - d)
            rows = slice(0, 512) if d == 1 else slice(512, 1024)
            cp = remote(
                buf.at[came, c, rows],
                buf.at[came, c, rows],
                s_f.at[n, m],
                r_f.at[n, m],
                {axis: ring(index, d)},
            )
            cp.start()
            fwd.append(cp)
            cp = remote(
                buf.at[came, c], buf.at[came, c], s_d.at[n, 1 + m], r_d.at[n, 1 + m], sib
            )
            cp.start()
            down.append(cp)

    for cp in zs:
        cp.wait()
    has_prev = (z > 0).astype(F32)
    has_next = (z < 3).astype(F32)
    prev_top = (z == 2).astype(F32)
    next_top = (z == 1).astype(F32)
    for p in range(2):
        (f0, r0, t0, a0, l0), (f1, r1, t1, a1, l1), (f2, r2, t2, a2, l2), (f3, r3, t3, a3, l3) = (
            chip(j, p) for j in range(4)
        )
        f01, r01, f23, r23 = joined(p)
        gains = gain_ref[pl.ds(c * 8 + 2 * x + p, 1)][0]
        g9, g10, g11, g12 = (gains[i : i + 1] for i in range(1, 5))
        zf = has_prev * tot_recv[0, p * 64 : p * 64 + 64, :]
        zl = tot_recv[0, 128 + p * 8 : 129 + p * 8, :]
        zr = has_next * tot_recv[1, p * 64 : p * 64 + 64, :]
        za = tot_recv[1, 128 + p * 8 : 129 + p * 8, :]
        gzf = g11 * (1.0 - prev_top) + g12 * prev_top
        gzr = g11 * (1.0 - next_top) + g12 * next_top
        sf = (
            gzf * same(zl, a0) * zf,
            gzf * linked(zl, a1, t0) * zf + g9 * same(l0, a1) * f0,
            gzf * linked(zl, a2, t0 + t1) * zf + g10 * same(l1, a2) * f01,
            gzf * linked(zl, a3, t0 + t1 + t2) * zf
            + g10 * linked(l1, a3, t2) * f01
            + g9 * same(l2, a3) * f2,
        )
        sr = (
            gzr * linked(za, l0, t1 + t2 + t3) * zr
            + g10 * linked(l0, a2, t1) * r23
            + g9 * same(l0, a1) * r1,
            gzr * linked(za, l1, t2 + t3) * zr + g10 * same(l1, a2) * r23,
            gzr * linked(za, l2, t3) * zr + g9 * same(l2, a3) * r3,
            gzr * same(za, l3) * zr,
        )
        for j in range(4):
            back_send[j, p * 64 : p * 64 + 64, :] = sf[j]
            back_send[j, 128 + p * 64 : 192 + p * 64, :] = sr[j]
        r_group = r01 + linked(a0, a2, t0 + t1) * r23
        d9 = same(l0, a1) * jnp.sum(f0 * r1, axis=0, keepdims=True) + same(l2, a3) * jnp.sum(
            f2 * r3, axis=0, keepdims=True
        )
        d10 = same(l1, a2) * jnp.sum(f01 * r23, axis=0, keepdims=True)
        dz = same(zl, a0) * jnp.sum(zf * r_group, axis=0, keepdims=True)
        rows = jnp.where(
            row8 == 1,
            d9,
            jnp.where(
                row8 == 2,
                d10,
                jnp.where(
                    row8 == 3, (1.0 - prev_top) * dz, jnp.where(row8 == 4, prev_top * dz, 0.0)
                ),
            ),
        )
        gsum_ref[pl.ds(2 * x + p, 1)] = gsum_ref[pl.ds(2 * x + p, 1)] + rows[None]

    bs = []
    for d in (1, 2, 3):
        to = ring(x, d)
        cp = remote(
            back_send.at[to], back_recv.at[x], s_back.at[d - 1], r_back.at[d - 1], {"x": to}
        )
        cp.start()
        bs.append(cp)
    back_recv[pl.ds(x, 1)] = back_send[pl.ds(x, 1)]
    for cp in bs:
        cp.wait()

    for pp in range(8):
        q, p = pp // 2, pp % 2
        f0 = both[0, pp * 64 : pp * 64 + 64, :]
        r1 = both[1, 512 + pp * 64 : 576 + pp * 64, :]
        m0 = both[0, 1024 + pp * 8 : 1032 + pp * 8, :]
        m1 = both[1, 1024 + pp * 8 : 1032 + pp * 8, :]
        t0, first0, last0 = m0[0:1], m0[1:2], m0[2:3]
        t1, first1, last1 = m1[0:1], m1[1:2], m1[2:3]
        g8 = gain_ref[pl.ds(c * 8 + pp, 1)][0][0:1]
        sf = back_recv[q, p * 64 : p * 64 + 64, :]
        sr = back_recv[q, 128 + p * 64 : 192 + p * 64, :]
        link = g8 * same(last0, first1)
        own_blocks[0, pp * 64 : pp * 64 + 64, :] = sf
        own_blocks[1, pp * 64 : pp * 64 + 64, :] = linked(first0, first1, t0) * sf + link * f0
        own_blocks[0, 512 + pp * 64 : 576 + pp * 64, :] = (
            linked(last0, last1, t1) * sr + link * r1
        )
        own_blocks[1, 512 + pp * 64 : 576 + pp * 64, :] = sr
    last_swap = remote(own_blocks.at[1 - c], out_ref.at[c], s_fin, r_fin, sib)
    last_swap.start()
    out_ref[pl.ds(c, 1)] = own_blocks[pl.ds(c, 1)]

    for n, (index, buf) in enumerate(((y, hy), (z, hz))):
        buf[pl.ds(index, 1), pl.ds(c, 1)] = hid_ref[...][None, None]
        fwd[2 * n].wait()
        fwd[2 * n + 1].wait()
        came = ring(index, 2)
        cp = remote(buf.at[came, c], buf.at[came, c], s_d.at[n, 3], r_d.at[n, 3], sib)
        cp.start()
        down.append(cp)
    last_swap.wait()
    for cp in down:
        cp.wait()
    for buf, out in ((hy, hy_out), (hz, hz_out)):
        for g in range(8):
            out[:, g * TOK : (g + 1) * TOK] = buf[g // 2, g % 2].astype(BF16)


def exchange(st, hidden_t, gain_rows):
    vm = pl.BlockSpec(memory_space=pltpu.VMEM)
    depth = hidden_t.shape[0]
    dma = pltpu.SemaphoreType.DMA
    return pl.pallas_call(
        exchange_kernel,
        in_specs=[vm] * 3,
        out_specs=[vm] * 4,
        out_shape=[
            jax.ShapeDtypeStruct((2, SROWS, PAIR), F32),
            jax.ShapeDtypeStruct((8, 8, PAIR), F32),
            jax.ShapeDtypeStruct((depth, 8 * TOK), BF16),
            jax.ShapeDtypeStruct((depth, 8 * TOK), BF16),
        ],
        scratch_shapes=[
            pltpu.VMEM((2, HALF_ROWS, PAIR), F32),
            pltpu.VMEM((4, 272, PAIR), F32),
            pltpu.VMEM((4, 272, PAIR), F32),
            pltpu.VMEM((2, 144, PAIR), F32),
            pltpu.VMEM((2, 144, PAIR), F32),
            pltpu.VMEM((4, 256, PAIR), F32),
            pltpu.VMEM((4, 256, PAIR), F32),
            pltpu.VMEM((2, SROWS, PAIR), F32),
            pltpu.VMEM((4, 2, depth, TOK), F32),
            pltpu.VMEM((4, 2, depth, TOK), F32),
            dma,
            dma,
            dma((3,)),
            dma((3,)),
            dma((2,)),
            dma((2,)),
            dma((3,)),
            dma((3,)),
            dma,
            dma,
            dma((2, 2)),
            dma((2, 2)),
            dma((2, 2)),
            dma((2, 2)),
            dma((2, 4)),
            dma((2, 4)),
        ],
        compiler_params=pltpu.CompilerParams(
            collective_id=0, has_side_effects=True, vmem_limit_bytes=40 * 2**20
        ),
        name="exchange",
    )(st, hidden_t, gain_rows)


def grads_kernel(
    k_ref,
    v_ref,
    q_ref,
    g_ref,
    lg_ref,
    segc_ref,
    segr_ref,
    gain_ref,
    s_ref,
    qg_ref,
    ks_ref,
    vs_ref,
    ksb_ref,
    vsb_ref,
    gate_ref,
    gsum_ref,
):
    step = pl.program_id(0)
    rows_i, cols_i = iota((TOK, TOK), 0), iota((TOK, TOK), 1)
    causal = cols_i <= rows_i
    seg_col, seg_row = segc_ref[...], segr_ref[...]
    allowed = causal & (seg_col == seg_row)
    lower = causal.astype(F32)
    strict = (rows_i < cols_i).astype(BF16)
    tail = (cols_i <= rows_i).astype(BF16)
    gap = jnp.bitwise_xor(rows_i, cols_i)
    cum_cols = dot_exact(lower, lg_ref[0], NT)
    cum_rows = dot_exact(lg_ref[0], lower, NT)
    low = iota((TOK, PAIR), 1) < 64
    low_half = iota((64, PAIR), 1) < 64
    half = step // 4
    head_pick = (iota((8, PAIR), 1) // 64 == iota((8, PAIR), 0)).astype(BF16)
    zero = jnp.zeros((TOK, PAIR), BF16)
    gate_rows, gain_rows = [], []
    for p in range(2):
        cols = slice(p * PAIR, (p + 1) * PAIR)
        k, v, q, g = (r[:, cols] for r in (k_ref, v_ref, q_ref, g_ref))
        kf, qf = k.astype(F32), q.astype(F32)
        pp = 2 * (step % 4) + p
        sf = s_ref[half, pl.ds(pl.multiple_of(pp * 64, 64), 64), :]
        sr = s_ref[half, pl.ds(pl.multiple_of(512 + pp * 64, 64), 64), :]

        def diag(s):
            return jnp.concatenate([jnp.where(low_half, s, 0.0), jnp.where(low_half, 0.0, s)], axis=0)

        first_w, last_w, _ = token_weights(pair_cumulative(cum_cols, p, low), seg_col)
        sg = first_w * dot_right(g, diag(sf), NT)
        rv = last_w * dot_right(v, diag(sr), NT)
        rk = last_w * dot_right(k, diag(sr), NN)
        diff = qf * sg - kf * rv
        hi, lo = split2(diff)
        diff_rows = dot(head_pick, hi, NT) + dot(head_pick, lo, NT)
        cross_rows = dot_left(diff_rows, tail, NN)

        weighted, scored, queries, keys, grads = [], [], [], [], []
        for h in range(2):
            head = 2 * p + h

            def own(a):
                return jnp.where(low, a, zero) if h == 0 else jnp.where(low, zero, a)

            qh, gh, kh = own(q), own(g), own(k)
            score = dot(qh, k, NT)
            dprob = dot(gh, v, NT)
            spread = cum_cols[:, head : head + 1] - cum_rows[head : head + 1, :]
            decay = jnp.where(allowed, jnp.exp(jnp.where(allowed, spread, 0.0)), 0.0)
            ds = decay * score
            joint = ds * dprob
            level = jnp.full((TOK, TOK), gain_ref[4 * step + head, 0], F32)
            gain_rows.append(jnp.sum(jnp.where(gap == 0, joint, 0.0), axis=0, keepdims=True))
            for l in range(1, 8):
                above = gap >= 2 ** (l - 1)
                level = jnp.where(above, gain_ref[4 * step + head, l], level)
                chosen = above & (gap < 2**l)
                gain_rows.append(jnp.sum(jnp.where(chosen, joint, 0.0), axis=0, keepdims=True))
            wd = level * decay * dprob
            weighted.append(wd.astype(BF16))
            scored.append((level * ds).astype(BF16))
            grid = (wd * score).astype(BF16)
            crossing = jnp.where(causal, dot(grid, strict, NN), 0.0)
            gate_rows.append(
                jnp.sum(crossing, axis=0, keepdims=True) + cross_rows[h : h + 1, :]
            )
            queries.append(qh)
            keys.append(kh)
            grads.append(gh)
        query_acc = dot(jnp.concatenate(weighted, axis=1), jnp.concatenate(keys, axis=0), NN)
        key_acc = dot(jnp.concatenate(weighted, axis=0), jnp.concatenate(queries, axis=0), TN)
        value_acc = dot(jnp.concatenate(scored, axis=0), jnp.concatenate(grads, axis=0), TN)
        qg_ref[:, cols] = (query_acc + sg).astype(BF16)
        ks = (key_acc + rv).astype(BF16)
        vs = (value_acc + rk).astype(BF16)
        ksb_ref[:, cols] = ks
        vsb_ref[:, cols] = vs
        ks_ref[0, :, cols] = ks.astype(F32)
        vs_ref[0, :, cols] = vs.astype(F32)
    gate_ref[0] = jnp.concatenate(gate_rows, axis=0)
    gsum_ref[0] = jnp.concatenate(gain_rows, axis=0)


def block_grads(keys, values, queries, out_grad, log_gate4, seg_col, seg_row, level_gain, states):
    cols = queries.shape[1]
    steps = cols // 256
    block = pl.BlockSpec((TOK, 256), lambda i: (0, i))
    slab = pl.BlockSpec((1, TOK, 256), lambda i: (i, 0, 0))
    return pl.pallas_call(
        grads_kernel,
        grid=(steps,),
        in_specs=[
            block,
            block,
            block,
            block,
            pl.BlockSpec((1, 4, TOK), lambda i: (i, 0, 0)),
            pl.BlockSpec((TOK, 1), lambda i: (0, 0)),
            pl.BlockSpec((1, TOK), lambda i: (0, 0)),
            pl.BlockSpec(memory_space=pltpu.SMEM),
            pl.BlockSpec((2, SROWS, PAIR), lambda i: (0, 0, 0)),
        ],
        out_specs=[
            block,
            slab,
            slab,
            block,
            block,
            pl.BlockSpec((1, 4, TOK), lambda i: (i, 0, 0)),
            pl.BlockSpec((1, 32, TOK), lambda i: (i, 0, 0)),
        ],
        out_shape=[
            jax.ShapeDtypeStruct((TOK, cols), BF16),
            jax.ShapeDtypeStruct((steps, TOK, 256), F32),
            jax.ShapeDtypeStruct((steps, TOK, 256), F32),
            jax.ShapeDtypeStruct((TOK, cols), BF16),
            jax.ShapeDtypeStruct((TOK, cols), BF16),
            jax.ShapeDtypeStruct((steps, 4, TOK), F32),
            jax.ShapeDtypeStruct((steps, 32, TOK), F32),
        ],
        compiler_params=pltpu.CompilerParams(dimension_semantics=("arbitrary",)),
        name="grads",
    )(keys, values, queries, out_grad, log_gate4, seg_col, seg_row, level_gain, states)


def weights_kernel(
    ks_ref,
    vs_ref,
    hy_ref,
    hz_ref,
    small_ref,
    kout_ref,
    vout_ref,
    sout_ref,
    rk,
    rv,
    pk,
    pv,
    zk,
    xv,
    zsum,
    xsum,
    xk,
    yv,
    ksum,
    vsum,
    kfin,
    vfin,
    m1,
    m1s,
    m2,
    m2s,
    m3,
    s_k,
    r_k,
    s_v,
    r_v,
    s_zk,
    r_zk,
    s_xv,
    r_xv,
    s_xk,
    r_xk,
    s_yv,
    r_yv,
    s_kf,
    r_kf,
    s_vf,
    r_vf,
    s_m1,
    r_m1,
    s_m2,
    r_m2,
    s_m3,
    r_m3,
):
    x, y, z, c = (lax.axis_index(a) for a in ("x", "batch", "z", "core"))
    offsets = [(d, e) for d in range(4) for e in (0, 1) if d or e]

    def plane(axis, index, d, e):
        to, tc = ring(index, d), lax.rem(c + e, 2)
        return {axis: to, "core": tc}, to, tc

    peers = [plane("batch", y, d, e)[0] for d, e in offsets]
    peers += [plane("z", z, d, e)[0] for d, e in offsets if d]
    peers += [{"x": ring(x, d)} for d in (1, 2, 3)]
    entry_barrier(peers)

    firsts_k, firsts_v, smalls = [], [], []
    for n, (d, e) in enumerate(offsets):
        dev, to, tc = plane("batch", y, d, e)
        cp = remote(ks_ref.at[2 * to + tc], rk.at[2 * y + c], s_k.at[n], r_k.at[n], dev)
        cp.start()
        firsts_k.append(cp)
        dev, to, tc = plane("z", z, d, e)
        cp = remote(vs_ref.at[2 * to + tc], rv.at[2 * z + c], s_v.at[n], r_v.at[n], dev)
        cp.start()
        firsts_v.append(cp)
        cp = remote(small_ref, m1.at[2 * z + c], s_m1.at[n], r_m1.at[n], dev)
        cp.start()
        smalls.append(cp)
    rk[pl.ds(2 * y + c, 1)] = ks_ref[pl.ds(2 * y + c, 1)]
    rv[pl.ds(2 * z + c, 1)] = vs_ref[pl.ds(2 * z + c, 1)]
    m1[pl.ds(2 * z + c, 1)] = small_ref[...][None]

    for cp in smalls:
        cp.wait()
    total = m1[0, 0:8, :]
    for g in range(1, 8):
        total = total + m1[g, 0:8, :]
    m1s[0:8, :] = total
    for g in range(8):
        m1s[8 + g : 9 + g, :] = m1[g, 8:9, :]
    smalls = []
    for d in (1, 2, 3):
        cp = remote(m1s, m2.at[x], s_m2.at[d - 1], r_m2.at[d - 1], {"x": ring(x, d)})
        cp.start()
        smalls.append(cp)
    m2[pl.ds(x, 1)] = m1s[...][None]

    for cp in firsts_k:
        cp.wait()
    right = rk[...].reshape(8 * TOK, 256).astype(BF16)
    for b in range(4):
        pk[b] = dot(hy_ref[b * 256 : (b + 1) * 256, :], right, NN)
    zks = []
    for d in (1, 2, 3):
        to = ring(z, d)
        cp = remote(pk.at[to], zk.at[z], s_zk.at[d - 1], r_zk.at[d - 1], {"z": to})
        cp.start()
        zks.append(cp)
    zk[pl.ds(z, 1)] = pk[pl.ds(z, 1)]

    for cp in firsts_v:
        cp.wait()
    right = rv[...].reshape(8 * TOK, 256).astype(BF16)
    for b in range(4):
        part = dot(hz_ref[b * 256 : (b + 1) * 256, :], right, NN)
        for j in range(4):
            pv[j, b] = part[j * 64 : (j + 1) * 64, :]
    xvs = []
    for d in (1, 2, 3):
        to = ring(x, d)
        cp = remote(pv.at[to], xv.at[x], s_xv.at[d - 1], r_xv.at[d - 1], {"x": to})
        cp.start()
        xvs.append(cp)
    xv[pl.ds(x, 1)] = pv[pl.ds(x, 1)]

    for cp in smalls:
        cp.wait()
    total = m2[0, 0:8, :] + m2[1, 0:8, :] + m2[2, 0:8, :] + m2[3, 0:8, :]
    m2s[...] = total
    place = z * 8 + x * 2 + c
    later = jnp.zeros((1, PAIR), F32)
    for j in range(4):
        for g in range(8):
            spot = (g // 2) * 8 + j * 2 + g % 2
            later = later + (place < spot).astype(F32) * m2[j, 8 + g : 9 + g, :]
    smalls = []
    for d in (1, 2, 3):
        cp = remote(m2s, m3.at[y], s_m3.at[d - 1], r_m3.at[d - 1], {"batch": ring(y, d)})
        cp.start()
        smalls.append(cp)
    m3[pl.ds(y, 1)] = total[None]
    sout_ref[8:16, :] = jnp.broadcast_to(later, (8, PAIR))

    for cp in zks:
        cp.wait()
    zsum[...] = (zk[0] + zk[1] + zk[2] + zk[3]).reshape(4, 64, 256)
    xks = []
    for d in (1, 2, 3):
        to = ring(x, d)
        cp = remote(zsum.at[to], xk.at[x], s_xk.at[d - 1], r_xk.at[d - 1], {"x": to})
        cp.start()
        xks.append(cp)
    xk[pl.ds(x, 1)] = zsum[pl.ds(x, 1)]

    for cp in xvs:
        cp.wait()
    part = xv[0] + xv[1] + xv[2] + xv[3]
    for zz in range(4):
        for cc in range(2):
            for yy in range(4):
                at = cc * 32 + yy * 8
                xsum[yy, 2 * zz + cc] = part[zz, at : at + 8, :]
    yvs = []
    for d in (1, 2, 3):
        to = ring(y, d)
        cp = remote(xsum.at[to], yv.at[y], s_yv.at[d - 1], r_yv.at[d - 1], {"batch": to})
        cp.start()
        yvs.append(cp)
    yv[pl.ds(y, 1)] = xsum[pl.ds(y, 1)]

    for cp in smalls:
        cp.wait()
    sout_ref[0:8, :] = m3[0] + m3[1] + m3[2] + m3[3]

    for cp in xks:
        cp.wait()
    part = xk[0] + xk[1] + xk[2] + xk[3]
    for yy in range(4):
        for cc in range(2):
            at = cc * 32 + yy * 8
            ksum[2 * yy + cc] = part[at : at + 8, :]
    fins = []
    for n, (d, e) in enumerate(offsets):
        dev, to, tc = plane("batch", y, d, e)
        cp = remote(ksum.at[2 * to + tc], kfin.at[2 * y + c], s_kf.at[n], r_kf.at[n], dev)
        cp.start()
        fins.append(cp)
    kfin[pl.ds(2 * y + c, 1)] = ksum[pl.ds(2 * y + c, 1)]

    for cp in yvs:
        cp.wait()
    vsum[...] = yv[0] + yv[1] + yv[2] + yv[3]
    for n, (d, e) in enumerate(offsets):
        dev, to, tc = plane("z", z, d, e)
        cp = remote(vsum.at[2 * to + tc], vfin.at[2 * z + c], s_vf.at[n], r_vf.at[n], dev)
        cp.start()
        fins.append(cp)
    vfin[pl.ds(2 * z + c, 1)] = vsum[pl.ds(2 * z + c, 1)]
    for cp in fins:
        cp.wait()
    for g in range(8):
        kout_ref[:, g * 256 : (g + 1) * 256] = kfin[g]
        vout_ref[:, g * 256 : (g + 1) * 256] = vfin[g]


def weight_grads(ks, vs, hy, hz, small):
    vm = pl.BlockSpec(memory_space=pltpu.VMEM)
    dma = pltpu.SemaphoreType.DMA

    def buf(*shape):
        return pltpu.VMEM(shape, F32)

    sems = []
    for n in (7, 7, 3, 3, 3, 3, 7, 7, 7, 3, 3):
        sems += [dma((n,)), dma((n,))]
    return pl.pallas_call(
        weights_kernel,
        in_specs=[vm] * 5,
        out_specs=[vm] * 3,
        out_shape=[
            jax.ShapeDtypeStruct((8, 2048), F32),
            jax.ShapeDtypeStruct((8, 2048), F32),
            jax.ShapeDtypeStruct((16, PAIR), F32),
        ],
        scratch_shapes=[
            buf(8, TOK, 256),
            buf(8, TOK, 256),
            buf(4, 256, 256),
            buf(4, 4, 64, 256),
            buf(4, 256, 256),
            buf(4, 4, 64, 256),
            buf(4, 64, 256),
            buf(4, 8, 8, 256),
            buf(4, 64, 256),
            buf(4, 8, 8, 256),
            buf(8, 8, 256),
            buf(8, 8, 256),
            buf(8, 8, 256),
            buf(8, 8, 256),
            buf(8, 16, PAIR),
            buf(16, PAIR),
            buf(4, 16, PAIR),
            buf(8, PAIR),
            buf(4, 8, PAIR),
            *sems,
        ],
        compiler_params=pltpu.CompilerParams(
            collective_id=1, has_side_effects=True, vmem_limit_bytes=40 * 2**20
        ),
        name="weights",
    )(ks, vs, hy, hz, small)


def local(hidden, queries, w_key, w_value, log_gate, level_gain, segment_ids, out_grad):
    heads, levels = level_gain.shape
    core = lax.axis_index("core")
    hidden_rows, query_rows, grad_rows = hidden[0], queries[0], out_grad[0]
    log_gate4 = log_gate[0].reshape(heads // 4, 4, TOK)
    seg_row = segment_ids
    seg_col = segment_ids.reshape(TOK, 1)
    hidden_t = hidden_rows.T.astype(F32)
    cross = jnp.pad(level_gain[:, 8:13], ((0, 0), (0, 3)))
    gain_rows = jnp.repeat(cross.reshape(16, 2, 8).transpose(0, 2, 1), 64, axis=2)
    keys, values, states = block_states(
        hidden_rows, w_key, w_value, query_rows, grad_rows, log_gate4, seg_col
    )
    incoming, cross_sums, hy, hz = exchange(states, hidden_t, gain_rows)
    query_grad, ks, vs, key_sum, value_sum, gate, gain_sums = block_grads(
        keys, values, query_rows, grad_rows, log_gate4, seg_col, seg_row, level_gain, incoming
    )
    gate = gate.reshape(heads, TOK)
    inner = jnp.sum(gain_sums, axis=2).reshape(heads, 8)
    outer = jnp.sum(cross_sums.reshape(8, 8, 2, 64), axis=3).transpose(0, 2, 1).reshape(16, 8)
    outer = jnp.where(
        (jnp.arange(heads) // 16 == core)[:, None], jnp.concatenate([outer, outer], axis=0), 0.0
    )
    gains = jnp.concatenate([inner, outer, jnp.zeros((heads, 16), F32)], axis=1)
    own_total = jnp.pad(gate[:, 0][None], ((0, 7), (0, 96)))
    small = jnp.concatenate([gains.reshape(8, 128), own_total], axis=0)
    key_weight, value_weight, summed = weight_grads(ks, vs, hy, hz, small)
    input_grad = (dot(key_sum, w_key, NT) + dot(value_sum, w_value, NT)).astype(BF16)
    gain_total = summed[:8].reshape(heads, 32)[:, :levels]
    gate_grad = gate + summed[8, :heads][:, None]
    return (
        query_grad[None],
        input_grad[None],
        gate_grad[None],
        key_weight,
        value_weight,
        gain_total,
    )


def solution(mesh):
    split = Mesh(
        mesh.devices.reshape(4, 4, 2, mesh.shape["batch"]), ("z", "x", "core", "batch")
    )
    return jax.shard_map(
        local,
        mesh=split,
        in_specs=(
            P("batch", SEQ, None),
            P("batch", SEQ, None),
            P(),
            P(),
            P("batch", None, SEQ),
            P(),
            P("batch", SEQ),
            P("batch", SEQ, None),
        ),
        out_specs=(
            P("batch", SEQ, None),
            P("batch", SEQ, None),
            P("batch", None, SEQ),
            P(SEQ_BATCH, None),
            P(SEQ_BATCH, None),
            P(),
        ),
        check_vma=False,
    )
```

time: 527 us -> 132 us (0.25); the launches traced: 518 us -> 130 us
  waiting for transfers between devices: 202 us -> 0 us
  Pallas kernels: 0 us -> 105 us
  other arithmetic: 68.1 us -> 2.04 us
  matrix products: 61.2 us -> 6.07 us
  blocking collectives: 52.4 us -> 0 us
  starting transfers between devices: 44.9 us -> 0 us
  local copies, waits for them, and re-layouts: 53.5 us -> 16.2 us
  between operations: 28.6 us -> 0.81 us
  loops' own time: 6.79 us -> 0 us
    ppermute x24 -> x0, waiting for transfers between devices: 155 us -> none  [partner(): return lax.ppermute(value, axis, pairs)]
    pallas_call x0 -> x4, Pallas kernels: none -> 105 us  [the longest x1 41.2 us: weight_grads(): pl.pallas_call(weights_kernel, in_specs=[vm] * 5, out_specs=[vm] * 3, out...]
    dot_general x42 -> x2, matrix products: 61.2 us -> 6.07 us  [dot(): return lax.dot_general(a, b, dims, preferred_element_type=F32)]
    psum x4 -> x0, blocking collectives: 52.4 us -> none  [over_axes(): x = lax.psum(x, axis)]
    reduce_scatter x1 -> x0, waiting for transfers between devices: 39.4 us -> none  [local(): lax.psum_scatter(lax.dot_general(hidden_rows, both_grads, (((0,), (0,)),...]
    ppermute x24 -> x0, starting transfers between devices: 36.5 us -> none  [partner(): return lax.ppermute(value, axis, pairs)]
    another operation x52 -> x0, other arithmetic: 33.2 us -> none
    broadcast_in_dim x7 -> x0, other arithmetic: 11.7 us -> none  [the longest x1 8.79 us: cross_terms(): jnp.where((segment == rev_key)[None], jnp.exp(block_decay[:, None] - cumu...]
  transfers between devices with their start and end apart: 27 -> 0, of which waited for: 15 -> 0; matrix products, arithmetic and copies ran while one was open for 25% -> 0% of each run, Pallas kernels for 0% -> 0%
where the time goes in v1:
time: 132 us; the launch traced here: 130 us
  Pallas kernels  105 us (80%)
  local copies, waits for them, and re-layouts  16.2 us (12%)
  matrix products  6.07 us (5%)
  other arithmetic  2.04 us (2%)
    pallas_call x1, Pallas kernels, weight_grads(): pl.pallas_call(weights_kernel, in_specs=[vm] * 5, out_specs=[vm] * 3, out...  41.2 us
    pallas_call x1, Pallas kernels, exchange(): pl.pallas_call(exchange_kernel, in_specs=[vm] * 3, out_specs=[vm] * 4, ou...  34.2 us
    pallas_call x1, Pallas kernels, block_grads(): pl.pallas_call(grads_kernel, grid=(steps,), in_specs=[block, block, block...  18.6 us
    unnamed x27, local copies, waits for them, and re-layouts  13 us
    pallas_call x1, Pallas kernels, block_states(): pl.pallas_call(states_kernel, grid=(steps,), in_specs=[pl.BlockSpec((TOK,...  10.7 us
    dot_general x2, matrix products, dot(): return lax.dot_general(a, b, dims, preferred_element_type=F32)  6.07 us

profile of v1, /device:TPU:0, one launch (start us, length us, event | category | flops | bytes accessed | tf_op | source)
XLA Modules:
  0.0 129.9 jit_solution(12194246194927517038)
XLA Ops:
  0.7 0.7 slice.17
  1.4 0.1 copy.47
  1.5 1.4 %copy.37.gain_ref = f32[32,18]{1,0:T(8,128)} copy(f32[32,18]{0,1:T(8,128)} %param.13) | data formatting | bytes 4608 | tf_op args[5]
  2.9 0.2 copy.35
  3.1 1.4 %copy.33.seg_ref.segc_ref = s32[128,1]{1,0:T(8,128)} copy(s32[128,1]{0,1:T(1,128)} %bitcast.44) | data formatting | bytes 1024 | tf_op jit(solution)/shard_map/reshape | solution.py:867
  4.5 0.2 broadcast_in_dim.26
  4.7 0.1 reshape.92.gain_ref
  4.8 1.1 copy.31
  6.0 10.7 %states.1 = (bf16[128,2048]{1,0:T(8,128)(2,1)}, bf16[128,2048]{1,0:T(8,128)(2,1)}, f32[2,1088,128]{2,1,0:T(8,128)}) custom-call(bf16[128,1024]{1,0:T(8,128)(2,1)} %bitcast.34, bf16[1024,2048]{1,0:T(8,128)(2,1)} %wk_ref.1, bf16[1024,2048]{1,0:T(8,128)(2,1)} %wv_ref.1, bf16[128,2048]{1,0:T(8,128)(2,1)} %bitcast.30, bf16[128,2048]{1,0:T(8,128)(2,1)} %bitcast.32, ...), custom_call_target="tpu_custom_call" | custom-call | tf_op jit(solution)/shard_map/states/pallas_call | solution.py:108
  16.6 1.2 copy-done.2
  17.9 34.2 %exchange.1 = (f32[2,1024,128]{2,1,0:T(8,128)S(1)}, f32[8,8,128]{2,1,0:T(8,128)S(1)}, bf16[1024,1024]{1,0:T(8,128)(2,1)S(1)}, bf16[1024,1024]{1,0:T(8,128)(2,1)S(1)}) custom-call(f32[2,1088,128]{2,1,0:T(8,128)S(1)} %copy-done.2, f32[1024,128]{1,0:T(8,128)S(1)} %convert_bitcast_fusion.hid_ref, f32[16,8,128]{2,1,0:T(8,128)S(1)} %reshape.92.gain_ref), custom_call_target="tpu_custom_call" | custom-call | tf_op jit(solution)/shard_map/exchange/pallas_call | solution.py:422
  52.1 1.3 %copy-done = bf16[1024,1024]{1,0:T(8,128)(2,1)} copy-done((bf16[1024,1024]{1,0:T(8,128)(2,1)}, bf16[1024,1024]{1,0:T(8,128)(2,1)S(1)}, u32[]{:S(2)}) %copy-start) | copy-done | bytes 2097176
  53.5 1.0 copy-done.3
  54.4 0.1 reshape.95
  54.5 0.1 reduce_sum.19
  54.7 0.1 copy.38
  54.9 0.1 maximum_select_fusion
  54.9 0.1 copy.41
  55.0 18.6 %grads.1 = (bf16[128,2048]{1,0:T(8,128)(2,1)}, f32[8,128,256]{2,1,0:T(8,128)}, f32[8,128,256]{2,1,0:T(8,128)}, bf16[128,2048]{1,0:T(8,128)(2,1)}, bf16[128,2048]...) custom-call(bf16[128,2048]{1,0:T(8,128)(2,1)} %get-tuple-element.23.k_ref, ...), custom_call_target="tpu_custom_call" | custom-call | tf_op jit(solution)/shard_map/grads/pallas_call | solution.py:573
  73.7 0.9 copy.45
  74.5 1.0 reduce_sum.18
  75.6 0.1 maximum_maximum_fusion
  75.8 1.6 %copy-done.1 = bf16[1024,1024]{1,0:T(8,128)(2,1)S(1)} copy-done((bf16[1024,1024]{1,0:T(8,128)(2,1)S(1)}, bf16[1024,1024]{1,0:T(8,128)(2,1)}, u32[]{:S(2)}) %copy-start.1) | copy-done | bytes 2097176
  77.4 1.2 copy-done.4
  78.6 1.2 copy-done.5
  79.8 41.2 %weights.1 = (f32[8,2048]{1,0:T(8,128)S(1)}, f32[8,2048]{1,0:T(8,128)S(1)}, f32[16,128]{1,0:T(8,128)S(1)}) custom-call(f32[8,128,256]{2,1,0:T(8,128)S(1)} %copy-done.4, f32[8,128,256]{2,1,0:T(8,128)S(1)} %copy-done.5, bf16[1024,1024]{1,0:T(8,128)(2,1)S(1)} %get-tuple-element.33.hy_ref, bf16[1024,1024]{1,0:T(8,128)(2,1)S(1)} %copy-done.1, ...), custom_call_target="tpu_custom_call" | custom-call | tf_op jit(solution)/shard_map/weights/pallas_call | solution.py:823
  121.1 0.7 bitcast_add_fusion
  121.9 0.7 copy.46
  122.5 3.8 %fusion.3 = f32[128,1024]{1,0:T(8,128)S(1)} fusion(bf16[128,2048]{1,0:T(8,128)(2,1)S(1)} %copy-done.7, bf16[1024,2048]{1,0:T(8,128)(2,1)} %wk_ref.1), kind=kOutput, calls=%fused_computation.15 | convolution fusion | flops 536870912 | bytes 5242880 | tf_op jit(solution)/shard_map/dot_general | solution.py:29
  126.4 2.2 %fusion.1 = bf16[1,128,1024]{2,1,0:T(8,128)(2,1)} fusion(f32[128,1024]{1,0:T(8,128)S(1)} %fusion.3, bf16[128,2048]{1,0:T(8,128)(2,1)S(1)} %copy-done.8, bf16[1024,2048]{1,0:T(8,128)(2,1)S(1)} %copy-done.6), kind=kOutput, calls=%fused_computation.2 | convolution fusion | flops 537133056 | bytes 5505024 | tf_op jit(solution)/shard_map/dot_general | solution.py:29
  128.6 0.6 copy.50
  129.3 0.6 copy.51
  (26 shorter events, 0.5 us)
Async XLA Ops:
  16.6 1.2 copy-start.2
  52.1 1.3 %copy-start = (bf16[1024,1024]{1,0:T(8,128)(2,1)}, bf16[1024,1024]{1,0:T(8,128)(2,1)S(1)}, u32[]{:S(2)}) copy-start(bf16[1024,1024]{1,0:T(8,128)(2,1)S(1)} %get-tuple-element.34.hz_ref) | copy-start | bytes 6291460
  53.5 1.0 copy-start.3
  73.7 47.4 %copy-start.9 = (f32[8,4,128]{2,1,0:T(4,128)S(1)}, f32[8,4,128]{2,1,0:T(4,128)}, u32[]{:S(2)}) copy-start(f32[8,4,128]{2,1,0:T(4,128)} %get-tuple-element.30) | copy-start | bytes 49156
  75.8 1.6 %copy-start.1 = (bf16[1024,1024]{1,0:T(8,128)(2,1)S(1)}, bf16[1024,1024]{1,0:T(8,128)(2,1)}, u32[]{:S(2)}) copy-start(bf16[1024,1024]{1,0:T(8,128)(2,1)} %copy-done) | copy-start | bytes 6291460
  77.4 1.2 copy-start.4
  78.6 1.2 copy-start.5
  79.8 42.7 %copy-start.7 = (bf16[128,2048]{1,0:T(8,128)(2,1)S(1)}, bf16[128,2048]{1,0:T(8,128)(2,1)}, u32[]{:S(2)}) copy-start(bf16[128,2048]{1,0:T(8,128)(2,1)} %get-tuple-element.28) | copy-start | bytes 1572868
  121.1 5.3 %copy-start.8 = (bf16[128,2048]{1,0:T(8,128)(2,1)S(1)}, bf16[128,2048]{1,0:T(8,128)(2,1)}, u32[]{:S(2)}) copy-start(bf16[128,2048]{1,0:T(8,128)(2,1)} %get-tuple-element.29) | copy-start | bytes 1572868
  122.5 3.9 %copy-start.6 = (bf16[1024,2048]{1,0:T(8,128)(2,1)S(1)}, bf16[1024,2048]{1,0:T(8,128)(2,1)}, u32[]{:S(2)}) copy-start(bf16[1024,2048]{1,0:T(8,128)(2,1)} %wv_ref.1) | copy-start | bytes 12582916

commit v2 on v0

v2 whole, which is shorter than its diff:
```python
import functools

import jax
import jax.numpy as jnp
from jax import lax
from jax.experimental import pallas as pl
from jax.experimental.pallas import tpu as pltpu
from jax.sharding import Mesh
from jax.sharding import PartitionSpec as P

SEQ = ("z", "x", "core")
SEQ_BATCH = ("z", "x", "core", "batch")
MESH = pl.DeviceIdType.MESH
HIGHEST = lax.Precision.HIGHEST
F32 = jnp.float32
BF16 = jnp.bfloat16

NT = (((1,), (1,)), ((), ()))
TN = (((0,), (0,)), ((), ()))
NN = (((1,), (0,)), ((), ()))

TOK = 128
PAIR = 128
HALF_ROWS = 1088
SROWS = 1024


def dot(a, b, dims):
    return lax.dot_general(a, b, dims, preferred_element_type=F32)


def dot_exact(a, b, dims):
    return lax.dot_general(a, b, dims, preferred_element_type=F32, precision=HIGHEST)


def split2(x):
    hi = x.astype(BF16)
    return hi, (x - hi.astype(F32)).astype(BF16)


def dot_left(a, b, dims):
    hi, lo = split2(a)
    return dot(hi, b, dims) + dot(lo, b, dims)


def dot_right(a, b, dims):
    hi, lo = split2(b)
    return dot(a, hi, dims) + dot(a, lo, dims)


def iota(shape, dim):
    return lax.broadcasted_iota(jnp.int32, shape, dim)


def entry_signal(peers):
    barrier = pltpu.get_barrier_semaphore()
    for peer in peers:
        pl.semaphore_signal(barrier, inc=1, device_id=peer, device_id_type=MESH)
    return barrier


def ring(index, step):
    return lax.rem(index + step, 4)


def same(a, b):
    return jnp.where(a == b, 1.0, 0.0)


def linked(a, b, total):
    return jnp.where(a == b, jnp.exp(total), 0.0)


def rows_of(start, size):
    return pl.ds(pl.multiple_of(start, size), size)


SENDS = 128
LOCALS = 24


def scratch():
    def f(*shape):
        return pltpu.VMEM(shape, F32)

    def b(*shape):
        return pltpu.VMEM(shape, BF16)

    return dict(
        wk=b(1024, 2048),
        wv=b(1024, 2048),
        hid=b(TOK, 1024),
        q=b(TOK, 2048),
        g=b(TOK, 2048),
        k=b(16, TOK, PAIR),
        v=b(16, TOK, PAIR),
        hid_t=f(1024, TOK),
        cumx=f(16, TOK, PAIR),
        cumr=f(32, TOK),
        cumr3=f(16, 8, TOK),
        fw=f(16, TOK, PAIR),
        lw=f(16, TOK, PAIR),
        segc=f(TOK, TOK),
        st=f(2, HALF_ROWS, PAIR),
        both=f(2, HALF_ROWS, PAIR),
        chip_send=f(4, 272, PAIR),
        chip_recv=f(4, 272, PAIR),
        tot_send=f(2, 144, PAIR),
        tot_recv=f(2, 144, PAIR),
        back_send=f(4, 256, PAIR),
        back_recv=f(4, 256, PAIR),
        own_blocks=f(2, SROWS, PAIR),
        s_in=f(2, SROWS, PAIR),
        gcross=f(16, 8, PAIR),
        gint=f(16, 16, PAIR),
        gate=f(16, 8, TOK),
        hy=f(4, 2, 1024, TOK),
        hz=f(4, 2, 1024, TOK),
        hyb=b(1024, 8 * TOK),
        hzb=b(1024, 8 * TOK),
        qacc=f(16, TOK, PAIR),
        kacc=f(16, TOK, PAIR),
        vacc=f(16, TOK, PAIR),
        ks=f(2, 8, TOK, PAIR),
        vs=f(2, 8, TOK, PAIR),
        ksb=b(TOK, 2048),
        vsb=b(TOK, 2048),
        rk=f(2, 8, TOK, PAIR),
        rv=f(2, 8, TOK, PAIR),
        part1=f(4, 4, 256, PAIR),
        recv1=f(4, 4, 256, PAIR),
        part2=f(4, 4, 64, PAIR),
        recv2=f(4, 4, 64, PAIR),
        kown=f(8, 2, 8, PAIR),
        vown=f(8, 2, 8, PAIR),
        kfin=f(8, 2, 8, PAIR),
        vfin=f(8, 2, 8, PAIR),
        small=f(16, PAIR),
        m1=f(8, 16, PAIR),
        m1s=f(16, PAIR),
        m2=f(4, 16, PAIR),
        m2s=f(8, PAIR),
        m3=f(4, 8, PAIR),
        send_sem=pltpu.SemaphoreType.DMA((SENDS,)),
        recv_sem=pltpu.SemaphoreType.DMA((SENDS,)),
        local_sem=pltpu.SemaphoreType.DMA((LOCALS,)),
    )


def step_kernel(
    hid_hbm,
    q_hbm,
    g_hbm,
    wk_hbm,
    wv_hbm,
    lg_ref,
    segr_ref,
    gain_ref,
    qg_ref,
    ig_ref,
    gate_ref,
    kout_ref,
    vout_ref,
    sout_ref,
    *refs,
):
    s = dict(zip(scratch(), refs))
    x, y, z, c = (lax.axis_index(a) for a in ("x", "batch", "z", "core"))
    used = [0]

    def remote(src, dst, target):
        n = used[0]
        used[0] += 1
        cp = pltpu.make_async_remote_copy(
            src_ref=src,
            dst_ref=dst,
            send_sem=s["send_sem"].at[n],
            recv_sem=s["recv_sem"].at[n],
            device_id=target,
            device_id_type=MESH,
        )
        cp.start()
        return cp

    def wait(copies):
        for cp in copies:
            cp.wait()

    sib = {"core": 1 - c}
    offsets = [(d, e) for d in range(4) for e in (0, 1) if d or e]

    def plane(axis, index, d, e):
        to, tc = ring(index, d), lax.rem(c + e, 2)
        return {axis: to, "core": tc}, 2 * to + tc

    peers = [plane("batch", y, d, e)[0] for d, e in offsets]
    peers += [plane("z", z, d, e)[0] for d, e in offsets if d]
    peers += [{"x": ring(x, d)} for d in (1, 2, 3)]
    barrier = entry_signal(peers)

    local_sem = s["local_sem"]
    first_loads = [
        pltpu.make_async_copy(hid_hbm, s["hid"], local_sem.at[0]),
        pltpu.make_async_copy(q_hbm, s["q"], local_sem.at[1]),
        pltpu.make_async_copy(g_hbm, s["g"], local_sem.at[2]),
    ]

    def weight_load(hbm, name, i, base):
        cols = rows_of(i * 256, 256)
        return pltpu.make_async_copy(hbm.at[:, cols], s[name].at[:, cols], local_sem.at[base + i])

    first_loads[0].start()
    for i in range(8):
        weight_load(wk_hbm, "wk", i, 8).start()
        weight_load(wv_hbm, "wv", i, 16).start()
        if i == 0:
            first_loads[1].start()
            first_loads[2].start()

    rows_i, cols_i = iota((TOK, TOK), 0), iota((TOK, TOK), 1)
    causal = cols_i <= rows_i
    lower = causal.astype(F32)
    low = cols_i < 64
    low_half = iota((64, PAIR), 1) < 64
    row8 = iota((8, PAIR), 0)
    low_row = iota((1, PAIR), 1) < 64
    log_gate = lg_ref[...]
    cum_cols = dot_exact(lower, log_gate, NT)
    s["cumr"][...] = dot_exact(log_gate, lower, NT)
    for pair in range(16):
        s["cumx"][pair] = jnp.where(
            low, cum_cols[:, 2 * pair : 2 * pair + 1], cum_cols[:, 2 * pair + 1 : 2 * pair + 2]
        )
        s["cumr3"][pair, 0:2, :] = s["cumr"][2 * pair : 2 * pair + 2, :]
    seg_row = segr_ref[...].astype(F32)
    s["segc"][...] = jnp.broadcast_to(seg_row, (TOK, TOK)).T
    s["gcross"][...] = jnp.zeros((16, 8, PAIR), F32)

    first_loads[0].wait()
    for b in range(8):
        cols = slice(b * TOK, (b + 1) * TOK)
        s["hid_t"][cols, :] = s["hid"][:, cols].astype(F32).T
    pl.semaphore_wait(barrier, len(peers))
    gathers = (("batch", y, s["hy"]), ("z", z, s["hz"]))
    hops = []
    for axis, index, buf in gathers:
        for d in (1, 3):
            hops.append(remote(s["hid_t"], buf.at[index, c], {axis: ring(index, d)}))
    down = [remote(s["hid_t"], buf.at[index, c], sib) for _, index, buf in gathers]

    first_loads[1].wait()
    first_loads[2].wait()

    def project(step, carry):
        weight_load(wk_hbm, "wk", step, 8).wait()
        weight_load(wv_hbm, "wv", step, 16).wait()
        wide = rows_of(step * 256, 256)
        hid = s["hid"][...]
        keys = dot(hid, s["wk"][:, wide], NN).astype(BF16)
        values = dot(hid, s["wv"][:, wide], NN).astype(BF16)
        segc = s["segc"][...]
        half = step // 4
        for p in range(2):
            pair = 2 * step + p
            k, v = keys[:, p * PAIR : (p + 1) * PAIR], values[:, p * PAIR : (p + 1) * PAIR]
            s["k"][pair] = k
            s["v"][pair] = v
            cum = s["cumx"][pair]
            total = cum[TOK - 1 : TOK, :]
            last_w = jnp.where(segc == segc[TOK - 1 : TOK, :], jnp.exp(total - cum), 0.0)
            first_w = jnp.where(segc == segc[0:1, :], jnp.exp(cum), 0.0)
            s["lw"][pair] = last_w
            s["fw"][pair] = first_w
            cols = rows_of(pair * PAIR, PAIR)
            fwd = dot_left(k.astype(F32) * last_w, v, TN)
            rev = dot_left(s["q"][:, cols].astype(F32) * first_w, s["g"][:, cols], TN)
            pp = 2 * lax.rem(step, 4) + p
            s["st"][half, rows_of(pp * 64, 64), :] = jnp.where(low_half, fwd[:64], fwd[64:])
            s["st"][half, rows_of(512 + pp * 64, 64), :] = jnp.where(low_half, rev[:64], rev[64:])
            meta = jnp.where(
                row8 == 0,
                total,
                jnp.where(
                    row8 == 1, segc[0:1, :], jnp.where(row8 == 2, segc[TOK - 1 : TOK, :], 0.0)
                ),
            )
            s["st"][half, rows_of(1024 + pp * 8, 8), :] = meta
        return carry

    lax.fori_loop(0, 8, project, 0)

    def inner(pair, carry):
        cols = rows_of(pair * PAIR, PAIR)
        q, g = s["q"][:, cols], s["g"][:, cols]
        k, v = s["k"][pair], s["v"][pair]
        allowed = causal & (s["segc"][...] == seg_row)
        gap = jnp.bitwise_xor(rows_i, cols_i)
        strict = (rows_i < cols_i).astype(BF16)
        zero = jnp.zeros((TOK, PAIR), BF16)
        weighted, scored, queries, keys, grads, gate_rows, gain_rows = [], [], [], [], [], [], []
        for h in range(2):

            def own(a):
                return jnp.where(low, a, zero) if h == 0 else jnp.where(low, zero, a)

            qh, gh, kh = own(q), own(g), own(k)
            score = dot(qh, k, NT)
            dprob = dot(gh, v, NT)
            spread = s["cumx"][pair, :, 64 * h : 64 * h + 1] - s["cumr3"][pair, h : h + 1, :]
            decay = jnp.where(allowed, jnp.exp(jnp.where(allowed, spread, 0.0)), 0.0)
            ds = decay * score
            joint = ds * dprob
            head = 2 * pair + h
            level = jnp.full((TOK, TOK), gain_ref[head, 0], F32)
            gain_rows.append(jnp.sum(jnp.where(gap == 0, joint, 0.0), axis=0, keepdims=True))
            for l in range(1, 8):
                above = gap >= 2 ** (l - 1)
                level = jnp.where(above, gain_ref[head, l], level)
                chosen = above & (gap < 2**l)
                gain_rows.append(jnp.sum(jnp.where(chosen, joint, 0.0), axis=0, keepdims=True))
            wd = level * decay * dprob
            weighted.append(wd.astype(BF16))
            scored.append((level * ds).astype(BF16))
            grid = (wd * score).astype(BF16)
            crossing = jnp.where(causal, dot(grid, strict, NN), 0.0)
            gate_rows.append(jnp.sum(crossing, axis=0, keepdims=True))
            queries.append(qh)
            keys.append(kh)
            grads.append(gh)
        s["qacc"][pair] = dot(
            jnp.concatenate(weighted, axis=1), jnp.concatenate(keys, axis=0), NN
        )
        s["kacc"][pair] = dot(
            jnp.concatenate(weighted, axis=0), jnp.concatenate(queries, axis=0), TN
        )
        s["vacc"][pair] = dot(jnp.concatenate(scored, axis=0), jnp.concatenate(grads, axis=0), TN)
        s["gate"][pair] = jnp.concatenate([*gate_rows, jnp.zeros((6, TOK), F32)], axis=0)
        s["gint"][pair] = jnp.concatenate(gain_rows, axis=0)
        return carry

    both, st = s["both"], s["st"]
    swap = remote(st.at[1 - c], both.at[c], sib)
    both[pl.ds(c, 1)] = st[pl.ds(c, 1)]
    lax.fori_loop(0, 2, inner, 0)
    swap.wait()

    def meta_rows(total, first, last):
        return jnp.where(
            row8 == 0, total, jnp.where(row8 == 1, first, jnp.where(row8 == 2, last, 0.0))
        )

    chip_send, chip_recv = s["chip_send"], s["chip_recv"]
    for pp in range(8):
        f0 = both[0, pp * 64 : pp * 64 + 64, :]
        f1 = both[1, pp * 64 : pp * 64 + 64, :]
        r0 = both[0, 512 + pp * 64 : 576 + pp * 64, :]
        r1 = both[1, 512 + pp * 64 : 576 + pp * 64, :]
        m0 = both[0, 1024 + pp * 8 : 1032 + pp * 8, :]
        m1 = both[1, 1024 + pp * 8 : 1032 + pp * 8, :]
        t0, first0, last0 = m0[0:1], m0[1:2], m0[2:3]
        t1, first1, last1 = m1[0:1], m1[1:2], m1[2:3]
        n, p = pp // 2, pp % 2
        chip_send[n, p * 64 : p * 64 + 64, :] = f1 + linked(last0, last1, t1) * f0
        chip_send[n, 128 + p * 64 : 192 + p * 64, :] = r0 + linked(first0, first1, t0) * r1
        chip_send[n, 256 + p * 8 : 264 + p * 8, :] = meta_rows(t0 + t1, first0, last1)
        d8 = same(last0, first1) * jnp.sum(f0 * r1, axis=0, keepdims=True)
        s["gcross"][pl.ds(c * 8 + pp, 1)] = jnp.where(row8 == 0, d8, 0.0)[None]

    xs = []
    for d in (1, 2, 3):
        to = ring(x, d)
        xs.append(remote(chip_send.at[to], chip_recv.at[x], {"x": to}))
    chip_recv[pl.ds(x, 1)] = chip_send[pl.ds(x, 1)]

    def forward(n):
        axis, index, buf = gathers[n]
        out = []
        for m, d in enumerate((1, 3)):
            hops[2 * n + m].wait()
            came = ring(index, 4 - d)
            part = slice(0, 512) if d == 1 else slice(512, 1024)
            out.append(
                remote(buf.at[came, c, part], buf.at[came, c, part], {axis: ring(index, d)})
            )
            down.append(remote(buf.at[came, c], buf.at[came, c], sib))
        return out

    fwd_y = forward(0)
    lax.fori_loop(2, 8, inner, 0)
    wait(xs)

    def chip(j, p):
        return (
            chip_recv[j, p * 64 : p * 64 + 64, :],
            chip_recv[j, 128 + p * 64 : 192 + p * 64, :],
            chip_recv[j, 256 + p * 8 : 257 + p * 8, :],
            chip_recv[j, 257 + p * 8 : 258 + p * 8, :],
            chip_recv[j, 258 + p * 8 : 259 + p * 8, :],
        )

    def joined(p):
        (f0, r0, t0, a0, l0), (f1, r1, t1, a1, l1), (f2, r2, t2, a2, l2), (f3, r3, t3, a3, l3) = (
            chip(j, p) for j in range(4)
        )
        f01 = f1 + linked(l0, l1, t1) * f0
        r01 = r0 + linked(a0, a1, t0) * r1
        f23 = f3 + linked(l2, l3, t3) * f2
        r23 = r2 + linked(a2, a3, t2) * r3
        return f01, r01, f23, r23

    tot_send, tot_recv = s["tot_send"], s["tot_recv"]
    for p in range(2):
        f01, r01, f23, r23 = joined(p)
        t0, a0 = chip(0, p)[2:4]
        t1, l1 = chip(1, p)[2], chip(1, p)[4]
        t2, a2 = chip(2, p)[2:4]
        t3, l3 = chip(3, p)[2], chip(3, p)[4]
        tot_send[0, p * 64 : p * 64 + 64, :] = f23 + linked(l1, l3, t2 + t3) * f01
        tot_send[1, p * 64 : p * 64 + 64, :] = r01 + linked(a0, a2, t0 + t1) * r23
        tot_send[0, 128 + p * 8 : 136 + p * 8, :] = jnp.broadcast_to(l3, (8, PAIR))
        tot_send[1, 128 + p * 8 : 136 + p * 8, :] = jnp.broadcast_to(a0, (8, PAIR))
    zs = [
        remote(tot_send.at[n], tot_recv.at[n], {"z": ring(z, d)}) for n, d in ((0, 1), (1, 3))
    ]
    fwd_z = forward(1)
    lax.fori_loop(8, 10, inner, 0)
    wait(zs)

    has_prev = (z > 0).astype(F32)
    has_next = (z < 3).astype(F32)
    prev_top = (z == 2).astype(F32)
    next_top = (z == 1).astype(F32)
    back_send, back_recv = s["back_send"], s["back_recv"]

    def gain_row(pair, level):
        return jnp.where(low_row, gain_ref[2 * pair, level], gain_ref[2 * pair + 1, level])

    for p in range(2):
        (f0, r0, t0, a0, l0), (f1, r1, t1, a1, l1), (f2, r2, t2, a2, l2), (f3, r3, t3, a3, l3) = (
            chip(j, p) for j in range(4)
        )
        f01, r01, f23, r23 = joined(p)
        pair = c * 8 + 2 * x + p
        g9, g10, g11, g12 = (gain_row(pair, level) for level in range(9, 13))
        zf = has_prev * tot_recv[0, p * 64 : p * 64 + 64, :]
        zl = tot_recv[0, 128 + p * 8 : 129 + p * 8, :]
        zr = has_next * tot_recv[1, p * 64 : p * 64 + 64, :]
        za = tot_recv[1, 128 + p * 8 : 129 + p * 8, :]
        gzf = g11 * (1.0 - prev_top) + g12 * prev_top
        gzr = g11 * (1.0 - next_top) + g12 * next_top
        sf = (
            gzf * same(zl, a0) * zf,
            gzf * linked(zl, a1, t0) * zf + g9 * same(l0, a1) * f0,
            gzf * linked(zl, a2, t0 + t1) * zf + g10 * same(l1, a2) * f01,
            gzf * linked(zl, a3, t0 + t1 + t2) * zf
            + g10 * linked(l1, a3, t2) * f01
            + g9 * same(l2, a3) * f2,
        )
        sr = (
            gzr * linked(za, l0, t1 + t2 + t3) * zr
            + g10 * linked(l0, a2, t1) * r23
            + g9 * same(l0, a1) * r1,
            gzr * linked(za, l1, t2 + t3) * zr + g10 * same(l1, a2) * r23,
            gzr * linked(za, l2, t3) * zr + g9 * same(l2, a3) * r3,
            gzr * same(za, l3) * zr,
        )
        for j in range(4):
            back_send[j, p * 64 : p * 64 + 64, :] = sf[j]
            back_send[j, 128 + p * 64 : 192 + p * 64, :] = sr[j]
    bs = []
    for d in (1, 2, 3):
        to = ring(x, d)
        bs.append(remote(back_send.at[to], back_recv.at[x], {"x": to}))
    back_recv[pl.ds(x, 1)] = back_send[pl.ds(x, 1)]

    for p in range(2):
        (f0, r0, t0, a0, l0), (f1, r1, t1, a1, l1), (f2, r2, t2, a2, l2), (f3, r3, t3, a3, l3) = (
            chip(j, p) for j in range(4)
        )
        f01, r01, f23, r23 = joined(p)
        zf = has_prev * tot_recv[0, p * 64 : p * 64 + 64, :]
        zl = tot_recv[0, 128 + p * 8 : 129 + p * 8, :]
        r_group = r01 + linked(a0, a2, t0 + t1) * r23
        d9 = same(l0, a1) * jnp.sum(f0 * r1, axis=0, keepdims=True) + same(l2, a3) * jnp.sum(
            f2 * r3, axis=0, keepdims=True
        )
        d10 = same(l1, a2) * jnp.sum(f01 * r23, axis=0, keepdims=True)
        dz = same(zl, a0) * jnp.sum(zf * r_group, axis=0, keepdims=True)
        rows = jnp.where(
            row8 == 1,
            d9,
            jnp.where(
                row8 == 2,
                d10,
                jnp.where(
                    row8 == 3, (1.0 - prev_top) * dz, jnp.where(row8 == 4, prev_top * dz, 0.0)
                ),
            ),
        )
        pair = c * 8 + 2 * x + p
        s["gcross"][pl.ds(pair, 1)] = s["gcross"][pl.ds(pair, 1)] + rows[None]
    lax.fori_loop(10, 16, inner, 0)
    wait(bs)

    own_blocks, s_in = s["own_blocks"], s["s_in"]
    for pp in range(8):
        n, p = pp // 2, pp % 2
        f0 = both[0, pp * 64 : pp * 64 + 64, :]
        r1 = both[1, 512 + pp * 64 : 576 + pp * 64, :]
        m0 = both[0, 1024 + pp * 8 : 1032 + pp * 8, :]
        m1 = both[1, 1024 + pp * 8 : 1032 + pp * 8, :]
        t0, first0, last0 = m0[0:1], m0[1:2], m0[2:3]
        t1, first1, last1 = m1[0:1], m1[1:2], m1[2:3]
        sf = back_recv[n, p * 64 : p * 64 + 64, :]
        sr = back_recv[n, 128 + p * 64 : 192 + p * 64, :]
        link = gain_row(c * 8 + pp, 8) * same(last0, first1)
        own_blocks[0, pp * 64 : pp * 64 + 64, :] = sf
        own_blocks[1, pp * 64 : pp * 64 + 64, :] = linked(first0, first1, t0) * sf + link * f0
        own_blocks[0, 512 + pp * 64 : 576 + pp * 64, :] = linked(last0, last1, t1) * sr + link * r1
        own_blocks[1, 512 + pp * 64 : 576 + pp * 64, :] = sr
    swap = remote(own_blocks.at[1 - c], s_in.at[c], sib)
    s_in[pl.ds(c, 1)] = own_blocks[pl.ds(c, 1)]

    for (_, index, buf), copies in zip(gathers, (fwd_y, fwd_z)):
        buf[pl.ds(index, 1), pl.ds(c, 1)] = s["hid_t"][...][None, None]
        wait(copies)
        came = ring(index, 2)
        down.append(remote(buf.at[came, c], buf.at[came, c], sib))
    swap.wait()

    tail = causal.astype(BF16)
    head_pick = (cols_i[0:8, :] // 64 == row8).astype(BF16)

    def cross(pair, carry):
        half, pp = pair // 8, lax.rem(pair, 8)
        cols = rows_of(pair * PAIR, PAIR)
        q, g = s["q"][:, cols], s["g"][:, cols]
        k, v = s["k"][pair], s["v"][pair]
        first_w, last_w = s["fw"][pair], s["lw"][pair]
        sf = s_in[half, rows_of(pp * 64, 64), :]
        sr = s_in[half, rows_of(512 + pp * 64, 64), :]

        def diag(a):
            return jnp.concatenate([jnp.where(low_half, a, 0.0), jnp.where(low_half, 0.0, a)], axis=0)

        sg = first_w * dot_right(g, diag(sf), NT)
        rv = last_w * dot_right(v, diag(sr), NT)
        rk = last_w * dot_right(k, diag(sr), NN)
        diff = q.astype(F32) * sg - k.astype(F32) * rv
        hi, lo = split2(diff)
        diff_rows = dot(head_pick, hi, NT) + dot(head_pick, lo, NT)
        s["gate"][pair] = s["gate"][pair] + dot_left(diff_rows, tail, NN)
        qg_ref[:, cols] = (s["qacc"][pair] + sg).astype(BF16)
        key_sum = (s["kacc"][pair] + rv).astype(BF16)
        value_sum = (s["vacc"][pair] + rk).astype(BF16)
        s["ksb"][:, cols] = key_sum
        s["vsb"][:, cols] = value_sum
        s["ks"][half, pp] = key_sum.astype(F32)
        s["vs"][half, pp] = value_sum.astype(F32)
        return carry

    firsts = []
    me_y, me_z = 2 * y + c, 2 * z + c
    for n in range(2):
        lax.fori_loop(8 * n, 8 * n + 8, cross, 0)
        fk, fv = [], []
        for d, e in offsets:
            dev, to = plane("batch", y, d, e)
            fk.append(remote(s["ks"].at[n, to], s["rk"].at[n, me_y], dev))
            dev, to = plane("z", z, d, e)
            fv.append(remote(s["vs"].at[n, to], s["rv"].at[n, me_z], dev))
        s["rk"][n, pl.ds(me_y, 1)] = s["ks"][n, pl.ds(me_y, 1)]
        s["rv"][n, pl.ds(me_z, 1)] = s["vs"][n, pl.ds(me_z, 1)]
        firsts.append((fk, fv))

    ones = jnp.ones((8, PAIR), F32)
    inner_sum = dot_exact(ones, s["gint"][...].reshape(256, PAIR), NT)
    pick = (cols_i[0:8, :] // 64 == row8 - 2).astype(F32)
    outer_sum = dot_exact(pick, s["gcross"][...].reshape(128, PAIR), NT)
    start = (cols_i[0:8, :] == 0).astype(F32)
    own_total = dot_exact(start, s["gate"][...].reshape(128, TOK), NT)
    small, m1, m1s, m2, m2s, m3 = (s[n] for n in ("small", "m1", "m1s", "m2", "m2s", "m3"))
    small[0:8, :] = jnp.where(
        row8 == 0, inner_sum[:, :128], jnp.where(row8 == 1, inner_sum[:, 128:], outer_sum)
    )
    small[8:16, :] = own_total
    smalls = []
    for d, e in offsets:
        smalls.append(remote(small, m1.at[me_z], plane("z", z, d, e)[0]))
    m1[pl.ds(me_z, 1)] = small[...][None]

    wait(down)
    for name, out in (("hy", "hyb"), ("hz", "hzb")):
        for g in range(8):
            s[out][:, g * TOK : (g + 1) * TOK] = s[name][g // 2, g % 2].astype(BF16)

    def product(left, right, n):
        right = s[right][n].reshape(8 * TOK, PAIR).astype(BF16)
        for b in range(4):
            yield b, dot(s[left][b * 256 : (b + 1) * 256, :], right, NN)

    part1, recv1, part2, recv2 = s["part1"], s["recv1"], s["part2"], s["recv2"]

    def scatter(part, recv, chunk, axis, index):
        out = []
        for d in (1, 2, 3):
            to = ring(index, d)
            out.append(remote(part.at[chunk, to], recv.at[chunk, index], {axis: to}))
        recv[chunk, pl.ds(index, 1)] = part[chunk, pl.ds(index, 1)]
        return out

    wait(firsts[0][0])
    for b, block in product("hyb", "rk", 0):
        for j in range(4):
            part1[0, j, b * 64 : b * 64 + 64, :] = block[j * 64 : j * 64 + 64, :]
    k0 = scatter(part1, recv1, 0, "x", x)
    wait(firsts[0][1])
    for b, block in product("hzb", "rv", 0):
        for j in range(4):
            part1[2, j, b * 64 : b * 64 + 64, :] = block[j * 64 : j * 64 + 64, :]
    v0 = scatter(part1, recv1, 2, "x", x)

    def input_grad(n, carry):
        rows = rows_of(n * 256, 256)
        ig_ref[:, rows] = (
            dot(s["ksb"][...], s["wk"][rows, :], NT) + dot(s["vsb"][...], s["wv"][rows, :], NT)
        ).astype(BF16)
        return carry

    lax.fori_loop(0, 2, input_grad, 0)

    wait(firsts[1][0])
    for b, block in product("hyb", "rk", 1):
        part1[1, b] = block
    k1 = scatter(part1, recv1, 1, "z", z)
    wait(firsts[1][1])
    for b, block in product("hzb", "rv", 1):
        for j in range(8):
            for i in range(4):
                at = j * 32 + i * 8
                part1[3, i, b * 64 + j * 8 : b * 64 + j * 8 + 8, :] = block[at : at + 8, :]
    v1 = scatter(part1, recv1, 3, "batch", y)
    lax.fori_loop(2, 4, input_grad, 0)

    wait(smalls)
    total = m1[0, 0:8, :]
    for g in range(1, 8):
        total = total + m1[g, 0:8, :]
    m1s[0:8, :] = total
    for g in range(8):
        m1s[8 + g : 9 + g, :] = m1[g, 8:9, :]
    smalls = [remote(m1s, m2.at[x], {"x": ring(x, d)}) for d in (1, 2, 3)]
    m2[pl.ds(x, 1)] = m1s[...][None]

    def summed(recv, chunk):
        return recv[chunk, 0] + recv[chunk, 1] + recv[chunk, 2] + recv[chunk, 3]

    wait(k0)
    total = summed(recv1, 0)
    for j in range(4):
        part2[0, j] = total[j * 64 : j * 64 + 64, :]
    k0 = scatter(part2, recv2, 0, "z", z)
    wait(v0)
    total = summed(recv1, 2)
    for j in range(8):
        for i in range(4):
            at = j * 32 + i * 8
            part2[2, i, j * 8 : j * 8 + 8, :] = total[at : at + 8, :]
    v0 = scatter(part2, recv2, 2, "batch", y)
    wait(k1)
    total = summed(recv1, 1)
    for j in range(4):
        part2[1, j] = total[j * 64 : j * 64 + 64, :]
    k1 = scatter(part2, recv2, 1, "x", x)
    wait(v1)
    total = summed(recv1, 3)
    for j in range(4):
        for i in range(4):
            at = j * 64 + i * 16
            part2[3, i, j * 16 : j * 16 + 16, :] = total[at : at + 16, :]
    v1 = scatter(part2, recv2, 3, "x", x)

    wait(smalls)
    total = m2[0, 0:8, :] + m2[1, 0:8, :] + m2[2, 0:8, :] + m2[3, 0:8, :]
    m2s[...] = total
    smalls = [remote(m2s, m3.at[y], {"batch": ring(y, d)}) for d in (1, 2, 3)]
    m3[pl.ds(y, 1)] = total[None]
    place = z * 8 + x * 2 + c
    later = jnp.zeros((1, PAIR), F32)
    for j in range(4):
        for g in range(8):
            spot = (g // 2) * 8 + j * 2 + g % 2
            later = later + (place < spot).astype(F32) * m2[j, 8 + g : 9 + g, :]
    sout_ref[8:16, :] = jnp.broadcast_to(later, (8, PAIR))
    gate_ref[...] = s["gate"][...]

    fins = []
    wait(k0)
    wait(k1)
    for n in range(2):
        total = summed(recv2, n)
        for i in range(4):
            for j in range(2):
                at = j * 32 + i * 8
                s["kown"][2 * i + j, n] = total[at : at + 8, :]
    for d, e in offsets:
        dev, to = plane("batch", y, d, e)
        fins.append(remote(s["kown"].at[to], s["kfin"].at[me_y], dev))
    s["kfin"][pl.ds(me_y, 1)] = s["kown"][pl.ds(me_y, 1)]
    wait(v0)
    wait(v1)
    for n in range(2):
        total = summed(recv2, 2 + n)
        for j in range(8):
            s["vown"][j, n] = total[j * 8 : j * 8 + 8, :]
    for d, e in offsets:
        dev, to = plane("z", z, d, e)
        fins.append(remote(s["vown"].at[to], s["vfin"].at[me_z], dev))
    s["vfin"][pl.ds(me_z, 1)] = s["vown"][pl.ds(me_z, 1)]
    wait(smalls)
    sout_ref[0:8, :] = m3[0] + m3[1] + m3[2] + m3[3]
    wait(fins)
    for n in range(2):
        for g in range(8):
            cols = slice(n * 1024 + g * PAIR, n * 1024 + (g + 1) * PAIR)
            kout_ref[:, cols] = s["kfin"][g, n]
            vout_ref[:, cols] = s["vfin"][g, n]


def whole_step(hidden, queries, out_grad, w_key, w_value, log_gate, seg_row, level_gain):
    vm = pl.BlockSpec(memory_space=pltpu.VMEM)
    far = pl.BlockSpec(memory_space=pl.ANY)
    return pl.pallas_call(
        step_kernel,
        in_specs=[far] * 5 + [vm, vm, pl.BlockSpec(memory_space=pltpu.SMEM)],
        out_specs=[vm] * 6,
        out_shape=[
            jax.ShapeDtypeStruct((TOK, 2048), BF16),
            jax.ShapeDtypeStruct((TOK, 1024), BF16),
            jax.ShapeDtypeStruct((16, 8, TOK), F32),
            jax.ShapeDtypeStruct((8, 2048), F32),
            jax.ShapeDtypeStruct((8, 2048), F32),
            jax.ShapeDtypeStruct((16, PAIR), F32),
        ],
        scratch_shapes=list(scratch().values()),
        compiler_params=pltpu.CompilerParams(
            collective_id=0, has_side_effects=True, vmem_limit_bytes=63 * 2**20
        ),
        name="whole_step",
    )(hidden, queries, out_grad, w_key, w_value, log_gate, seg_row, level_gain)


def local(hidden, queries, w_key, w_value, log_gate, level_gain, segment_ids, out_grad):
    heads, levels = level_gain.shape
    query_grad, input_grad, gate, key_weight, value_weight, summed = whole_step(
        hidden[0], queries[0], out_grad[0], w_key, w_value, log_gate[0], segment_ids, level_gain
    )
    inner = summed[:2].reshape(heads, 8)
    outer = summed[2:4].reshape(2, heads // 2, 8).transpose(1, 0, 2).reshape(heads, 8)
    gain_total = jnp.concatenate([inner, outer, jnp.zeros((heads, levels - 16), F32)], axis=1)
    gate_grad = (gate + summed[8].reshape(16, 8)[:, :, None])[:, :2].reshape(heads, TOK)
    return (
        query_grad[None],
        input_grad[None],
        gate_grad[None],
        key_weight,
        value_weight,
        gain_total,
    )


def solution(mesh):
    split = Mesh(
        mesh.devices.reshape(4, 4, 2, mesh.shape["batch"]), ("z", "x", "core", "batch")
    )
    return jax.shard_map(
        local,
        mesh=split,
        in_specs=(
            P("batch", SEQ, None),
            P("batch", SEQ, None),
            P(),
            P(),
            P("batch", None, SEQ),
            P(),
            P("batch", SEQ),
            P("batch", SEQ, None),
        ),
        out_specs=(
            P("batch", SEQ, None),
            P("batch", SEQ, None),
            P("batch", None, SEQ),
            P(SEQ_BATCH, None),
            P(SEQ_BATCH, None),
            P(),
        ),
        check_vma=False,
    )
```

time: 527 us -> 92.8 us (0.18); the launches traced: 518 us -> 91.3 us
  waiting for transfers between devices: 202 us -> 0 us
  Pallas kernels: 0 us -> 78.7 us
  other arithmetic: 68.1 us -> 1.62 us
  matrix products: 61.2 us -> 0 us
  blocking collectives: 52.4 us -> 0 us
  starting transfers between devices: 44.9 us -> 0 us
  local copies, waits for them, and re-layouts: 53.5 us -> 10.3 us
  between operations: 28.6 us -> 0.66 us
  loops' own time: 6.79 us -> 0 us
    ppermute x24 -> x0, waiting for transfers between devices: 155 us -> none  [partner(): return lax.ppermute(value, axis, pairs)]
    pallas_call x0 -> x1, Pallas kernels: none -> 78.7 us  [whole_step(): pl.pallas_call(step_kernel, in_specs=[far] * 5 + [vm, vm, pl.BlockSpec(me...]
    dot_general x42 -> x0, matrix products: 61.2 us -> none  [the longest x4 9.71 us: pair_terms(): jnp.einsum('hts,thp->shp', coeffs * scores, grad_g.astype(jnp.float32), p...]
    psum x4 -> x0, blocking collectives: 52.4 us -> none  [over_axes(): x = lax.psum(x, axis)]
    reduce_scatter x1 -> x0, waiting for transfers between devices: 39.4 us -> none  [local(): lax.psum_scatter(lax.dot_general(hidden_rows, both_grads, (((0,), (0,)),...]
    ppermute x24 -> x0, starting transfers between devices: 36.5 us -> none  [partner(): return lax.ppermute(value, axis, pairs)]
    another operation x52 -> x0, other arithmetic: 33.2 us -> none
    unnamed x129 -> x6, local copies, waits for them, and re-layouts: 23.2 us -> 8.57 us
  transfers between devices with their start and end apart: 27 -> 0, of which waited for: 15 -> 0; matrix products, arithmetic and copies ran while one was open for 25% -> 0% of each run, Pallas kernels for 0% -> 0%
where the time goes in v2:
time: 92.8 us; the launch traced here: 91.3 us
  Pallas kernels  78.7 us (85%)
  local copies, waits for them, and re-layouts  10.3 us (11%)
  other arithmetic  1.62 us (2%)
    pallas_call x1, Pallas kernels, whole_step(): pl.pallas_call(step_kernel, in_specs=[far] * 5 + [vm, vm, pl.BlockSpec(me...  78.7 us
    unnamed x6, local copies, waits for them, and re-layouts  8.57 us

profile of v2, /device:TPU:0, one launch (start us, length us, event | category | flops | bytes accessed | tf_op | source)
XLA Modules:
  0.0 91.3 jit_solution(6399851892147008249)
XLA Ops:
  0.6 1.4 %copy.17.gain_ref = f32[32,18]{1,0:T(8,128)} copy(f32[32,18]{0,1:T(8,128)} %param.13) | data formatting | bytes 4608 | tf_op args[5]
  2.0 78.7 %whole_step.1 = (bf16[128,2048]{1,0:T(8,128)(2,1)}, bf16[128,1024]{1,0:T(8,128)(2,1)}, f32[16,8,128]{2,1,0:T(8,128)}, f32[8,2048]{1,0:T(8,128)}, f32[8,2048]{1,0:T(8,128)}, /*index=5*/f32[16,128]{1,0:T(8,128)}) custom-call(bf16[128,1024]{1,0:T(8,128)(2,1)} %bitcast.13, bf16[128,2048]{1,0:T(8,128)(2,1)} %bitcast.10, bf16[128,2048]{1,0:T(8,128)(2,1)} %bitcast.11, ...), custom_call_target="tpu_custom_call" | custom-call | tf_op jit(solution)/shard_map/whole_step/pallas_call | solution.py:733
  80.7 0.8 fusion
  81.5 0.1 reshape.23
  81.6 0.1 reshape.22
  81.7 0.1 pad.2.clone
  81.8 0.1 maximum_maximum_fusion
  81.8 0.7 copy.19
  82.5 0.7 slice_reduce_fusion
  83.2 0.1 add.10
  83.3 1.5 %slice_add_fusion = f32[16,2,128]{2,1,0:T(2,128)} fusion(f32[16,8,128]{2,1,0:T(8,128)} %get-tuple-element.14, f32[16,2]{1,0:T(8,128)S(1)} %bitcast.17), kind=kLoop, calls=%fused_computation | loop fusion | flops 4096 | bytes 32896 | tf_op jit(solution)/shard_map/add | solution.py:761
  84.8 1.9 %copy.24 = bf16[1,128,2048]{2,1,0:T(8,128)(2,1)} copy(bf16[1,128,2048]{2,1,0:T(8,128)(2,1)} %bitcast.12) | data formatting | bytes 1048576
  86.7 1.7 %copy.25 = bf16[1,128,1024]{2,1,0:T(8,128)(2,1)} copy(bf16[1,128,1024]{2,1,0:T(8,128)(2,1)} %bitcast.14) | data formatting | bytes 524288
  88.4 1.5 %copy.26 = f32[8,2048]{1,0:T(8,128)} copy(f32[8,2048]{1,0:T(8,128)} %get-tuple-element.35) | data formatting | bytes 131072
  89.9 1.5 %copy.27 = f32[8,2048]{1,0:T(8,128)} copy(f32[8,2048]{1,0:T(8,128)} %get-tuple-element.36) | data formatting | bytes 131072
  (2 shorter events, 0.0 us)

commit v3 on v2

--- a/solution.py
+++ b/solution.py
@@ -77,6 +77,7 @@
 
 SENDS = 128
 LOCALS = 24
+VMEM_LIMIT = 56 * 2**20
 
 
 def scratch():
@@ -311,11 +312,11 @@
             ds = decay * score
             joint = ds * dprob
             head = 2 * pair + h
-            level = jnp.full((TOK, TOK), gain_ref[head, 0], F32)
+            level = jnp.full((TOK, TOK), gain_ref[0, head], F32)
             gain_rows.append(jnp.sum(jnp.where(gap == 0, joint, 0.0), axis=0, keepdims=True))
             for l in range(1, 8):
                 above = gap >= 2 ** (l - 1)
-                level = jnp.where(above, gain_ref[head, l], level)
+                level = jnp.where(above, gain_ref[l, head], level)
                 chosen = above & (gap < 2**l)
                 gain_rows.append(jnp.sum(jnp.where(chosen, joint, 0.0), axis=0, keepdims=True))
             wd = level * decay * dprob
@@ -433,7 +434,7 @@
     back_send, back_recv = s["back_send"], s["back_recv"]
 
     def gain_row(pair, level):
-        return jnp.where(low_row, gain_ref[2 * pair, level], gain_ref[2 * pair + 1, level])
+        return jnp.where(low_row, gain_ref[level, 2 * pair], gain_ref[level, 2 * pair + 1])
 
     for p in range(2):
         (f0, r0, t0, a0, l0), (f1, r1, t1, a1, l1), (f2, r2, t2, a2, l2), (f3, r3, t3, a3, l3) = (
@@ -744,28 +745,70 @@
         ],
         scratch_shapes=list(scratch().values()),
         compiler_params=pltpu.CompilerParams(
-            collective_id=0, has_side_effects=True, vmem_limit_bytes=63 * 2**20
+            collective_id=0, has_side_effects=True, vmem_limit_bytes=VMEM_LIMIT
         ),
         name="whole_step",
     )(hidden, queries, out_grad, w_key, w_value, log_gate, seg_row, level_gain)
 
 
+def finish_kernel(
+    qg_ref, ig_ref, gate_ref, kw_ref, vw_ref, small_ref, qg, ig, gate, kw, vw, gains
+):
+    qg[...] = qg_ref[...]
+    ig[...] = ig_ref[...]
+    kw[...] = kw_ref[...]
+    vw[...] = vw_ref[...]
+    heads = gate.shape[0]
+    lane = iota((heads, PAIR), 1)
+    head = iota((heads, PAIR), 0)
+    small = small_ref[...]
+    later = jnp.broadcast_to(small[8:9, :], (TOK, TOK)).T
+    rows = gate_ref[...].reshape(TOK, TOK) + later
+    gate[...] = dot_exact((lane == (head // 2) * 8 + head % 2).astype(F32), rows, NN)
+    levels = gains.shape[0]
+    level, at = iota((levels, PAIR), 0), iota((levels, PAIR), 1) % 8
+    first = (level == at).astype(F32)
+    second = (level == at + 8).astype(F32)
+    pick0 = jnp.where(lane // 8 == head, small[0:1, :], 0.0)
+    pick1 = jnp.where(lane // 8 + 16 == head, small[1:2, :], 0.0)
+    pair = jnp.where(head % 2 == 0, small[2:3, :], small[3:4, :])
+    pick2 = jnp.where(lane // 8 == head // 2, pair, 0.0)
+    gains[...] = dot_exact(first, pick0 + pick1, NT) + dot_exact(second, pick2, NT)
+
+
+def finish(query_grad, input_grad, gate, key_weight, value_weight, small, heads, levels):
+    vm = pl.BlockSpec(memory_space=pltpu.VMEM)
+    outs = [
+        jax.ShapeDtypeStruct(a.shape, a.dtype)
+        for a in (query_grad, input_grad)
+    ]
+    outs.append(jax.ShapeDtypeStruct((heads, TOK), F32))
+    outs += [jax.ShapeDtypeStruct(a.shape, a.dtype) for a in (key_weight, value_weight)]
+    outs.append(jax.ShapeDtypeStruct((levels, heads), F32))
+    return pl.pallas_call(
+        finish_kernel,
+        in_specs=[vm] * 6,
+        out_specs=[vm] * 6,
+        out_shape=outs,
+        name="finish",
+    )(query_grad, input_grad, gate, key_weight, value_weight, small)
+
+
 def local(hidden, queries, w_key, w_value, log_gate, level_gain, segment_ids, out_grad):
     heads, levels = level_gain.shape
-    query_grad, input_grad, gate, key_weight, value_weight, summed = whole_step(
-        hidden[0], queries[0], out_grad[0], w_key, w_value, log_gate[0], segment_ids, level_gain
+    parts = whole_step(
+        hidden[0], queries[0], out_grad[0], w_key, w_value, log_gate[0], segment_ids, level_gain.T
     )
-    inner = summed[:2].reshape(heads, 8)
-    outer = summed[2:4].reshape(2, heads // 2, 8).transpose(1, 0, 2).reshape(heads, 8)
-    gain_total = jnp.concatenate([inner, outer, jnp.zeros((heads, levels - 16), F32)], axis=1)
-    gate_grad = (gate + summed[8].reshape(16, 8)[:, :, None])[:, :2].reshape(heads, TOK)
+    query_grad, input_grad, gate_grad, key_weight, value_weight, gains = finish(
+        *parts, heads, levels
+    )
     return (
         query_grad[None],
         input_grad[None],
         gate_grad[None],
         key_weight,
         value_weight,
-        gain_total,
+        gains.T,
     )
 
 

time: 92.8 us -> 82.9 us (0.89)
  local copies, waits for them, and re-layouts: 10.3 us -> 0 us
  Pallas kernels: 78.7 us -> 81 us
  other arithmetic: 1.62 us -> 0 us
    unnamed x6 -> x0, local copies, waits for them, and re-layouts: 8.57 us -> none
    pallas_call x0 -> x1, Pallas kernels: none -> 2.29 us  [finish(): pl.pallas_call(finish_kernel, in_specs=[vm] * 6, out_specs=[vm] * 6, out_...]
    add x1 -> x0, other arithmetic: 1.54 us -> none  [local(): gate + summed[8].reshape(16, 8)[:, :, None]]
    slice x2 -> x0, local copies, waits for them, and re-layouts: 1.44 us -> none  [the longest x1 0.75 us: local(): inner = summed[:2].reshape(heads, 8)]
where the time goes in v3:
time: 82.9 us; the launch traced here: 81.7 us
  Pallas kernels  81 us (98%)
    pallas_call x1, Pallas kernels, whole_step(): pl.pallas_call(step_kernel, in_specs=[far] * 5 + [vm, vm, pl.BlockSpec(me...  78.7 us
    pallas_call x1, Pallas kernels, finish(): pl.pallas_call(finish_kernel, in_specs=[vm] * 6, out_specs=[vm] * 6, out_...  2.29 us

profile of v3, /device:TPU:0, one launch (start us, length us, event | category | flops | bytes accessed | tf_op | source)
XLA Modules:
  0.0 81.7 jit_solution(17871314036103050828)
XLA Ops:
  0.6 78.7 %whole_step.1 = (bf16[128,2048]{1,0:T(8,128)(2,1)}, bf16[128,1024]{1,0:T(8,128)(2,1)}, f32[16,8,128]{2,1,0:T(8,128)}, f32[8,2048]{1,0:T(8,128)}, f32[8,2048]{1,0:T(8,128)}, /*index=5*/f32[16,128]{1,0:T(8,128)}) custom-call(bf16[128,1024]{1,0:T(8,128)(2,1)} %bitcast.11, bf16[128,2048]{1,0:T(8,128)(2,1)} %bitcast.9, bf16[128,2048]{1,0:T(8,128)(2,1)} %bitcast.10, ...), custom_call_target="tpu_custom_call" | custom-call | tf_op jit(solution)/shard_map/whole_step/pallas_call | solution.py:734
  79.4 2.3 %finish.1 = (bf16[128,2048]{1,0:T(8,128)(2,1)}, bf16[128,1024]{1,0:T(8,128)(2,1)}, f32[32,128]{1,0:T(8,128)}, f32[8,2048]{1,0:T(8,128)}, f32[8,2048]{1,0:T(8,128)}, /*index=5*/f32[18,32]{1,0:T(8,128)}) custom-call(bf16[128,2048]{1,0:T(8,128)(2,1)} %get-tuple-element.18.qg_ref, bf16[128,1024]{1,0:T(8,128)(2,1)} %get-tuple-element.19.ig_ref, ...), custom_call_target="tpu_custom_call" | custom-call | tf_op jit(solution)/shard_map/finish/pallas_call | solution.py:788

commit v4 on v3

--- a/solution.py
+++ b/solution.py
@@ -22,7 +22,6 @@
 TOK = 128
 PAIR = 128
 HALF_ROWS = 1088
-SROWS = 1024
 
 
 def dot(a, b, dims):
@@ -104,14 +103,14 @@
         segc=f(TOK, TOK),
         st=f(2, HALF_ROWS, PAIR),
         both=f(2, HALF_ROWS, PAIR),
-        chip_send=f(4, 272, PAIR),
-        chip_recv=f(4, 272, PAIR),
-        tot_send=f(2, 144, PAIR),
-        tot_recv=f(2, 144, PAIR),
-        back_send=f(4, 256, PAIR),
-        back_recv=f(4, 256, PAIR),
-        own_blocks=f(2, SROWS, PAIR),
-        s_in=f(2, SROWS, PAIR),
+        chip_send=f(2, 4, 136, PAIR),
+        chip_recv=f(2, 4, 136, PAIR),
+        tot_send=f(2, 2, 72, PAIR),
+        tot_recv=f(2, 2, 72, PAIR),
+        back_send=f(2, 4, 128, PAIR),
+        back_recv=f(2, 4, 128, PAIR),
+        own_blocks=f(2, 2, 512, PAIR),
+        s_in=f(2, 2, 512, PAIR),
         gcross=f(16, 8, PAIR),
         gint=f(16, 16, PAIR),
         gate=f(16, 8, TOK),
@@ -342,7 +341,7 @@
     both, st = s["both"], s["st"]
     swap = remote(st.at[1 - c], both.at[c], sib)
     both[pl.ds(c, 1)] = st[pl.ds(c, 1)]
-    lax.fori_loop(0, 2, inner, 0)
+    lax.fori_loop(0, 1, inner, 0)
     swap.wait()
 
     def meta_rows(total, first, last):
@@ -351,52 +350,42 @@
         )
 
     chip_send, chip_recv = s["chip_send"], s["chip_recv"]
-    for pp in range(8):
+
+    def block_pair(pp):
         f0 = both[0, pp * 64 : pp * 64 + 64, :]
         f1 = both[1, pp * 64 : pp * 64 + 64, :]
         r0 = both[0, 512 + pp * 64 : 576 + pp * 64, :]
         r1 = both[1, 512 + pp * 64 : 576 + pp * 64, :]
         m0 = both[0, 1024 + pp * 8 : 1032 + pp * 8, :]
         m1 = both[1, 1024 + pp * 8 : 1032 + pp * 8, :]
-        t0, first0, last0 = m0[0:1], m0[1:2], m0[2:3]
-        t1, first1, last1 = m1[0:1], m1[1:2], m1[2:3]
-        n, p = pp // 2, pp % 2
-        chip_send[n, p * 64 : p * 64 + 64, :] = f1 + linked(last0, last1, t1) * f0
-        chip_send[n, 128 + p * 64 : 192 + p * 64, :] = r0 + linked(first0, first1, t0) * r1
-        chip_send[n, 256 + p * 8 : 264 + p * 8, :] = meta_rows(t0 + t1, first0, last1)
+        return f0, f1, r0, r1, m0[0:1], m0[1:2], m0[2:3], m1[0:1], m1[1:2], m1[2:3]
+
+    xs = []
+    for p in range(2):
+        for n in range(4):
+            f0, f1, r0, r1, t0, first0, last0, t1, first1, last1 = block_pair(2 * n + p)
+            chip_send[p, n, 0:64, :] = f1 + linked(last0, last1, t1) * f0
+            chip_send[p, n, 64:128, :] = r0 + linked(first0, first1, t0) * r1
+            chip_send[p, n, 128:136, :] = meta_rows(t0 + t1, first0, last1)
+        copies = []
+        for d in (1, 2, 3):
+            to = ring(x, d)
+            copies.append(remote(chip_send.at[p, to], chip_recv.at[p, x], {"x": to}))
+        chip_recv[p, pl.ds(x, 1)] = chip_send[p, pl.ds(x, 1)]
+        xs.append(copies)
+    for pp in range(8):
+        f0, _, _, r1, _, _, last0, _, first1, _ = block_pair(pp)
         d8 = same(last0, first1) * jnp.sum(f0 * r1, axis=0, keepdims=True)
         s["gcross"][pl.ds(c * 8 + pp, 1)] = jnp.where(row8 == 0, d8, 0.0)[None]
-
-    xs = []
-    for d in (1, 2, 3):
-        to = ring(x, d)
-        xs.append(remote(chip_send.at[to], chip_recv.at[x], {"x": to}))
-    chip_recv[pl.ds(x, 1)] = chip_send[pl.ds(x, 1)]
-
-    def forward(n):
-        axis, index, buf = gathers[n]
-        out = []
-        for m, d in enumerate((1, 3)):
-            hops[2 * n + m].wait()
-            came = ring(index, 4 - d)
-            part = slice(0, 512) if d == 1 else slice(512, 1024)
-            out.append(
-                remote(buf.at[came, c, part], buf.at[came, c, part], {axis: ring(index, d)})
-            )
-            down.append(remote(buf.at[came, c], buf.at[came, c], sib))
-        return out
-
-    fwd_y = forward(0)
-    lax.fori_loop(2, 8, inner, 0)
-    wait(xs)
+    lax.fori_loop(1, 7, inner, 0)
 
     def chip(j, p):
         return (
-            chip_recv[j, p * 64 : p * 64 + 64, :],
-            chip_recv[j, 128 + p * 64 : 192 + p * 64, :],
-            chip_recv[j, 256 + p * 8 : 257 + p * 8, :],
-            chip_recv[j, 257 + p * 8 : 258 + p * 8, :],
-            chip_recv[j, 258 + p * 8 : 259 + p * 8, :],
+            chip_recv[p, j, 0:64, :],
+            chip_recv[p, j, 64:128, :],
+            chip_recv[p, j, 128:129, :],
+            chip_recv[p, j, 129:130, :],
+            chip_recv[p, j, 130:131, :],
         )
 
     def joined(p):
@@ -410,22 +399,25 @@
         return f01, r01, f23, r23
 
     tot_send, tot_recv = s["tot_send"], s["tot_recv"]
+    zs = []
     for p in range(2):
+        wait(xs[p])
         f01, r01, f23, r23 = joined(p)
         t0, a0 = chip(0, p)[2:4]
         t1, l1 = chip(1, p)[2], chip(1, p)[4]
         t2, a2 = chip(2, p)[2:4]
         t3, l3 = chip(3, p)[2], chip(3, p)[4]
-        tot_send[0, p * 64 : p * 64 + 64, :] = f23 + linked(l1, l3, t2 + t3) * f01
-        tot_send[1, p * 64 : p * 64 + 64, :] = r01 + linked(a0, a2, t0 + t1) * r23
-        tot_send[0, 128 + p * 8 : 136 + p * 8, :] = jnp.broadcast_to(l3, (8, PAIR))
-        tot_send[1, 128 + p * 8 : 136 + p * 8, :] = jnp.broadcast_to(a0, (8, PAIR))
-    zs = [
-        remote(tot_send.at[n], tot_recv.at[n], {"z": ring(z, d)}) for n, d in ((0, 1), (1, 3))
-    ]
-    fwd_z = forward(1)
-    lax.fori_loop(8, 10, inner, 0)
-    wait(zs)
+        tot_send[p, 0, 0:64, :] = f23 + linked(l1, l3, t2 + t3) * f01
+        tot_send[p, 1, 0:64, :] = r01 + linked(a0, a2, t0 + t1) * r23
+        tot_send[p, 0, 64:72, :] = jnp.broadcast_to(l3, (8, PAIR))
+        tot_send[p, 1, 64:72, :] = jnp.broadcast_to(a0, (8, PAIR))
+        zs.append(
+            [
+                remote(tot_send.at[p, n], tot_recv.at[p, n], {"z": ring(z, d)})
+                for n, d in ((0, 1), (1, 3))
+            ]
+        )
+    lax.fori_loop(7, 10, inner, 0)
 
     has_prev = (z > 0).astype(F32)
     has_next = (z < 3).astype(F32)
@@ -436,17 +428,19 @@
     def gain_row(pair, level):
         return jnp.where(low_row, gain_ref[level, 2 * pair], gain_ref[level, 2 * pair + 1])
 
+    bs = []
     for p in range(2):
+        wait(zs[p])
         (f0, r0, t0, a0, l0), (f1, r1, t1, a1, l1), (f2, r2, t2, a2, l2), (f3, r3, t3, a3, l3) = (
             chip(j, p) for j in range(4)
         )
         f01, r01, f23, r23 = joined(p)
         pair = c * 8 + 2 * x + p
         g9, g10, g11, g12 = (gain_row(pair, level) for level in range(9, 13))
-        zf = has_prev * tot_recv[0, p * 64 : p * 64 + 64, :]
-        zl = tot_recv[0, 128 + p * 8 : 129 + p * 8, :]
-        zr = has_next * tot_recv[1, p * 64 : p * 64 + 64, :]
-        za = tot_recv[1, 128 + p * 8 : 129 + p * 8, :]
+        zf = has_prev * tot_recv[p, 0, 0:64, :]
+        zl = tot_recv[p, 0, 64:65, :]
+        zr = has_next * tot_recv[p, 1, 0:64, :]
+        za = tot_recv[p, 1, 64:65, :]
         gzf = g11 * (1.0 - prev_top) + g12 * prev_top
         gzr = g11 * (1.0 - next_top) + g12 * next_top
         sf = (
@@ -466,21 +460,33 @@
             gzr * same(za, l3) * zr,
         )
         for j in range(4):
-            back_send[j, p * 64 : p * 64 + 64, :] = sf[j]
-            back_send[j, 128 + p * 64 : 192 + p * 64, :] = sr[j]
-    bs = []
-    for d in (1, 2, 3):
-        to = ring(x, d)
-        bs.append(remote(back_send.at[to], back_recv.at[x], {"x": to}))
-    back_recv[pl.ds(x, 1)] = back_send[pl.ds(x, 1)]
+            back_send[p, j, 0:64, :] = sf[j]
+            back_send[p, j, 64:128, :] = sr[j]
+        copies = []
+        for d in (1, 2, 3):
+            to = ring(x, d)
+            copies.append(remote(back_send.at[p, to], back_recv.at[p, x], {"x": to}))
+        back_recv[p, pl.ds(x, 1)] = back_send[p, pl.ds(x, 1)]
+        bs.append(copies)
+
+    fwd = []
+    for n, (axis, index, buf) in enumerate(gathers):
+        for m, d in enumerate((1, 3)):
+            hops[2 * n + m].wait()
+            came = ring(index, 4 - d)
+            part = slice(0, 512) if d == 1 else slice(512, 1024)
+            fwd.append(
+                remote(buf.at[came, c, part], buf.at[came, c, part], {axis: ring(index, d)})
+            )
+            down.append(remote(buf.at[came, c], buf.at[came, c], sib))
 
     for p in range(2):
         (f0, r0, t0, a0, l0), (f1, r1, t1, a1, l1), (f2, r2, t2, a2, l2), (f3, r3, t3, a3, l3) = (
             chip(j, p) for j in range(4)
         )
         f01, r01, f23, r23 = joined(p)
-        zf = has_prev * tot_recv[0, p * 64 : p * 64 + 64, :]
-        zl = tot_recv[0, 128 + p * 8 : 129 + p * 8, :]
+        zf = has_prev * tot_recv[p, 0, 0:64, :]
+        zl = tot_recv[p, 0, 64:65, :]
         r_group = r01 + linked(a0, a2, t0 + t1) * r23
         d9 = same(l0, a1) * jnp.sum(f0 * r1, axis=0, keepdims=True) + same(l2, a3) * jnp.sum(
             f2 * r3, axis=0, keepdims=True
@@ -501,45 +507,37 @@
         pair = c * 8 + 2 * x + p
         s["gcross"][pl.ds(pair, 1)] = s["gcross"][pl.ds(pair, 1)] + rows[None]
     lax.fori_loop(10, 16, inner, 0)
-    wait(bs)
 
     own_blocks, s_in = s["own_blocks"], s["s_in"]
-    for pp in range(8):
-        n, p = pp // 2, pp % 2
-        f0 = both[0, pp * 64 : pp * 64 + 64, :]
-        r1 = both[1, 512 + pp * 64 : 576 + pp * 64, :]
-        m0 = both[0, 1024 + pp * 8 : 1032 + pp * 8, :]
-        m1 = both[1, 1024 + pp * 8 : 1032 + pp * 8, :]
-        t0, first0, last0 = m0[0:1], m0[1:2], m0[2:3]
-        t1, first1, last1 = m1[0:1], m1[1:2], m1[2:3]
-        sf = back_recv[n, p * 64 : p * 64 + 64, :]
-        sr = back_recv[n, 128 + p * 64 : 192 + p * 64, :]
-        link = gain_row(c * 8 + pp, 8) * same(last0, first1)
-        own_blocks[0, pp * 64 : pp * 64 + 64, :] = sf
-        own_blocks[1, pp * 64 : pp * 64 + 64, :] = linked(first0, first1, t0) * sf + link * f0
-        own_blocks[0, 512 + pp * 64 : 576 + pp * 64, :] = linked(last0, last1, t1) * sr + link * r1
-        own_blocks[1, 512 + pp * 64 : 576 + pp * 64, :] = sr
-    swap = remote(own_blocks.at[1 - c], s_in.at[c], sib)
-    s_in[pl.ds(c, 1)] = own_blocks[pl.ds(c, 1)]
-
-    for (_, index, buf), copies in zip(gathers, (fwd_y, fwd_z)):
-        buf[pl.ds(index, 1), pl.ds(c, 1)] = s["hid_t"][...][None, None]
-        wait(copies)
-        came = ring(index, 2)
-        down.append(remote(buf.at[came, c], buf.at[came, c], sib))
-    swap.wait()
+    swaps = []
+    for p in range(2):
+        wait(bs[p])
+        for n in range(4):
+            pp = 2 * n + p
+            f0, _, _, r1, t0, first0, last0, t1, first1, last1 = block_pair(pp)
+            sf = back_recv[p, n, 0:64, :]
+            sr = back_recv[p, n, 64:128, :]
+            link = gain_row(c * 8 + pp, 8) * same(last0, first1)
+            at = n * 128
+            own_blocks[p, 0, at : at + 64, :] = sf
+            own_blocks[p, 1, at : at + 64, :] = linked(first0, first1, t0) * sf + link * f0
+            own_blocks[p, 0, at + 64 : at + 128, :] = linked(last0, last1, t1) * sr + link * r1
+            own_blocks[p, 1, at + 64 : at + 128, :] = sr
+        swaps.append(remote(own_blocks.at[p, 1 - c], s_in.at[p, c], sib))
+        s_in[p, pl.ds(c, 1)] = own_blocks[p, pl.ds(c, 1)]
 
     tail = causal.astype(BF16)
     head_pick = (cols_i[0:8, :] // 64 == row8).astype(BF16)
 
-    def cross(pair, carry):
-        half, pp = pair // 8, lax.rem(pair, 8)
+    def cross(to, p):
+        pair = 2 * to + p
+        half, quarter = to // 4, lax.rem(to, 4)
         cols = rows_of(pair * PAIR, PAIR)
         q, g = s["q"][:, cols], s["g"][:, cols]
         k, v = s["k"][pair], s["v"][pair]
         first_w, last_w = s["fw"][pair], s["lw"][pair]
-        sf = s_in[half, rows_of(pp * 64, 64), :]
-        sr = s_in[half, rows_of(512 + pp * 64, 64), :]
+        sf = s_in[p, half, rows_of(quarter * 128, 64), :]
+        sr = s_in[p, half, rows_of(quarter * 128 + 64, 64), :]
 
         def diag(a):
             return jnp.concatenate([jnp.where(low_half, a, 0.0), jnp.where(low_half, 0.0, a)], axis=0)
@@ -556,14 +554,14 @@
         value_sum = (s["vacc"][pair] + rk).astype(BF16)
         s["ksb"][:, cols] = key_sum
         s["vsb"][:, cols] = value_sum
-        s["ks"][half, pp] = key_sum.astype(F32)
-        s["vs"][half, pp] = value_sum.astype(F32)
-        return carry
+        s["ks"][p, to] = key_sum.astype(F32)
+        s["vs"][p, to] = value_sum.astype(F32)
 
     firsts = []
     me_y, me_z = 2 * y + c, 2 * z + c
     for n in range(2):
-        lax.fori_loop(8 * n, 8 * n + 8, cross, 0)
+        swaps[n].wait()
+        lax.fori_loop(0, 8, lambda to, carry: cross(to, n), None)
         fk, fv = [], []
         for d, e in offsets:
             dev, to = plane("batch", y, d, e)
@@ -590,6 +588,11 @@
         smalls.append(remote(small, m1.at[me_z], plane("z", z, d, e)[0]))
     m1[pl.ds(me_z, 1)] = small[...][None]
 
+    for n, (_, index, buf) in enumerate(gathers):
+        buf[pl.ds(index, 1), pl.ds(c, 1)] = s["hid_t"][...][None, None]
+        wait(fwd[2 * n : 2 * n + 2])
+        came = ring(index, 2)
+        down.append(remote(buf.at[came, c], buf.at[came, c], sib))
     wait(down)
     for name, out in (("hy", "hyb"), ("hz", "hzb")):
         for g in range(8):
@@ -723,7 +726,7 @@
     wait(fins)
     for n in range(2):
         for g in range(8):
-            cols = slice(n * 1024 + g * PAIR, n * 1024 + (g + 1) * PAIR)
+            cols = slice((2 * g + n) * PAIR, (2 * g + n + 1) * PAIR)
             kout_ref[:, cols] = s["kfin"][g, n]
             vout_ref[:, cols] = s["vfin"][g, n]
 

time: 82.9 us -> 77.7 us (0.937)
  Pallas kernels: 81 us -> 75.8 us
    pallas_call x1, Pallas kernels: 78.7 us -> 73.5 us  [whole_step(): pl.pallas_call(step_kernel, in_specs=[far] * 5 + [vm, vm, pl.BlockSpec(me...]
where the time goes in v4:
time: 77.7 us; the launch traced here: 76.5 us
  Pallas kernels  75.8 us (98%)
    pallas_call x1, Pallas kernels, whole_step(): pl.pallas_call(step_kernel, in_specs=[far] * 5 + [vm, vm, pl.BlockSpec(me...  73.5 us
    pallas_call x1, Pallas kernels, finish(): pl.pallas_call(finish_kernel, in_specs=[vm] * 6, out_specs=[vm] * 6, out_...  2.29 us

profile of v4, /device:TPU:0, one launch (start us, length us, event | category | flops | bytes accessed | tf_op | source)
XLA Modules:
  0.0 76.5 jit_solution(16130370398070793440)
XLA Ops:
  0.6 73.5 %whole_step.1 = (bf16[128,2048]{1,0:T(8,128)(2,1)}, bf16[128,1024]{1,0:T(8,128)(2,1)}, f32[16,8,128]{2,1,0:T(8,128)}, f32[8,2048]{1,0:T(8,128)}, f32[8,2048]{1,0:T(8,128)}, /*index=5*/f32[16,128]{1,0:T(8,128)}) custom-call(bf16[128,1024]{1,0:T(8,128)(2,1)} %bitcast.11, bf16[128,2048]{1,0:T(8,128)(2,1)} %bitcast.9, bf16[128,2048]{1,0:T(8,128)(2,1)} %bitcast.10, ...), custom_call_target="tpu_custom_call" | custom-call | tf_op jit(solution)/shard_map/whole_step/pallas_call | solution.py:737
  74.2 2.3 %finish.1 = (bf16[128,2048]{1,0:T(8,128)(2,1)}, bf16[128,1024]{1,0:T(8,128)(2,1)}, f32[32,128]{1,0:T(8,128)}, f32[8,2048]{1,0:T(8,128)}, f32[8,2048]{1,0:T(8,128)}, /*index=5*/f32[18,32]{1,0:T(8,128)}) custom-call(bf16[128,2048]{1,0:T(8,128)(2,1)} %get-tuple-element.18.qg_ref, bf16[128,1024]{1,0:T(8,128)(2,1)} %get-tuple-element.19.ig_ref, ...), custom_call_target="tpu_custom_call" | custom-call | tf_op jit(solution)/shard_map/finish/pallas_call | solution.py:791

commit v5 on v4

--- a/solution.py
+++ b/solution.py
@@ -75,7 +75,7 @@
 
 
 SENDS = 128
-LOCALS = 24
+LOCALS = 32
 VMEM_LIMIT = 56 * 2**20
 
 
@@ -101,7 +101,7 @@
         fw=f(16, TOK, PAIR),
         lw=f(16, TOK, PAIR),
         segc=f(TOK, TOK),
-        st=f(2, HALF_ROWS, PAIR),
+        st=f(HALF_ROWS, PAIR),
         both=f(2, HALF_ROWS, PAIR),
         chip_send=f(2, 4, 136, PAIR),
         chip_recv=f(2, 4, 136, PAIR),
@@ -141,6 +141,14 @@
         m2=f(4, 16, PAIR),
         m2s=f(8, PAIR),
         m3=f(4, 8, PAIR),
+        lg=f(32, TOK),
+        segr=pltpu.VMEM((1, TOK), jnp.int32),
+        gain=pltpu.SMEM((18, 32), F32),
+        qg=b(TOK, 2048),
+        ig=b(TOK, 1024),
+        kout=f(8, 2048),
+        vout=f(8, 2048),
+        sout=f(16, PAIR),
         send_sem=pltpu.SemaphoreType.DMA((SENDS,)),
         recv_sem=pltpu.SemaphoreType.DMA((SENDS,)),
         local_sem=pltpu.SemaphoreType.DMA((LOCALS,)),
@@ -153,18 +161,20 @@
     g_hbm,
     wk_hbm,
     wv_hbm,
-    lg_ref,
-    segr_ref,
-    gain_ref,
-    qg_ref,
-    ig_ref,
-    gate_ref,
-    kout_ref,
-    vout_ref,
-    sout_ref,
+    lg_hbm,
+    segr_hbm,
+    gain_hbm,
+    qg_hbm,
+    ig_hbm,
+    gate_hbm,
+    kout_hbm,
+    vout_hbm,
+    sout_hbm,
     *refs,
 ):
     s = dict(zip(scratch(), refs))
+    gain_ref, qg_ref, ig_ref = s["gain"], s["qg"], s["ig"]
+    kout_ref, vout_ref, sout_ref = s["kout"], s["vout"], s["sout"]
     x, y, z, c = (lax.axis_index(a) for a in ("x", "batch", "z", "core"))
     used = [0]
 
@@ -203,13 +213,21 @@
         pltpu.make_async_copy(hid_hbm, s["hid"], local_sem.at[0]),
         pltpu.make_async_copy(q_hbm, s["q"], local_sem.at[1]),
         pltpu.make_async_copy(g_hbm, s["g"], local_sem.at[2]),
+        pltpu.make_async_copy(lg_hbm, s["lg"], local_sem.at[3]),
+        pltpu.make_async_copy(segr_hbm, s["segr"], local_sem.at[4]),
+        pltpu.make_async_copy(gain_hbm, s["gain"], local_sem.at[5]),
     ]
 
+    def step_at(i):
+        return lax.rem(i + 4 - 4 * c, 8)
+
     def weight_load(hbm, name, i, base):
-        cols = rows_of(i * 256, 256)
+        cols = rows_of(step_at(i) * 256, 256)
         return pltpu.make_async_copy(hbm.at[:, cols], s[name].at[:, cols], local_sem.at[base + i])
 
     first_loads[0].start()
+    for n in (3, 4, 5):
+        first_loads[n].start()
     for i in range(8):
         weight_load(wk_hbm, "wk", i, 8).start()
         weight_load(wv_hbm, "wv", i, 16).start()
@@ -224,7 +242,9 @@
     low_half = iota((64, PAIR), 1) < 64
     row8 = iota((8, PAIR), 0)
     low_row = iota((1, PAIR), 1) < 64
-    log_gate = lg_ref[...]
+    for n in (3, 4, 5):
+        first_loads[n].wait()
+    log_gate = s["lg"][...]
     cum_cols = dot_exact(lower, log_gate, NT)
     s["cumr"][...] = dot_exact(log_gate, lower, NT)
     for pair in range(16):
@@ -232,7 +252,7 @@
             low, cum_cols[:, 2 * pair : 2 * pair + 1], cum_cols[:, 2 * pair + 1 : 2 * pair + 2]
         )
         s["cumr3"][pair, 0:2, :] = s["cumr"][2 * pair : 2 * pair + 2, :]
-    seg_row = segr_ref[...].astype(F32)
+    seg_row = s["segr"][...].astype(F32)
     s["segc"][...] = jnp.broadcast_to(seg_row, (TOK, TOK)).T
     s["gcross"][...] = jnp.zeros((16, 8, PAIR), F32)
 
@@ -240,26 +260,19 @@
     for b in range(8):
         cols = slice(b * TOK, (b + 1) * TOK)
         s["hid_t"][cols, :] = s["hid"][:, cols].astype(F32).T
-    pl.semaphore_wait(barrier, len(peers))
-    gathers = (("batch", y, s["hy"]), ("z", z, s["hz"]))
-    hops = []
-    for axis, index, buf in gathers:
-        for d in (1, 3):
-            hops.append(remote(s["hid_t"], buf.at[index, c], {axis: ring(index, d)}))
-    down = [remote(s["hid_t"], buf.at[index, c], sib) for _, index, buf in gathers]
 
     first_loads[1].wait()
     first_loads[2].wait()
 
-    def project(step, carry):
-        weight_load(wk_hbm, "wk", step, 8).wait()
-        weight_load(wv_hbm, "wv", step, 16).wait()
+    def project(i, st):
+        step = step_at(i)
+        weight_load(wk_hbm, "wk", i, 8).wait()
+        weight_load(wv_hbm, "wv", i, 16).wait()
         wide = rows_of(step * 256, 256)
         hid = s["hid"][...]
         keys = dot(hid, s["wk"][:, wide], NN).astype(BF16)
         values = dot(hid, s["wv"][:, wide], NN).astype(BF16)
         segc = s["segc"][...]
-        half = step // 4
         for p in range(2):
             pair = 2 * step + p
             k, v = keys[:, p * PAIR : (p + 1) * PAIR], values[:, p * PAIR : (p + 1) * PAIR]
@@ -275,8 +288,8 @@
             fwd = dot_left(k.astype(F32) * last_w, v, TN)
             rev = dot_left(s["q"][:, cols].astype(F32) * first_w, s["g"][:, cols], TN)
             pp = 2 * lax.rem(step, 4) + p
-            s["st"][half, rows_of(pp * 64, 64), :] = jnp.where(low_half, fwd[:64], fwd[64:])
-            s["st"][half, rows_of(512 + pp * 64, 64), :] = jnp.where(low_half, rev[:64], rev[64:])
+            st[rows_of(pp * 64, 64), :] = jnp.where(low_half, fwd[:64], fwd[64:])
+            st[rows_of(512 + pp * 64, 64), :] = jnp.where(low_half, rev[:64], rev[64:])
             meta = jnp.where(
                 row8 == 0,
                 total,
@@ -284,10 +297,20 @@
                     row8 == 1, segc[0:1, :], jnp.where(row8 == 2, segc[TOK - 1 : TOK, :], 0.0)
                 ),
             )
-            s["st"][half, rows_of(1024 + pp * 8, 8), :] = meta
-        return carry
-
-    lax.fori_loop(0, 8, project, 0)
+            st[rows_of(1024 + pp * 8, 8), :] = meta
+
+    both = s["both"]
+    lax.fori_loop(0, 4, lambda i, carry: project(i, s["st"]), None)
+    pl.semaphore_wait(barrier, len(peers))
+    swap = remote(s["st"], both.at[c], sib)
+
+    gathers = (("batch", y, s["hy"]), ("z", z, s["hz"]))
+    hops = []
+    for axis, index, buf in gathers:
+        for d in (1, 3):
+            hops.append(remote(s["hid_t"], buf.at[index, c], {axis: ring(index, d)}))
+    down = [remote(s["hid_t"], buf.at[index, c], sib) for _, index, buf in gathers]
+    lax.fori_loop(4, 8, lambda i, carry: project(i, both.at[c]), None)
 
     def inner(pair, carry):
         cols = rows_of(pair * PAIR, PAIR)
@@ -338,10 +361,6 @@
         s["gint"][pair] = jnp.concatenate(gain_rows, axis=0)
         return carry
 
-    both, st = s["both"], s["st"]
-    swap = remote(st.at[1 - c], both.at[c], sib)
-    both[pl.ds(c, 1)] = st[pl.ds(c, 1)]
-    lax.fori_loop(0, 1, inner, 0)
     swap.wait()
 
     def meta_rows(total, first, last):
@@ -377,7 +396,7 @@
         f0, _, _, r1, _, _, last0, _, first1, _ = block_pair(pp)
         d8 = same(last0, first1) * jnp.sum(f0 * r1, axis=0, keepdims=True)
         s["gcross"][pl.ds(c * 8 + pp, 1)] = jnp.where(row8 == 0, d8, 0.0)[None]
-    lax.fori_loop(1, 7, inner, 0)
+    lax.fori_loop(0, 7, inner, 0)
 
     def chip(j, p):
         return (
@@ -529,48 +548,67 @@
     tail = causal.astype(BF16)
     head_pick = (cols_i[0:8, :] // 64 == row8).astype(BF16)
 
-    def cross(to, p):
+    def diag(a):
+        return jnp.concatenate([jnp.where(low_half, a, 0.0), jnp.where(low_half, 0.0, a)], axis=0)
+
+    def incoming(to, p, part):
+        at = lax.rem(to, 4) * 128 + part * 64
+        return diag(s_in[p, to // 4, rows_of(at, 64), :])
+
+    def key_part(to, p):
         pair = 2 * to + p
-        half, quarter = to // 4, lax.rem(to, 4)
+        rv = s["lw"][pair] * dot_right(s["v"][pair], incoming(to, p, 1), NT)
+        key_sum = (s["kacc"][pair] + rv).astype(BF16)
+        s["kacc"][pair] = s["k"][pair].astype(F32) * rv
+        s["ksb"][:, rows_of(pair * PAIR, PAIR)] = key_sum
+        s["ks"][p, to] = key_sum.astype(F32)
+
+    def value_part(to, p):
+        pair = 2 * to + p
+        rk = s["lw"][pair] * dot_right(s["k"][pair], incoming(to, p, 1), NN)
+        value_sum = (s["vacc"][pair] + rk).astype(BF16)
+        s["vsb"][:, rows_of(pair * PAIR, PAIR)] = value_sum
+        s["vs"][p, to] = value_sum.astype(F32)
+
+    def query_part(to, p):
+        pair = 2 * to + p
         cols = rows_of(pair * PAIR, PAIR)
-        q, g = s["q"][:, cols], s["g"][:, cols]
-        k, v = s["k"][pair], s["v"][pair]
-        first_w, last_w = s["fw"][pair], s["lw"][pair]
-        sf = s_in[p, half, rows_of(quarter * 128, 64), :]
-        sr = s_in[p, half, rows_of(quarter * 128 + 64, 64), :]
-
-        def diag(a):
-            return jnp.concatenate([jnp.where(low_half, a, 0.0), jnp.where(low_half, 0.0, a)], axis=0)
-
-        sg = first_w * dot_right(g, diag(sf), NT)
-        rv = last_w * dot_right(v, diag(sr), NT)
-        rk = last_w * dot_right(k, diag(sr), NN)
-        diff = q.astype(F32) * sg - k.astype(F32) * rv
+        sg = s["fw"][pair] * dot_right(s["g"][:, cols], incoming(to, p, 0), NT)
+        qg_ref[:, cols] = (s["qacc"][pair] + sg).astype(BF16)
+        diff = s["q"][:, cols].astype(F32) * sg - s["kacc"][pair]
         hi, lo = split2(diff)
         diff_rows = dot(head_pick, hi, NT) + dot(head_pick, lo, NT)
         s["gate"][pair] = s["gate"][pair] + dot_left(diff_rows, tail, NN)
-        qg_ref[:, cols] = (s["qacc"][pair] + sg).astype(BF16)
-        key_sum = (s["kacc"][pair] + rv).astype(BF16)
-        value_sum = (s["vacc"][pair] + rk).astype(BF16)
-        s["ksb"][:, cols] = key_sum
-        s["vsb"][:, cols] = value_sum
-        s["ks"][p, to] = key_sum.astype(F32)
-        s["vs"][p, to] = value_sum.astype(F32)
 
     firsts = []
     me_y, me_z = 2 * y + c, 2 * z + c
+    far_first = [(2, 0), (2, 1), (1, 0), (3, 0), (1, 1), (3, 1), (0, 1)]
     for n in range(2):
         swaps[n].wait()
-        lax.fori_loop(0, 8, lambda to, carry: cross(to, n), None)
         fk, fv = [], []
-        for d, e in offsets:
+        for d, e in far_first:
             dev, to = plane("batch", y, d, e)
+            key_part(to, n)
             fk.append(remote(s["ks"].at[n, to], s["rk"].at[n, me_y], dev))
             dev, to = plane("z", z, d, e)
+            value_part(to, n)
             fv.append(remote(s["vs"].at[n, to], s["rv"].at[n, me_z], dev))
+        key_part(me_y, n)
+        value_part(me_z, n)
         s["rk"][n, pl.ds(me_y, 1)] = s["ks"][n, pl.ds(me_y, 1)]
         s["rv"][n, pl.ds(me_z, 1)] = s["vs"][n, pl.ds(me_z, 1)]
         firsts.append((fk, fv))
+    for n in range(2):
+        lax.fori_loop(0, 8, lambda to, carry: query_part(to, n), None)
+    stores = []
+
+    def store(ref, hbm):
+        cp = pltpu.make_async_copy(ref, hbm, local_sem.at[24 + len(stores)])
+        cp.start()
+        stores.append(cp)
+
+    store(qg_ref, qg_hbm)
+    store(s["gate"], gate_hbm)
 
     ones = jnp.ones((8, PAIR), F32)
     inner_sum = dot_exact(ones, s["gint"][...].reshape(256, PAIR), NT)
@@ -645,6 +683,7 @@
                 part1[3, i, b * 64 + j * 8 : b * 64 + j * 8 + 8, :] = block[at : at + 8, :]
     v1 = scatter(part1, recv1, 3, "batch", y)
     lax.fori_loop(2, 4, input_grad, 0)
+    store(ig_ref, ig_hbm)
 
     wait(smalls)
     total = m1[0, 0:8, :]
@@ -696,7 +735,6 @@
             spot = (g // 2) * 8 + j * 2 + g % 2
             later = later + (place < spot).astype(F32) * m2[j, 8 + g : 9 + g, :]
     sout_ref[8:16, :] = jnp.broadcast_to(later, (8, PAIR))
-    gate_ref[...] = s["gate"][...]
 
     fins = []
     wait(k0)
@@ -723,21 +761,24 @@
     s["vfin"][pl.ds(me_z, 1)] = s["vown"][pl.ds(me_z, 1)]
     wait(smalls)
     sout_ref[0:8, :] = m3[0] + m3[1] + m3[2] + m3[3]
+    store(sout_ref, sout_hbm)
     wait(fins)
     for n in range(2):
         for g in range(8):
             cols = slice((2 * g + n) * PAIR, (2 * g + n + 1) * PAIR)
             kout_ref[:, cols] = s["kfin"][g, n]
             vout_ref[:, cols] = s["vfin"][g, n]
+    store(kout_ref, kout_hbm)
+    store(vout_ref, vout_hbm)
+    wait(stores)
 
 
 def whole_step(hidden, queries, out_grad, w_key, w_value, log_gate, seg_row, level_gain):
-    vm = pl.BlockSpec(memory_space=pltpu.VMEM)
-    far = pl.BlockSpec(memory_space=pl.ANY)
+    far = pl.BlockSpec(memory_space=pltpu.HBM)
     return pl.pallas_call(
         step_kernel,
-        in_specs=[far] * 5 + [vm, vm, pl.BlockSpec(memory_space=pltpu.SMEM)],
-        out_specs=[vm] * 6,
+        in_specs=[far] * 8,
+        out_specs=[far] * 6,
         out_shape=[
             jax.ShapeDtypeStruct((TOK, 2048), BF16),
             jax.ShapeDtypeStruct((TOK, 1024), BF16),
@@ -755,12 +796,26 @@
 
 
 def finish_kernel(
-    qg_ref, ig_ref, gate_ref, kw_ref, vw_ref, small_ref, qg, ig, gate, kw, vw, gains
+    qg_in, ig_in, gate_in, kw_in, vw_in, small_in, qg_out, ig_out, gate_out, kw_out, vw_out, gains_out,
+    qg, ig, gate_ref, kw, vw, small_ref, gate, gains, load_sem, store_sem
 ):
-    qg[...] = qg_ref[...]
-    ig[...] = ig_ref[...]
-    kw[...] = kw_ref[...]
-    vw[...] = vw_ref[...]
+    loads = [
+        pltpu.make_async_copy(a, b, load_sem.at[n])
+        for n, (a, b) in enumerate(
+            ((gate_in, gate_ref), (small_in, small_ref), (qg_in, qg), (ig_in, ig), (kw_in, kw), (vw_in, vw))
+        )
+    ]
+    for cp in loads:
+        cp.start()
+    stores = []
+
+    def store(ref, out):
+        cp = pltpu.make_async_copy(ref, out, store_sem.at[len(stores)])
+        cp.start()
+        stores.append(cp)
+
+    loads[0].wait()
+    loads[1].wait()
     heads = gate.shape[0]
     lane = iota((heads, PAIR), 1)
     head = iota((heads, PAIR), 0)
@@ -777,24 +832,32 @@
     pair = jnp.where(head % 2 == 0, small[2:3, :], small[3:4, :])
     pick2 = jnp.where(lane // 8 == head // 2, pair, 0.0)
     gains[...] = dot_exact(first, pick0 + pick1, NT) + dot_exact(second, pick2, NT)
+    for cp, ref, out in zip(
+        loads[2:], (qg, ig, kw, vw), (qg_out, ig_out, kw_out, vw_out)
+    ):
+        cp.wait()
+        store(ref, out)
+    store(gate, gate_out)
+    store(gains, gains_out)
+    for cp in stores:
+        cp.wait()
 
 
 def finish(query_grad, input_grad, gate, key_weight, value_weight, small, heads, levels):
-    vm = pl.BlockSpec(memory_space=pltpu.VMEM)
-    outs = [
-        jax.ShapeDtypeStruct(a.shape, a.dtype)
-        for a in (query_grad, input_grad)
-    ]
-    outs.append(jax.ShapeDtypeStruct((heads, TOK), F32))
-    outs += [jax.ShapeDtypeStruct(a.shape, a.dtype) for a in (key_weight, value_weight)]
-    outs.append(jax.ShapeDtypeStruct((levels, heads), F32))
+    far = pl.BlockSpec(memory_space=pltpu.HBM)
+    parts = (query_grad, input_grad, gate, key_weight, value_weight, small)
+    outs = [jax.ShapeDtypeStruct(a.shape, a.dtype) for a in parts]
+    outs[2] = jax.ShapeDtypeStruct((heads, TOK), F32)
+    outs[5] = jax.ShapeDtypeStruct((levels, heads), F32)
     return pl.pallas_call(
         finish_kernel,
-        in_specs=[vm] * 6,
-        out_specs=[vm] * 6,
+        in_specs=[far] * 6,
+        out_specs=[far] * 6,
         out_shape=outs,
+        scratch_shapes=[pltpu.VMEM(a.shape, a.dtype) for a in (*parts, outs[2], outs[5])]
+        + [pltpu.SemaphoreType.DMA((6,)), pltpu.SemaphoreType.DMA((6,))],
         name="finish",
-    )(query_grad, input_grad, gate, key_weight, value_weight, small)
+    )(*parts)
 
 
 def local(hidden, queries, w_key, w_value, log_gate, level_gain, segment_ids, out_grad):

time: 77.7 us -> 80 us (1.030)
  Pallas kernels: 75.8 us -> 78.3 us
    pallas_call x2, Pallas kernels: 75.8 us -> 78.3 us  [the longest x1 76.1 us: whole_step(): pl.pallas_call(step_kernel, in_specs=[far] * 8, out_specs=[far] * 6, out_...]
where the time goes in v5:
time: 80 us; the launch traced here: 78.9 us
  Pallas kernels  78.3 us (98%)
    pallas_call x1, Pallas kernels, whole_step(): pl.pallas_call(step_kernel, in_specs=[far] * 8, out_specs=[far] * 6, out_...  76.1 us
    pallas_call x1, Pallas kernels, finish(): pl.pallas_call(finish_kernel, in_specs=[far] * 6, out_specs=[far] * 6, ou...  2.17 us

profile of v5, /device:TPU:0, one launch (start us, length us, event | category | flops | bytes accessed | tf_op | source)
XLA Modules:
  0.0 78.9 jit_solution(9944621422066441555)
XLA Ops:
  0.6 76.1 %whole_step.1 = (bf16[128,2048]{1,0:T(8,128)(2,1)}, bf16[128,1024]{1,0:T(8,128)(2,1)}, f32[16,8,128]{2,1,0:T(8,128)}, f32[8,2048]{1,0:T(8,128)}, f32[8,2048]{1,0:T(8,128)}, /*index=5*/f32[16,128]{1,0:T(8,128)}) custom-call(bf16[128,1024]{1,0:T(8,128)(2,1)} %bitcast.11, bf16[128,2048]{1,0:T(8,128)(2,1)} %bitcast.9, bf16[128,2048]{1,0:T(8,128)(2,1)} %bitcast.10, ...), custom_call_target="tpu_custom_call" | custom-call | tf_op jit(solution)/shard_map/whole_step/pallas_call | solution.py:778
  76.8 2.2 %finish.1 = (bf16[128,2048]{1,0:T(8,128)(2,1)}, bf16[128,1024]{1,0:T(8,128)(2,1)}, f32[32,128]{1,0:T(8,128)}, f32[8,2048]{1,0:T(8,128)}, f32[8,2048]{1,0:T(8,128)}, /*index=5*/f32[18,32]{1,0:T(8,128)}) custom-call(bf16[128,2048]{1,0:T(8,128)(2,1)} %get-tuple-element.18.qg_in, bf16[128,1024]{1,0:T(8,128)(2,1)} %get-tuple-element.19.ig_in, ...), custom_call_target="tpu_custom_call" | custom-call | tf_op jit(solution)/shard_map/finish/pallas_call | solution.py:852

commit v6 on v5

--- a/solution.py
+++ b/solution.py
@@ -196,6 +196,10 @@
         for cp in copies:
             cp.wait()
 
+    def wait_recv(copies):
+        for cp in copies:
+            cp.wait_recv()
+
     sib = {"core": 1 - c}
     offsets = [(d, e) for d in range(4) for e in (0, 1) if d or e]
 
@@ -300,15 +304,16 @@
             st[rows_of(1024 + pp * 8, 8), :] = meta
 
     both = s["both"]
-    lax.fori_loop(0, 4, lambda i, carry: project(i, s["st"]), None)
+    project(0, s["st"])
     pl.semaphore_wait(barrier, len(peers))
-    swap = remote(s["st"], both.at[c], sib)
 
     gathers = (("batch", y, s["hy"]), ("z", z, s["hz"]))
     hops = []
     for axis, index, buf in gathers:
         for d in (1, 3):
             hops.append(remote(s["hid_t"], buf.at[index, c], {axis: ring(index, d)}))
+    lax.fori_loop(1, 4, lambda i, carry: project(i, s["st"]), None)
+    swap = remote(s["st"], both.at[c], sib)
     down = [remote(s["hid_t"], buf.at[index, c], sib) for _, index, buf in gathers]
     lax.fori_loop(4, 8, lambda i, carry: project(i, both.at[c]), None)
 
@@ -379,24 +384,33 @@
         m1 = both[1, 1024 + pp * 8 : 1032 + pp * 8, :]
         return f0, f1, r0, r1, m0[0:1], m0[1:2], m0[2:3], m1[0:1], m1[1:2], m1[2:3]
 
-    xs = []
-    for p in range(2):
+    def chip_sums(p):
         for n in range(4):
             f0, f1, r0, r1, t0, first0, last0, t1, first1, last1 = block_pair(2 * n + p)
             chip_send[p, n, 0:64, :] = f1 + linked(last0, last1, t1) * f0
             chip_send[p, n, 64:128, :] = r0 + linked(first0, first1, t0) * r1
             chip_send[p, n, 128:136, :] = meta_rows(t0 + t1, first0, last1)
+
+    def chip_sends(p):
         copies = []
-        for d in (1, 2, 3):
+        for d in (2, 1, 3):
             to = ring(x, d)
             copies.append(remote(chip_send.at[p, to], chip_recv.at[p, x], {"x": to}))
         chip_recv[p, pl.ds(x, 1)] = chip_send[p, pl.ds(x, 1)]
-        xs.append(copies)
+        return copies
+
+    chip_sums(0)
+    xs = [chip_sends(0)]
+    chip_sums(1)
     for pp in range(8):
         f0, _, _, r1, _, _, last0, _, first1, _ = block_pair(pp)
         d8 = same(last0, first1) * jnp.sum(f0 * r1, axis=0, keepdims=True)
         s["gcross"][pl.ds(c * 8 + pp, 1)] = jnp.where(row8 == 0, d8, 0.0)[None]
-    lax.fori_loop(0, 7, inner, 0)
+    lax.fori_loop(0, 4, inner, 0)
+    for cp in xs[0]:
+        cp.wait_send()
+    xs.append(chip_sends(1))
+    lax.fori_loop(4, 7, inner, 0)
 
     def chip(j, p):
         return (
@@ -420,7 +434,11 @@
     tot_send, tot_recv = s["tot_send"], s["tot_recv"]
     zs = []
     for p in range(2):
-        wait(xs[p])
+        for cp in xs[p]:
+            if p == 0:
+                cp.wait_recv()
+            else:
+                cp.wait()
         f01, r01, f23, r23 = joined(p)
         t0, a0 = chip(0, p)[2:4]
         t1, l1 = chip(1, p)[2], chip(1, p)[4]
@@ -436,7 +454,19 @@
                 for n, d in ((0, 1), (1, 3))
             ]
         )
-    lax.fori_loop(7, 10, inner, 0)
+
+    fwd = []
+    for n, (axis, index, buf) in enumerate(gathers):
+        for m, d in enumerate((1, 3)):
+            hops[2 * n + m].wait()
+            came = ring(index, 4 - d)
+            part = slice(0, 512) if d == 1 else slice(512, 1024)
+            fwd.append(
+                remote(buf.at[came, c, part], buf.at[came, c, part], {axis: ring(index, d)})
+            )
+            down.append(remote(buf.at[came, c], buf.at[came, c], sib))
+
+    lax.fori_loop(7, 9, inner, 0)
 
     has_prev = (z > 0).astype(F32)
     has_next = (z < 3).astype(F32)
@@ -488,17 +518,6 @@
         back_recv[p, pl.ds(x, 1)] = back_send[p, pl.ds(x, 1)]
         bs.append(copies)
 
-    fwd = []
-    for n, (axis, index, buf) in enumerate(gathers):
-        for m, d in enumerate((1, 3)):
-            hops[2 * n + m].wait()
-            came = ring(index, 4 - d)
-            part = slice(0, 512) if d == 1 else slice(512, 1024)
-            fwd.append(
-                remote(buf.at[came, c, part], buf.at[came, c, part], {axis: ring(index, d)})
-            )
-            down.append(remote(buf.at[came, c], buf.at[came, c], sib))
-
     for p in range(2):
         (f0, r0, t0, a0, l0), (f1, r1, t1, a1, l1), (f2, r2, t2, a2, l2), (f3, r3, t3, a3, l3) = (
             chip(j, p) for j in range(4)
@@ -525,7 +544,7 @@
         )
         pair = c * 8 + 2 * x + p
         s["gcross"][pl.ds(pair, 1)] = s["gcross"][pl.ds(pair, 1)] + rows[None]
-    lax.fori_loop(10, 16, inner, 0)
+    lax.fori_loop(9, 16, inner, 0)
 
     own_blocks, s_in = s["own_blocks"], s["s_in"]
     swaps = []
@@ -583,23 +602,40 @@
     firsts = []
     me_y, me_z = 2 * y + c, 2 * z + c
     far_first = [(2, 0), (2, 1), (1, 0), (3, 0), (1, 1), (3, 1), (0, 1)]
+    swaps[0].wait()
+    fk, fv = [], []
+    for d, e in far_first:
+        dev, to = plane("batch", y, d, e)
+        key_part(to, 0)
+        fk.append(remote(s["ks"].at[0, to], s["rk"].at[0, me_y], dev))
+        dev, to = plane("z", z, d, e)
+        value_part(to, 0)
+        fv.append(remote(s["vs"].at[0, to], s["rv"].at[0, me_z], dev))
+    key_part(me_y, 0)
+    value_part(me_z, 0)
+    firsts.append((fk, fv))
+    swaps[1].wait()
+
+    def both_parts(to, carry):
+        key_part(to, 1)
+        value_part(to, 1)
+        return carry
+
+    lax.fori_loop(0, 8, both_parts, 0)
+    lax.fori_loop(0, 8, lambda to, carry: query_part(to, 0), None)
+    for cp in fk + fv:
+        cp.wait_send()
+    fk, fv = [], []
+    for d, e in far_first:
+        dev, to = plane("batch", y, d, e)
+        fk.append(remote(s["ks"].at[1, to], s["rk"].at[1, me_y], dev))
+        dev, to = plane("z", z, d, e)
+        fv.append(remote(s["vs"].at[1, to], s["rv"].at[1, me_z], dev))
+    firsts.append((fk, fv))
     for n in range(2):
-        swaps[n].wait()
-        fk, fv = [], []
-        for d, e in far_first:
-            dev, to = plane("batch", y, d, e)
-            key_part(to, n)
-            fk.append(remote(s["ks"].at[n, to], s["rk"].at[n, me_y], dev))
-            dev, to = plane("z", z, d, e)
-            value_part(to, n)
-            fv.append(remote(s["vs"].at[n, to], s["rv"].at[n, me_z], dev))
-        key_part(me_y, n)
-        value_part(me_z, n)
         s["rk"][n, pl.ds(me_y, 1)] = s["ks"][n, pl.ds(me_y, 1)]
         s["rv"][n, pl.ds(me_z, 1)] = s["vs"][n, pl.ds(me_z, 1)]
-        firsts.append((fk, fv))
-    for n in range(2):
-        lax.fori_loop(0, 8, lambda to, carry: query_part(to, n), None)
+    lax.fori_loop(0, 8, lambda to, carry: query_part(to, 1), None)
     stores = []
 
     def store(ref, hbm):
@@ -651,12 +687,12 @@
         recv[chunk, pl.ds(index, 1)] = part[chunk, pl.ds(index, 1)]
         return out
 
-    wait(firsts[0][0])
+    wait_recv(firsts[0][0])
     for b, block in product("hyb", "rk", 0):
         for j in range(4):
             part1[0, j, b * 64 : b * 64 + 64, :] = block[j * 64 : j * 64 + 64, :]
     k0 = scatter(part1, recv1, 0, "x", x)
-    wait(firsts[0][1])
+    wait_recv(firsts[0][1])
     for b, block in product("hzb", "rv", 0):
         for j in range(4):
             part1[2, j, b * 64 : b * 64 + 64, :] = block[j * 64 : j * 64 + 64, :]

time: 80 us -> 78.3 us (0.979)
  Pallas kernels: 78.3 us -> 76.6 us
    pallas_call x1, Pallas kernels: 76.1 us -> 74.4 us  [whole_step(): pl.pallas_call(step_kernel, in_specs=[far] * 8, out_specs=[far] * 6, out_...]
where the time goes in v6:
time: 78.3 us; the launch traced here: 77.2 us
  Pallas kernels  76.6 us (98%)
    pallas_call x1, Pallas kernels, whole_step(): pl.pallas_call(step_kernel, in_specs=[far] * 8, out_specs=[far] * 6, out_...  74.4 us
    pallas_call x1, Pallas kernels, finish(): pl.pallas_call(finish_kernel, in_specs=[far] * 6, out_specs=[far] * 6, ou...  2.17 us

profile of v6, /device:TPU:0, one launch (start us, length us, event | category | flops | bytes accessed | tf_op | source)
XLA Modules:
  0.0 77.2 jit_solution(7264652428875432224)
XLA Ops:
  0.6 74.4 %whole_step.1 = (bf16[128,2048]{1,0:T(8,128)(2,1)}, bf16[128,1024]{1,0:T(8,128)(2,1)}, f32[16,8,128]{2,1,0:T(8,128)}, f32[8,2048]{1,0:T(8,128)}, f32[8,2048]{1,0:T(8,128)}, /*index=5*/f32[16,128]{1,0:T(8,128)}) custom-call(bf16[128,1024]{1,0:T(8,128)(2,1)} %bitcast.11, bf16[128,2048]{1,0:T(8,128)(2,1)} %bitcast.9, bf16[128,2048]{1,0:T(8,128)(2,1)} %bitcast.10, ...), custom_call_target="tpu_custom_call" | custom-call | tf_op jit(solution)/shard_map/whole_step/pallas_call | solution.py:814
  75.1 2.2 %finish.1 = (bf16[128,2048]{1,0:T(8,128)(2,1)}, bf16[128,1024]{1,0:T(8,128)(2,1)}, f32[32,128]{1,0:T(8,128)}, f32[8,2048]{1,0:T(8,128)}, f32[8,2048]{1,0:T(8,128)}, /*index=5*/f32[18,32]{1,0:T(8,128)}) custom-call(bf16[128,2048]{1,0:T(8,128)(2,1)} %get-tuple-element.18.qg_in, bf16[128,1024]{1,0:T(8,128)(2,1)} %get-tuple-element.19.ig_in, ...), custom_call_target="tpu_custom_call" | custom-call | tf_op jit(solution)/shard_map/finish/pallas_call | solution.py:888

commit v7 on v5

--- a/solution.py
+++ b/solution.py
@@ -300,15 +300,16 @@
             st[rows_of(1024 + pp * 8, 8), :] = meta
 
     both = s["both"]
-    lax.fori_loop(0, 4, lambda i, carry: project(i, s["st"]), None)
+    project(0, s["st"])
     pl.semaphore_wait(barrier, len(peers))
-    swap = remote(s["st"], both.at[c], sib)
 
     gathers = (("batch", y, s["hy"]), ("z", z, s["hz"]))
     hops = []
     for axis, index, buf in gathers:
         for d in (1, 3):
             hops.append(remote(s["hid_t"], buf.at[index, c], {axis: ring(index, d)}))
+    lax.fori_loop(1, 4, lambda i, carry: project(i, s["st"]), None)
+    swap = remote(s["st"], both.at[c], sib)
     down = [remote(s["hid_t"], buf.at[index, c], sib) for _, index, buf in gathers]
     lax.fori_loop(4, 8, lambda i, carry: project(i, both.at[c]), None)
 
@@ -379,19 +380,25 @@
         m1 = both[1, 1024 + pp * 8 : 1032 + pp * 8, :]
         return f0, f1, r0, r1, m0[0:1], m0[1:2], m0[2:3], m1[0:1], m1[1:2], m1[2:3]
 
-    xs = []
-    for p in range(2):
+    def chip_sums(p):
         for n in range(4):
             f0, f1, r0, r1, t0, first0, last0, t1, first1, last1 = block_pair(2 * n + p)
             chip_send[p, n, 0:64, :] = f1 + linked(last0, last1, t1) * f0
             chip_send[p, n, 64:128, :] = r0 + linked(first0, first1, t0) * r1
             chip_send[p, n, 128:136, :] = meta_rows(t0 + t1, first0, last1)
+
+    def chip_sends(p):
         copies = []
-        for d in (1, 2, 3):
+        for d in (2, 1, 3):
             to = ring(x, d)
             copies.append(remote(chip_send.at[p, to], chip_recv.at[p, x], {"x": to}))
         chip_recv[p, pl.ds(x, 1)] = chip_send[p, pl.ds(x, 1)]
-        xs.append(copies)
+        return copies
+
+    xs = []
+    for p in range(2):
+        chip_sums(p)
+        xs.append(chip_sends(p))
     for pp in range(8):
         f0, _, _, r1, _, _, last0, _, first1, _ = block_pair(pp)
         d8 = same(last0, first1) * jnp.sum(f0 * r1, axis=0, keepdims=True)
@@ -436,7 +443,19 @@
                 for n, d in ((0, 1), (1, 3))
             ]
         )
-    lax.fori_loop(7, 10, inner, 0)
+
+    fwd = []
+    for n, (axis, index, buf) in enumerate(gathers):
+        for m, d in enumerate((1, 3)):
+            hops[2 * n + m].wait()
+            came = ring(index, 4 - d)
+            part = slice(0, 512) if d == 1 else slice(512, 1024)
+            fwd.append(
+                remote(buf.at[came, c, part], buf.at[came, c, part], {axis: ring(index, d)})
+            )
+            down.append(remote(buf.at[came, c], buf.at[came, c], sib))
+
+    lax.fori_loop(7, 9, inner, 0)
 
     has_prev = (z > 0).astype(F32)
     has_next = (z < 3).astype(F32)
@@ -488,17 +507,6 @@
         back_recv[p, pl.ds(x, 1)] = back_send[p, pl.ds(x, 1)]
         bs.append(copies)
 
-    fwd = []
-    for n, (axis, index, buf) in enumerate(gathers):
-        for m, d in enumerate((1, 3)):
-            hops[2 * n + m].wait()
-            came = ring(index, 4 - d)
-            part = slice(0, 512) if d == 1 else slice(512, 1024)
-            fwd.append(
-                remote(buf.at[came, c, part], buf.at[came, c, part], {axis: ring(index, d)})
-            )
-            down.append(remote(buf.at[came, c], buf.at[came, c], sib))
-
     for p in range(2):
         (f0, r0, t0, a0, l0), (f1, r1, t1, a1, l1), (f2, r2, t2, a2, l2), (f3, r3, t3, a3, l3) = (
             chip(j, p) for j in range(4)
@@ -525,7 +533,12 @@
         )
         pair = c * 8 + 2 * x + p
         s["gcross"][pl.ds(pair, 1)] = s["gcross"][pl.ds(pair, 1)] + rows[None]
-    lax.fori_loop(10, 16, inner, 0)
+    lax.fori_loop(9, 16, inner, 0)
+    for n, (_, index, buf) in enumerate(gathers):
+        buf[pl.ds(index, 1), pl.ds(c, 1)] = s["hid_t"][...][None, None]
+        wait(fwd[2 * n : 2 * n + 2])
+        came = ring(index, 2)
+        down.append(remote(buf.at[came, c], buf.at[came, c], sib))
 
     own_blocks, s_in = s["own_blocks"], s["s_in"]
     swaps = []
@@ -595,9 +608,16 @@
             fv.append(remote(s["vs"].at[n, to], s["rv"].at[n, me_z], dev))
         key_part(me_y, n)
         value_part(me_z, n)
+        firsts.append((fk, fv))
+    for n in range(2):
         s["rk"][n, pl.ds(me_y, 1)] = s["ks"][n, pl.ds(me_y, 1)]
         s["rv"][n, pl.ds(me_z, 1)] = s["vs"][n, pl.ds(me_z, 1)]
-        firsts.append((fk, fv))
+
+    wait(down)
+    for name, out in (("hy", "hyb"), ("hz", "hzb")):
+        for g in range(8):
+            s[out][:, g * TOK : (g + 1) * TOK] = s[name][g // 2, g % 2].astype(BF16)
+
     for n in range(2):
         lax.fori_loop(0, 8, lambda to, carry: query_part(to, n), None)
     stores = []
@@ -609,6 +629,32 @@
 
     store(qg_ref, qg_hbm)
     store(s["gate"], gate_hbm)
+
+    def product(left, right, n):
+        right = s[right][n].reshape(8 * TOK, PAIR).astype(BF16)
+        for b in range(4):
+            yield b, dot(s[left][b * 256 : (b + 1) * 256, :], right, NN)
+
+    part1, recv1, part2, recv2 = s["part1"], s["recv1"], s["part2"], s["recv2"]
+
+    def scatter(part, recv, chunk, axis, index):
+        out = []
+        for d in (1, 2, 3):
+            to = ring(index, d)
+            out.append(remote(part.at[chunk, to], recv.at[chunk, index], {axis: to}))
+        recv[chunk, pl.ds(index, 1)] = part[chunk, pl.ds(index, 1)]
+        return out
+
+    wait(firsts[0][0])
+    for b, block in product("hyb", "rk", 0):
+        for j in range(4):
+            part1[0, j, b * 64 : b * 64 + 64, :] = block[j * 64 : j * 64 + 64, :]
+    k0 = scatter(part1, recv1, 0, "x", x)
+    wait(firsts[0][1])
+    for b, block in product("hzb", "rv", 0):
+        for j in range(4):
+            part1[2, j, b * 64 : b * 64 + 64, :] = block[j * 64 : j * 64 + 64, :]
+    v0 = scatter(part1, recv1, 2, "x", x)
 
     ones = jnp.ones((8, PAIR), F32)
     inner_sum = dot_exact(ones, s["gint"][...].reshape(256, PAIR), NT)
@@ -625,42 +671,6 @@
     for d, e in offsets:
         smalls.append(remote(small, m1.at[me_z], plane("z", z, d, e)[0]))
     m1[pl.ds(me_z, 1)] = small[...][None]
-
-    for n, (_, index, buf) in enumerate(gathers):
-        buf[pl.ds(index, 1), pl.ds(c, 1)] = s["hid_t"][...][None, None]
-        wait(fwd[2 * n : 2 * n + 2])
-        came = ring(index, 2)
-        down.append(remote(buf.at[came, c], buf.at[came, c], sib))
-    wait(down)
-    for name, out in (("hy", "hyb"), ("hz", "hzb")):
-        for g in range(8):
-            s[out][:, g * TOK : (g + 1) * TOK] = s[name][g // 2, g % 2].astype(BF16)
-
-    def product(left, right, n):
-        right = s[right][n].reshape(8 * TOK, PAIR).astype(BF16)
-        for b in range(4):
-            yield b, dot(s[left][b * 256 : (b + 1) * 256, :], right, NN)
-
-    part1, recv1, part2, recv2 = s["part1"], s["recv1"], s["part2"], s["recv2"]
-
-    def scatter(part, recv, chunk, axis, index):
-        out = []
-        for d in (1, 2, 3):
-            to = ring(index, d)
-            out.append(remote(part.at[chunk, to], recv.at[chunk, index], {axis: to}))
-        recv[chunk, pl.ds(index, 1)] = part[chunk, pl.ds(index, 1)]
-        return out
-
-    wait(firsts[0][0])
-    for b, block in product("hyb", "rk", 0):
-        for j in range(4):
-            part1[0, j, b * 64 : b * 64 + 64, :] = block[j * 64 : j * 64 + 64, :]
-    k0 = scatter(part1, recv1, 0, "x", x)
-    wait(firsts[0][1])
-    for b, block in product("hzb", "rv", 0):
-        for j in range(4):
-            part1[2, j, b * 64 : b * 64 + 64, :] = block[j * 64 : j * 64 + 64, :]
-    v0 = scatter(part1, recv1, 2, "x", x)
 
     def input_grad(n, carry):
         rows = rows_of(n * 256, 256)

time: 80 us -> 77.2 us (0.965)
  Pallas kernels: 78.3 us -> 75.4 us
    pallas_call x1, Pallas kernels: 76.1 us -> 73.2 us  [whole_step(): pl.pallas_call(step_kernel, in_specs=[far] * 8, out_specs=[far] * 6, out_...]
where the time goes in v7:
time: 77.2 us; the launch traced here: 76.1 us
  Pallas kernels  75.4 us (98%)
    pallas_call x1, Pallas kernels, whole_step(): pl.pallas_call(step_kernel, in_specs=[far] * 8, out_specs=[far] * 6, out_...  73.2 us
    pallas_call x1, Pallas kernels, finish(): pl.pallas_call(finish_kernel, in_specs=[far] * 6, out_specs=[far] * 6, ou...  2.17 us

profile of v7, /device:TPU:0, one launch (start us, length us, event | category | flops | bytes accessed | tf_op | source)
XLA Modules:
  0.0 76.1 jit_solution(17537861904151509319)
XLA Ops:
  0.6 73.2 %whole_step.1 = (bf16[128,2048]{1,0:T(8,128)(2,1)}, bf16[128,1024]{1,0:T(8,128)(2,1)}, f32[16,8,128]{2,1,0:T(8,128)}, f32[8,2048]{1,0:T(8,128)}, f32[8,2048]{1,0:T(8,128)}, /*index=5*/f32[16,128]{1,0:T(8,128)}) custom-call(bf16[128,1024]{1,0:T(8,128)(2,1)} %bitcast.11, bf16[128,2048]{1,0:T(8,128)(2,1)} %bitcast.9, bf16[128,2048]{1,0:T(8,128)(2,1)} %bitcast.10, ...), custom_call_target="tpu_custom_call" | custom-call | tf_op jit(solution)/shard_map/whole_step/pallas_call | solution.py:788
  73.9 2.2 %finish.1 = (bf16[128,2048]{1,0:T(8,128)(2,1)}, bf16[128,1024]{1,0:T(8,128)(2,1)}, f32[32,128]{1,0:T(8,128)}, f32[8,2048]{1,0:T(8,128)}, f32[8,2048]{1,0:T(8,128)}, /*index=5*/f32[18,32]{1,0:T(8,128)}) custom-call(bf16[128,2048]{1,0:T(8,128)(2,1)} %get-tuple-element.18.qg_in, bf16[128,1024]{1,0:T(8,128)(2,1)} %get-tuple-element.19.ig_in, ...), custom_call_target="tpu_custom_call" | custom-call | tf_op jit(solution)/shard_map/finish/pallas_call | solution.py:862

commit v8 on v7

--- a/solution.py
+++ b/solution.py
@@ -534,8 +534,20 @@
         pair = c * 8 + 2 * x + p
         s["gcross"][pl.ds(pair, 1)] = s["gcross"][pl.ds(pair, 1)] + rows[None]
     lax.fori_loop(9, 16, inner, 0)
+    def rounded(n, block, core):
+        buf, out = gathers[n][2], s[("hyb", "hzb")[n]]
+        out[:, rows_of((2 * block + core) * TOK, TOK)] = buf[block, core].astype(BF16)
+
     for n, (_, index, buf) in enumerate(gathers):
-        buf[pl.ds(index, 1), pl.ds(c, 1)] = s["hid_t"][...][None, None]
+        s[("hyb", "hzb")[n]][:, rows_of((2 * index + c) * TOK, TOK)] = s["hid_t"][...].astype(BF16)
+        down[n].wait()
+        rounded(n, index, 1 - c)
+        for m, d in enumerate((1, 3)):
+            came = ring(index, 4 - d)
+            rounded(n, came, c)
+            down[2 + 2 * n + m].wait()
+            rounded(n, came, 1 - c)
+    for n, (_, index, buf) in enumerate(gathers):
         wait(fwd[2 * n : 2 * n + 2])
         came = ring(index, 2)
         down.append(remote(buf.at[came, c], buf.at[came, c], sib))
@@ -613,22 +625,11 @@
         s["rk"][n, pl.ds(me_y, 1)] = s["ks"][n, pl.ds(me_y, 1)]
         s["rv"][n, pl.ds(me_z, 1)] = s["vs"][n, pl.ds(me_z, 1)]
 
-    wait(down)
-    for name, out in (("hy", "hyb"), ("hz", "hzb")):
-        for g in range(8):
-            s[out][:, g * TOK : (g + 1) * TOK] = s[name][g // 2, g % 2].astype(BF16)
-
-    for n in range(2):
-        lax.fori_loop(0, 8, lambda to, carry: query_part(to, n), None)
-    stores = []
-
-    def store(ref, hbm):
-        cp = pltpu.make_async_copy(ref, hbm, local_sem.at[24 + len(stores)])
-        cp.start()
-        stores.append(cp)
-
-    store(qg_ref, qg_hbm)
-    store(s["gate"], gate_hbm)
+    for n, (_, index, buf) in enumerate(gathers):
+        came = ring(index, 2)
+        rounded(n, came, c)
+        down[6 + n].wait()
+        rounded(n, came, 1 - c)
 
     def product(left, right, n):
         right = s[right][n].reshape(8 * TOK, PAIR).astype(BF16)
@@ -655,6 +656,18 @@
         for j in range(4):
             part1[2, j, b * 64 : b * 64 + 64, :] = block[j * 64 : j * 64 + 64, :]
     v0 = scatter(part1, recv1, 2, "x", x)
+
+    for n in range(2):
+        lax.fori_loop(0, 8, lambda to, carry: query_part(to, n), None)
+    stores = []
+
+    def store(ref, hbm):
+        cp = pltpu.make_async_copy(ref, hbm, local_sem.at[24 + len(stores)])
+        cp.start()
+        stores.append(cp)
+
+    store(qg_ref, qg_hbm)
+    store(s["gate"], gate_hbm)
 
     ones = jnp.ones((8, PAIR), F32)
     inner_sum = dot_exact(ones, s["gint"][...].reshape(256, PAIR), NT)

time: 77.2 us -> 78 us (1.010)
  Pallas kernels: 75.4 us -> 76.3 us
    pallas_call x1, Pallas kernels: 73.2 us -> 74.1 us  [whole_step(): pl.pallas_call(step_kernel, in_specs=[far] * 8, out_specs=[far] * 6, out_...]
where the time goes in v8:
time: 78 us; the launch traced here: 76.9 us
  Pallas kernels  76.3 us (98%)
    pallas_call x1, Pallas kernels, whole_step(): pl.pallas_call(step_kernel, in_specs=[far] * 8, out_specs=[far] * 6, out_...  74.1 us
    pallas_call x1, Pallas kernels, finish(): pl.pallas_call(finish_kernel, in_specs=[far] * 6, out_specs=[far] * 6, ou...  2.17 us

profile of v8, /device:TPU:0, one launch (start us, length us, event | category | flops | bytes accessed | tf_op | source)
XLA Modules:
  0.0 76.9 jit_solution(17074461359896530945)
XLA Ops:
  0.6 74.1 %whole_step.1 = (bf16[128,2048]{1,0:T(8,128)(2,1)}, bf16[128,1024]{1,0:T(8,128)(2,1)}, f32[16,8,128]{2,1,0:T(8,128)}, f32[8,2048]{1,0:T(8,128)}, f32[8,2048]{1,0:T(8,128)}, /*index=5*/f32[16,128]{1,0:T(8,128)}) custom-call(bf16[128,1024]{1,0:T(8,128)(2,1)} %bitcast.11, bf16[128,2048]{1,0:T(8,128)(2,1)} %bitcast.9, bf16[128,2048]{1,0:T(8,128)(2,1)} %bitcast.10, ...), custom_call_target="tpu_custom_call" | custom-call | tf_op jit(solution)/shard_map/whole_step/pallas_call | solution.py:801
  74.7 2.2 %finish.1 = (bf16[128,2048]{1,0:T(8,128)(2,1)}, bf16[128,1024]{1,0:T(8,128)(2,1)}, f32[32,128]{1,0:T(8,128)}, f32[8,2048]{1,0:T(8,128)}, f32[8,2048]{1,0:T(8,128)}, /*index=5*/f32[18,32]{1,0:T(8,128)}) custom-call(bf16[128,2048]{1,0:T(8,128)(2,1)} %get-tuple-element.18.qg_in, bf16[128,1024]{1,0:T(8,128)(2,1)} %get-tuple-element.19.ig_in, ...), custom_call_target="tpu_custom_call" | custom-call | tf_op jit(solution)/shard_map/finish/pallas_call | solution.py:875

commit v9 on v8

--- a/solution.py
+++ b/solution.py
@@ -577,6 +577,9 @@
         return jnp.concatenate([jnp.where(low_half, a, 0.0), jnp.where(low_half, 0.0, a)], axis=0)
 
     def incoming(to, p, part):
+        if isinstance(to, int):
+            at = to % 4 * 128 + part * 64
+            return diag(s_in[p, to // 4, at : at + 64, :])
         at = lax.rem(to, 4) * 128 + part * 64
         return diag(s_in[p, to // 4, rows_of(at, 64), :])
 
@@ -597,7 +600,7 @@
 
     def query_part(to, p):
         pair = 2 * to + p
-        cols = rows_of(pair * PAIR, PAIR)
+        cols = slice(pair * PAIR, (pair + 1) * PAIR)
         sg = s["fw"][pair] * dot_right(s["g"][:, cols], incoming(to, p, 0), NT)
         qg_ref[:, cols] = (s["qacc"][pair] + sg).astype(BF16)
         diff = s["q"][:, cols].astype(F32) * sg - s["kacc"][pair]
@@ -658,7 +661,8 @@
     v0 = scatter(part1, recv1, 2, "x", x)
 
     for n in range(2):
-        lax.fori_loop(0, 8, lambda to, carry: query_part(to, n), None)
+        for to in range(8):
+            query_part(to, n)
     stores = []
 
     def store(ref, hbm):
@@ -692,7 +696,6 @@
         ).astype(BF16)
         return carry
 
-    lax.fori_loop(0, 2, input_grad, 0)
 
     wait(firsts[1][0])
     for b, block in product("hyb", "rk", 1):
@@ -705,7 +708,7 @@
                 at = j * 32 + i * 8
                 part1[3, i, b * 64 + j * 8 : b * 64 + j * 8 + 8, :] = block[at : at + 8, :]
     v1 = scatter(part1, recv1, 3, "batch", y)
-    lax.fori_loop(2, 4, input_grad, 0)
+    lax.fori_loop(0, 4, input_grad, 0)
     store(ig_ref, ig_hbm)
 
     wait(smalls)

time: 78 us -> 74.4 us (0.954)
  Pallas kernels: 76.3 us -> 72.6 us
    pallas_call x1, Pallas kernels: 74.1 us -> 70.5 us  [whole_step(): pl.pallas_call(step_kernel, in_specs=[far] * 8, out_specs=[far] * 6, out_...]
where the time goes in v9:
time: 74.4 us; the launch traced here: 73.3 us
  Pallas kernels  72.6 us (98%)
    pallas_call x1, Pallas kernels, whole_step(): pl.pallas_call(step_kernel, in_specs=[far] * 8, out_specs=[far] * 6, out_...  70.5 us
    pallas_call x1, Pallas kernels, finish(): pl.pallas_call(finish_kernel, in_specs=[far] * 6, out_specs=[far] * 6, ou...  2.17 us

profile of v9, /device:TPU:0, one launch (start us, length us, event | category | flops | bytes accessed | tf_op | source)
XLA Modules:
  0.0 73.3 jit_solution(14441115408103201073)
XLA Ops:
  0.6 70.5 %whole_step.1 = (bf16[128,2048]{1,0:T(8,128)(2,1)}, bf16[128,1024]{1,0:T(8,128)(2,1)}, f32[16,8,128]{2,1,0:T(8,128)}, f32[8,2048]{1,0:T(8,128)}, f32[8,2048]{1,0:T(8,128)}, /*index=5*/f32[16,128]{1,0:T(8,128)}) custom-call(bf16[128,1024]{1,0:T(8,128)(2,1)} %bitcast.11, bf16[128,2048]{1,0:T(8,128)(2,1)} %bitcast.9, bf16[128,2048]{1,0:T(8,128)(2,1)} %bitcast.10, ...), custom_call_target="tpu_custom_call" | custom-call | tf_op jit(solution)/shard_map/whole_step/pallas_call | solution.py:804
  71.1 2.2 %finish.1 = (bf16[128,2048]{1,0:T(8,128)(2,1)}, bf16[128,1024]{1,0:T(8,128)(2,1)}, f32[32,128]{1,0:T(8,128)}, f32[8,2048]{1,0:T(8,128)}, f32[8,2048]{1,0:T(8,128)}, /*index=5*/f32[18,32]{1,0:T(8,128)}) custom-call(bf16[128,2048]{1,0:T(8,128)(2,1)} %get-tuple-element.18.qg_in, bf16[128,1024]{1,0:T(8,128)(2,1)} %get-tuple-element.19.ig_in, ...), custom_call_target="tpu_custom_call" | custom-call | tf_op jit(solution)/shard_map/finish/pallas_call | solution.py:878

commit v10 on v9

--- a/solution.py
+++ b/solution.py
@@ -235,6 +235,17 @@
             first_loads[1].start()
             first_loads[2].start()
 
+    first_loads[0].wait()
+    for b in range(8):
+        cols = slice(b * TOK, (b + 1) * TOK)
+        s["hid_t"][cols, :] = s["hid"][:, cols].astype(F32).T
+    pl.semaphore_wait(barrier, len(peers))
+    gathers = (("batch", y, s["hy"]), ("z", z, s["hz"]))
+    hops = []
+    for axis, index, buf in gathers:
+        for d in (1, 3):
+            hops.append(remote(s["hid_t"], buf.at[index, c], {axis: ring(index, d)}))
+
     rows_i, cols_i = iota((TOK, TOK), 0), iota((TOK, TOK), 1)
     causal = cols_i <= rows_i
     lower = causal.astype(F32)
@@ -255,11 +266,6 @@
     seg_row = s["segr"][...].astype(F32)
     s["segc"][...] = jnp.broadcast_to(seg_row, (TOK, TOK)).T
     s["gcross"][...] = jnp.zeros((16, 8, PAIR), F32)
-
-    first_loads[0].wait()
-    for b in range(8):
-        cols = slice(b * TOK, (b + 1) * TOK)
-        s["hid_t"][cols, :] = s["hid"][:, cols].astype(F32).T
 
     first_loads[1].wait()
     first_loads[2].wait()
@@ -300,15 +306,7 @@
             st[rows_of(1024 + pp * 8, 8), :] = meta
 
     both = s["both"]
-    project(0, s["st"])
-    pl.semaphore_wait(barrier, len(peers))
-
-    gathers = (("batch", y, s["hy"]), ("z", z, s["hz"]))
-    hops = []
-    for axis, index, buf in gathers:
-        for d in (1, 3):
-            hops.append(remote(s["hid_t"], buf.at[index, c], {axis: ring(index, d)}))
-    lax.fori_loop(1, 4, lambda i, carry: project(i, s["st"]), None)
+    lax.fori_loop(0, 4, lambda i, carry: project(i, s["st"]), None)
     swap = remote(s["st"], both.at[c], sib)
     down = [remote(s["hid_t"], buf.at[index, c], sib) for _, index, buf in gathers]
     lax.fori_loop(4, 8, lambda i, carry: project(i, both.at[c]), None)
@@ -547,10 +545,6 @@
             rounded(n, came, c)
             down[2 + 2 * n + m].wait()
             rounded(n, came, 1 - c)
-    for n, (_, index, buf) in enumerate(gathers):
-        wait(fwd[2 * n : 2 * n + 2])
-        came = ring(index, 2)
-        down.append(remote(buf.at[came, c], buf.at[came, c], sib))
 
     own_blocks, s_in = s["own_blocks"], s["s_in"]
     swaps = []
@@ -624,6 +618,10 @@
         key_part(me_y, n)
         value_part(me_z, n)
         firsts.append((fk, fv))
+    for n, (_, index, buf) in enumerate(gathers):
+        wait(fwd[2 * n : 2 * n + 2])
+        came = ring(index, 2)
+        down.append(remote(buf.at[came, c], buf.at[came, c], sib))
     for n in range(2):
         s["rk"][n, pl.ds(me_y, 1)] = s["ks"][n, pl.ds(me_y, 1)]
         s["rv"][n, pl.ds(me_z, 1)] = s["vs"][n, pl.ds(me_z, 1)]

time: 74.4 us -> 74 us (level)
  no operation moved by 1% of the time
where the time goes in v10:
time: 74 us; the launch traced here: 72.9 us
  Pallas kernels  72.2 us (98%)
    pallas_call x1, Pallas kernels, whole_step(): pl.pallas_call(step_kernel, in_specs=[far] * 8, out_specs=[far] * 6, out_...  70.1 us
    pallas_call x1, Pallas kernels, finish(): pl.pallas_call(finish_kernel, in_specs=[far] * 6, out_specs=[far] * 6, ou...  2.17 us

profile of v10, /device:TPU:0, one launch (start us, length us, event | category | flops | bytes accessed | tf_op | source)
XLA Modules:
  0.0 72.9 jit_solution(9714392735797621164)
XLA Ops:
  0.6 70.1 %whole_step.1 = (bf16[128,2048]{1,0:T(8,128)(2,1)}, bf16[128,1024]{1,0:T(8,128)(2,1)}, f32[16,8,128]{2,1,0:T(8,128)}, f32[8,2048]{1,0:T(8,128)}, f32[8,2048]{1,0:T(8,128)}, /*index=5*/f32[16,128]{1,0:T(8,128)}) custom-call(bf16[128,1024]{1,0:T(8,128)(2,1)} %bitcast.11, bf16[128,2048]{1,0:T(8,128)(2,1)} %bitcast.9, bf16[128,2048]{1,0:T(8,128)(2,1)} %bitcast.10, ...), custom_call_target="tpu_custom_call" | custom-call | tf_op jit(solution)/shard_map/whole_step/pallas_call | solution.py:802
  70.7 2.2 %finish.1 = (bf16[128,2048]{1,0:T(8,128)(2,1)}, bf16[128,1024]{1,0:T(8,128)(2,1)}, f32[32,128]{1,0:T(8,128)}, f32[8,2048]{1,0:T(8,128)}, f32[8,2048]{1,0:T(8,128)}, /*index=5*/f32[18,32]{1,0:T(8,128)}) custom-call(bf16[128,2048]{1,0:T(8,128)(2,1)} %get-tuple-element.18.qg_in, bf16[128,1024]{1,0:T(8,128)(2,1)} %get-tuple-element.19.ig_in, ...), custom_call_target="tpu_custom_call" | custom-call | tf_op jit(solution)/shard_map/finish/pallas_call | solution.py:876

commit v11 on v10

--- a/solution.py
+++ b/solution.py
@@ -360,6 +360,10 @@
         s["gint"][pair] = jnp.concatenate(gain_rows, axis=0)
         return carry
 
+    def inner_two(n, carry):
+        inner(2 * n, carry)
+        return inner(2 * n + 1, carry)
+
     swap.wait()
 
     def meta_rows(total, first, last):
@@ -401,7 +405,7 @@
         f0, _, _, r1, _, _, last0, _, first1, _ = block_pair(pp)
         d8 = same(last0, first1) * jnp.sum(f0 * r1, axis=0, keepdims=True)
         s["gcross"][pl.ds(c * 8 + pp, 1)] = jnp.where(row8 == 0, d8, 0.0)[None]
-    lax.fori_loop(0, 7, inner, 0)
+    lax.fori_loop(0, 3, inner_two, 0)
 
     def chip(j, p):
         return (
@@ -453,7 +457,7 @@
             )
             down.append(remote(buf.at[came, c], buf.at[came, c], sib))
 
-    lax.fori_loop(7, 9, inner, 0)
+    lax.fori_loop(3, 4, inner_two, 0)
 
     has_prev = (z > 0).astype(F32)
     has_next = (z < 3).astype(F32)
@@ -531,7 +535,7 @@
         )
         pair = c * 8 + 2 * x + p
         s["gcross"][pl.ds(pair, 1)] = s["gcross"][pl.ds(pair, 1)] + rows[None]
-    lax.fori_loop(9, 16, inner, 0)
+    lax.fori_loop(4, 8, inner_two, 0)
     def rounded(n, block, core):
         buf, out = gathers[n][2], s[("hyb", "hzb")[n]]
         out[:, rows_of((2 * block + core) * TOK, TOK)] = buf[block, core].astype(BF16)

time: 74 us -> 74.1 us (level)
  no operation moved by 1% of the time
where the time goes in v11:
time: 74.1 us; the launch traced here: 73 us
  Pallas kernels  72.3 us (98%)
    pallas_call x1, Pallas kernels, whole_step(): pl.pallas_call(step_kernel, in_specs=[far] * 8, out_specs=[far] * 6, out_...  70.2 us
    pallas_call x1, Pallas kernels, finish(): pl.pallas_call(finish_kernel, in_specs=[far] * 6, out_specs=[far] * 6, ou...  2.17 us

profile of v11, /device:TPU:0, one launch (start us, length us, event | category | flops | bytes accessed | tf_op | source)
XLA Modules:
  0.0 73.0 jit_solution(13008684448832929975)
XLA Ops:
  0.6 70.2 %whole_step.1 = (bf16[128,2048]{1,0:T(8,128)(2,1)}, bf16[128,1024]{1,0:T(8,128)(2,1)}, f32[16,8,128]{2,1,0:T(8,128)}, f32[8,2048]{1,0:T(8,128)}, f32[8,2048]{1,0:T(8,128)}, /*index=5*/f32[16,128]{1,0:T(8,128)}) custom-call(bf16[128,1024]{1,0:T(8,128)(2,1)} %bitcast.11, bf16[128,2048]{1,0:T(8,128)(2,1)} %bitcast.9, bf16[128,2048]{1,0:T(8,128)(2,1)} %bitcast.10, ...), custom_call_target="tpu_custom_call" | custom-call | tf_op jit(solution)/shard_map/whole_step/pallas_call | solution.py:806
  70.8 2.2 %finish.1 = (bf16[128,2048]{1,0:T(8,128)(2,1)}, bf16[128,1024]{1,0:T(8,128)(2,1)}, f32[32,128]{1,0:T(8,128)}, f32[8,2048]{1,0:T(8,128)}, f32[8,2048]{1,0:T(8,128)}, /*index=5*/f32[18,32]{1,0:T(8,128)}) custom-call(bf16[128,2048]{1,0:T(8,128)(2,1)} %get-tuple-element.18.qg_in, bf16[128,1024]{1,0:T(8,128)(2,1)} %get-tuple-element.19.ig_in, ...), custom_call_target="tpu_custom_call" | custom-call | tf_op jit(solution)/shard_map/finish/pallas_call | solution.py:880
